TPU v7x, 256 devices: a whole 4x4x8 slice. The times are simulated.
256 devices in a mesh: set: 16 (over z, core), col: 16 (over y, x).
Axes of the slice: x: 4, y: 4, z: 8, core: 2. Of those that a mesh axis runs over, the one named last changes fastest.
Arguments:
- factor: float32 [32, 2, 131072], P('col'), may hold values from -8 to 8
- velocity: float32 [32, 2, 131072], P(None, None, ('set', 'col')), may hold values from -4 to 4
- labels: int32 [16, 17], P('set'), may hold values from 0 to 2
- counts: int32 [16, 131072], P('set'), may hold values from 1 to 28, as said below
Outputs:
- new_factor: float32 [32, 2, 131072], P(None, None, ('set', 'col'))
- new_velocity: float32 [32, 2, 131072], P(None, None, ('set', 'col'))
Inputs may be any that keep to these rules, and one draw needn't show every extreme that they name: `labels`: 0 selects the X basis, 1 the Y basis, 2 the Z basis. The counts of setting s lie between 1 and 4 + (24 s) // 15.
All inputs are finite; a program needn't handle non-finite values.
Results may differ from a plain program's by a relative error of at most 0.0003.
Values sent between devices are 32-bit elements; how exact they have to be, the bound alone decides.
No kernel may reach another device: no remote copies, remote signals or barrier semaphores. Data moves between devices by JAX's collectives and lax.ppermute only.
A program may use at most 64 MiB of HBM per device.

v0:
```python
import functools

import jax
import jax.numpy as jnp
from jax import lax
from jax.experimental import pallas as pl
from jax.experimental.pallas import tpu as pltpu
from jax.sharding import Mesh
from jax.sharding import PartitionSpec as P

QA, QB, QUBITS = 8, 9, 17
ORDER = 2**QUBITS
LEFT, RIGHT = 2**QA, 2**QB
LANES = 128
HIGHS = RIGHT // LANES
ROWS = ORDER // LANES
COLS = 16
SETS = 16
ZS = 8

COL = ("y", "x")
SET = ("z", "core")

mixing = 0.1
penalty = 8.0
momentum = 0.9
step_size = 0.5
count_norm = 8.0

F32 = jnp.float32
BF16 = jnp.bfloat16
HIGH = lax.Precision.HIGHEST
PCHUNK = ROWS // COLS
VMEM = pl.BlockSpec(memory_space=pltpu.VMEM)
SMEM = pl.BlockSpec(memory_space=pltpu.SMEM)


def halves(x):
    high = x.astype(BF16)
    return high, (x - high.astype(F32)).astype(BF16)


def masks_of(labels_ref):
    rotated_bits = jnp.int32(0)
    y_bits = jnp.int32(0)
    scale = jnp.float32(1.0)
    for q in range(QUBITS):
        label = labels_ref[0, q]
        bit = jnp.int32(1 << (QUBITS - 1 - q))
        rotated_bits = rotated_bits + jnp.where(label == 2, 0, bit)
        y_bits = y_bits + jnp.where(label == 1, bit, 0)
        scale = scale * jnp.where(label == 2, jnp.float32(1.0), jnp.float32(0.5))
    return rotated_bits, y_bits, scale


def hadamard(row, size, bits):
    col = lax.broadcasted_iota(jnp.int32, row.shape, 1)
    odd = lax.population_count(row & col & bits) & 1
    same = ((row ^ col) & (size - 1 - bits)) == 0
    return jnp.where(same, (1 - 2 * odd).astype(F32), 0.0).astype(BF16)


def quarter_turns(row, high, y_bits):
    lane = lax.broadcasted_iota(jnp.int32, row.shape, 1)
    index = row * RIGHT + high * LANES + lane
    return lax.population_count(index & y_bits) & 3


def forward_kernel(labels_ref, factor_ref, rotated_ref, send_ref, xh, xl, th, tl, prob, hb):
    set_index = lax.axis_index("z") * 2 + lax.axis_index("core")
    bits, y_bits, scale = masks_of(labels_ref)
    a_bits, b_bits = bits >> QB, bits & (RIGHT - 1)
    hb[...] = hadamard(lax.broadcasted_iota(jnp.int32, (RIGHT, RIGHT), 0), RIGHT, b_bits)
    ha = hadamard(lax.broadcasted_iota(jnp.int32, (LEFT, LEFT), 0), LEFT, a_bits)
    row = lax.broadcasted_iota(jnp.int32, (LEFT, LANES), 0)
    for high in range(HIGHS):
        turns = quarter_turns(row, high, y_bits)
        swap = (turns & 1) == 1
        sign_real = jnp.where(turns >= 2, -1.0, 1.0)
        sign_imag = jnp.where((turns == 1) | (turns == 2), -1.0, 1.0)
        block = pl.ds(high * LANES, LANES)
        for r in range(2):
            real = factor_ref[r, pl.ds(2 * high, LEFT, stride=2 * HIGHS), :]
            imag = factor_ref[r, pl.ds(2 * high + 1, LEFT, stride=2 * HIGHS), :]
            for c, turned in (
                (0, sign_real * jnp.where(swap, imag, real)),
                (1, sign_imag * jnp.where(swap, real, imag)),
            ):
                xh[2 * r + c, :, block], xl[2 * r + c, :, block] = halves(turned)
    prob[...] = jnp.zeros_like(prob)

    def one(i, carry):
        for n in range(2):
            part = pl.ds(n * 256, 256)
            first = jnp.dot(ha, xh[i, :, part], preferred_element_type=F32) + jnp.dot(
                ha, xl[i, :, part], preferred_element_type=F32
            )
            th[:, part], tl[:, part] = halves(first)
        for n in range(2):
            part = pl.ds(n * 256, 256)
            second = jnp.dot(th[...], hb[:, part], preferred_element_type=F32) + jnp.dot(
                tl[...], hb[:, part], preferred_element_type=F32
            )
            rotated_ref[i, :, part] = second
            prob[:, part] += second * second
        return carry

    lax.fori_loop(0, 4, one, 0)
    for c in range(COLS):
        for high in range(HIGHS):
            send_ref[c, pl.ds(16 * high, 16), :] = (
                prob[pl.ds(16 * c, 16), pl.ds(high * LANES, LANES)] * scale
            )
        start = pl.multiple_of(set_index * (ROWS * 2 // SETS) + 8 * c, 8)
        for r in range(2):
            send_ref[c, pl.ds(PCHUNK + 8 * r, 8), :] = factor_ref[r, pl.ds(start, 8), :]


def summed_kernel(got_ref, send_ref, rows):
    total = got_ref[0, pl.ds(0, PCHUNK), :]
    for c in range(1, COLS):
        total = total + got_ref[c, pl.ds(0, PCHUNK), :]
    for c in range(COLS):
        rows[pl.ds(16 * c, 16), :] = got_ref[c, pl.ds(PCHUNK, 16), :]
    parts = both_parts(rows)
    gram = lax.dot_general(
        parts, parts, (((1,), (1,)), ((), ())), precision=HIGH, preferred_element_type=F32
    )
    rows[pl.ds(0, 64), :] = jnp.zeros((64, LANES), F32)
    rows[pl.ds(0, 64), pl.ds(0, 64)] = gram
    for c in range(COLS):
        send_ref[c, pl.ds(0, PCHUNK), :] = total
        send_ref[c, pl.ds(PCHUNK, 8), :] = jnp.zeros((8, LANES), F32)
        send_ref[c, pl.ds(PCHUNK, 4), :] = rows[pl.ds(4 * c, 4), :]


def both_parts(rows):
    real, imag = (
        jnp.concatenate(
            [rows[pl.ds(2 * high + c, 32, stride=2 * HIGHS), :] for high in range(HIGHS)], axis=1
        )
        for c in range(2)
    )
    return jnp.concatenate([real, imag], axis=0)


def back_kernel(labels_ref, got_ref, rotated_ref, counts_ref, keep_ref, send_ref, weight, wh, wl, th, tl, hb):
    core = lax.axis_index("core")
    bits, y_bits, scale = masks_of(labels_ref)
    a_bits, b_bits = bits >> QB, bits & (RIGHT - 1)
    hb[...] = hadamard(lax.broadcasted_iota(jnp.int32, (RIGHT, RIGHT), 0), RIGHT, b_bits)

    def owners(shape):
        i = lax.broadcasted_iota(jnp.int32, shape, 0)
        half, z, own = i >> 7, (i >> 4) & 7, i & 15
        return z * 32 + (half ^ core) * 16 + own

    ha = hadamard(owners((LEFT, LEFT)), LEFT, a_bits)
    total = jnp.zeros((PCHUNK, LANES), F32)
    gram = jnp.zeros((8, LANES), F32)
    for c in range(COLS):
        total = total + got_ref[c, pl.ds(0, PCHUNK), :]
        gram = gram + got_ref[c, pl.ds(PCHUNK, 8), :]
    trace = jnp.sum(total)
    slope = (1.0 - mixing) / trace
    ratio_sum = jnp.zeros((16, LANES), F32)
    for high in range(HIGHS):
        count = counts_ref[pl.ds(high, LEFT, stride=HIGHS), :].astype(F32)
        for c in range(COLS):
            p = got_ref[c, pl.ds(16 * high, 16), :]
            w = count[16 * c : 16 * c + 16] / ((count_norm * ORDER) * (slope * p + mixing / ORDER))
            weight[pl.ds(16 * c, 16), pl.ds(high * LANES, LANES)] = w
            ratio_sum = ratio_sum + w * p
    ratio = jnp.sum(ratio_sum) / trace

    def one(i, carry):
        for n in range(2):
            part = pl.ds(n * 256, 256)
            wh[:, part], wl[:, part] = halves(
                (weight[:, part] - ratio) * scale * rotated_ref[i, :, part]
            )
        for n in range(2):
            part = pl.ds(n * 256, 256)
            first = jnp.dot(wh[...], hb[:, part], preferred_element_type=F32) + jnp.dot(
                wl[...], hb[:, part], preferred_element_type=F32
            )
            th[i, :, part], tl[i, :, part] = halves(first)
        return carry

    lax.fori_loop(0, 4, one, 0)
    row = owners((LEFT, LANES))
    for high in range(HIGHS):
        turns = quarter_turns(row, high, y_bits)
        swap = (turns & 1) == 1
        sign_real = jnp.where((turns == 1) | (turns == 2), -1.0, 1.0)
        sign_imag = jnp.where(turns >= 2, -1.0, 1.0)
        block = pl.ds(high * LANES, LANES)
        for r in range(2):
            real, imag = (
                jnp.dot(ha, th[2 * r + c, :, block], preferred_element_type=F32)
                + jnp.dot(ha, tl[2 * r + c, :, block], preferred_element_type=F32)
                for c in range(2)
            )
            for c, turned in (
                (0, sign_real * jnp.where(swap, imag, real)),
                (1, sign_imag * jnp.where(swap, real, imag)),
            ):
                for half, out in ((0, keep_ref), (1, send_ref)):
                    for z in range(ZS):
                        at = 128 * half + 16 * z
                        out[z, pl.ds(128 * r + 2 * high + c, 16, stride=2 * HIGHS), :] = turned[
                            at : at + 16
                        ]
    for z in range(ZS):
        keep_ref[z, pl.ds(256, 8), :] = gram
        send_ref[z, pl.ds(256, 8), :] = gram


def packed_kernel(got_ref, send_ref):
    total = got_ref[0]
    for z in range(1, ZS):
        total = total + got_ref[z]
    for c in range(COLS):
        for r in range(2):
            send_ref[c, pl.ds(8 * r, 8), :] = total[128 * r + 8 * c : 128 * r + 8 * c + 8]
        send_ref[c, pl.ds(16, 8), :] = total[256:264]


def update_kernel(got_ref, first_ref, velocity_ref, factor_ref_out, velocity_ref_out, rows, gram_ref, mixed_ref):
    for c in range(COLS):
        rows[pl.ds(16 * c, 16), :] = first_ref[c, pl.ds(PCHUNK, 16), :]
        gram_ref[pl.ds(4 * c, 4), :] = got_ref[c, pl.ds(16, 4), :]
    gram = gram_ref[:, pl.ds(0, 64)]
    i = lax.broadcasted_iota(jnp.int32, (64, 64), 0)
    j = lax.broadcasted_iota(jnp.int32, (64, 64), 1)
    turn = jnp.where(j == i + 32, -1.0, jnp.where(j == i - 32, 1.0, 0.0)).astype(F32)
    turned = jnp.dot(turn, gram, precision=HIGH, preferred_element_type=F32)
    turned = lax.dot_general(
        turned, turn, (((1,), (1,)), ((), ())), precision=HIGH, preferred_element_type=F32
    )
    whole = gram + turned
    trace = jnp.sum(jnp.where(i == j, gram, 0.0))
    purity = 0.5 * jnp.sum(whole * whole) / (trace * trace)
    mixed = jnp.dot(whole, both_parts(rows), precision=HIGH, preferred_element_type=F32)
    for high in range(HIGHS):
        for c in range(2):
            mixed_ref[pl.ds(2 * high + c, 32, stride=2 * HIGHS), :] = mixed[
                32 * c : 32 * c + 32, high * LANES : (high + 1) * LANES
            ]
    for c in range(COLS):
        at = pl.ds(16 * c, 16)
        own = rows[at, :]
        gradient = -((1.0 - mixing) / SETS) * got_ref[c, pl.ds(0, 16), :] + penalty * (
            2.0 * mixed_ref[at, :] / trace - 2.0 * purity * own
        )
        velocity = momentum * velocity_ref[at, :] + gradient
        velocity_ref_out[at, :] = velocity
        factor_ref_out[at, :] = own - step_size * velocity


def shape(*dims):
    return jax.ShapeDtypeStruct(dims, F32)


def call(kernel, name, out, n_in, scratch=(), scalars=0):
    return pl.pallas_call(
        kernel,
        name=name,
        out_shape=out,
        in_specs=[SMEM] * scalars + [VMEM] * (n_in - scalars),
        out_specs=jax.tree.map(lambda _: VMEM, out),
        scratch_shapes=list(scratch),
        compiler_params=pltpu.CompilerParams(vmem_limit_bytes=48 * 2**20),
    )


def exchange(array, axis):
    return lax.all_to_all(array, axis, split_axis=0, concat_axis=0, tiled=True)


def shards(factor, velocity, labels, counts):
    own = factor.reshape(2, 2, ROWS, LANES).transpose(0, 2, 1, 3).reshape(2, 2 * ROWS, LANES)
    counted = counts.reshape(ROWS, LANES)
    moved = velocity.reshape(32, 2, HIGHS, LANES).transpose(0, 2, 1, 3).reshape(256, LANES)
    matrix = (LEFT, RIGHT)
    rotated, sent = call(
        forward_kernel,
        "forward",
        (shape(4, *matrix), shape(COLS, PCHUNK + 16, LANES)),
        2,
        [
            pltpu.VMEM((4, *matrix), BF16),
            pltpu.VMEM((4, *matrix), BF16),
            pltpu.VMEM(matrix, BF16),
            pltpu.VMEM(matrix, BF16),
            pltpu.VMEM(matrix, F32),
            pltpu.VMEM((RIGHT, RIGHT), BF16),
        ],
        scalars=1,
    )(labels, own)
    first = exchange(sent, COL)
    sent = call(
        summed_kernel, "summed", shape(COLS, PCHUNK + 8, LANES), 1, [pltpu.VMEM((256, LANES), F32)]
    )(first)
    second = exchange(sent, COL)
    kept, sent = call(
        back_kernel,
        "back",
        (shape(ZS, 264, LANES), shape(ZS, 264, LANES)),
        4,
        [
            pltpu.VMEM(matrix, F32),
            pltpu.VMEM(matrix, BF16),
            pltpu.VMEM(matrix, BF16),
            pltpu.VMEM((4, *matrix), BF16),
            pltpu.VMEM((4, *matrix), BF16),
            pltpu.VMEM((RIGHT, RIGHT), BF16),
        ],
        scalars=1,
    )(labels, second, rotated, counted)
    pair = kept + lax.ppermute(sent, "core", [(0, 1), (1, 0)])
    third = exchange(pair, "z")
    sent = call(packed_kernel, "packed", shape(COLS, 24, LANES), 1)(third)
    fourth = exchange(sent, COL)
    new_factor, new_velocity = call(
        update_kernel,
        "update",
        (shape(256, LANES), shape(256, LANES)),
        3,
        [pltpu.VMEM((256, LANES), F32), pltpu.VMEM((64, LANES), F32), pltpu.VMEM((256, LANES), F32)],
    )(fourth, first, moved)

    def back_to_rows(array):
        return array.reshape(32, HIGHS, 2, LANES).transpose(0, 2, 1, 3).reshape(32, 2, RIGHT)

    return back_to_rows(new_factor), back_to_rows(new_velocity)


def solution(mesh):
    split = Mesh(mesh.devices.reshape(8, 2, 4, 4), ("z", "core", "y", "x"))
    every = ("z", "core", "y", "x")
    return jax.shard_map(
        shards,
        mesh=split,
        in_specs=(P(COL, None, None), P(None, None, every), P(SET, None), P(SET, None)),
        out_specs=(P(None, None, every), P(None, None, every)),
        check_vma=False,
    )
```

profile of v0, /device:TPU:8, one launch (start us, length us, event | category | flops | bytes accessed | tf_op | source)
XLA Modules:
  0.0 99.4 jit_solution(12806650543546760784)
XLA Ops:
  0.6 0.0 copy-start
  0.6 1.6 %copy-done = f32[2,2,131072]{2,1,0:T(2,128)S(1)} copy-done((f32[2,2,131072]{2,1,0:T(2,128)S(1)}, f32[2,2,131072]{2,1,0:T(2,128)}, u32[]{:S(2)}) %copy-start) | copy-done | bytes 2097176
  2.2 0.0 copy-start.3
  2.2 0.7 copy-done.3
  2.9 4.8 %forward.1 = (f32[4,256,512]{2,1,0:T(8,128)S(1)}, f32[16,80,128]{2,1,0:T(8,128)S(1)}) custom-call(s32[1,17]{1,0:T(1,128)S(1)} %copy-done.3, f32[2,2048,128]{2,1,0:T(8,128)S(1)} %bitcast.21), custom_call_target="tpu_custom_call" | custom-call | tf_op jit(solution)/shard_map/forward/pallas_call | solution.py:286
  7.7 18.4 %all_to_all.20.got_ref.first_ref = f32[16,80,128]{2,1,0:T(8,128)S(1)} all-to-all(f32[16,80,128]{2,1,0:T(8,128)S(1)} %get-tuple-element.8), channel_id=1, replica_groups=mesh['z'=8,'core'=2,'y'=4,'x'=4] {'y','x'}, dimensions={0} | all-to-all | bytes 1310720 | tf_op jit(solution)/shard_map/all_to_all | solution.py:278
  26.1 0.0 copy-start.1
  26.1 0.0 copy-start.4
  26.1 0.3 summed.1
  26.4 14.5 %all_to_all.21.got_ref = f32[16,72,128]{2,1,0:T(8,128)S(1)} all-to-all(f32[16,72,128]{2,1,0:T(8,128)S(1)} %summed.1), channel_id=1, replica_groups=mesh['z'=8,'core'=2,'y'=4,'x'=4] {'y','x'}, dimensions={0} | all-to-all | bytes 1179648 | tf_op jit(solution)/shard_map/all_to_all | solution.py:278
  40.9 0.0 copy-done.1
  41.0 0.0 copy-done.4
  41.0 5.1 %back.1 = (f32[8,264,128]{2,1,0:T(8,128)S(1)}, f32[8,264,128]{2,1,0:T(8,128)S(1)}) custom-call(s32[1,17]{1,0:T(1,128)S(1)} %copy-done.4, f32[16,72,128]{2,1,0:T(8,128)S(1)} %all_to_all.21.got_ref, f32[4,256,512]{2,1,0:T(8,128)S(1)} %get-tuple-element.9.rotated_ref, s32[1024,128]{1,0:T(8,128)S(1)} %bitcast.22), custom_call_target="tpu_custom_call" | custom-call | tf_op jit(solution)/shard_map/back/pallas_call | solution.py:306
  46.0 0.1 collective-permute-start
  46.1 2.7 %collective-permute-done = f32[8,264,128]{2,1,0:T(8,128)S(1)} collective-permute-done((f32[8,264,128]{2,1,0:T(8,128)S(1)}, f32[8,264,128]{2,1,0:T(8,128)S(1)}, u32[]{:S(2)}, u32[]{:S(2)}) %collective-permute-start) | collective-permute-done | bytes 1081376 | tf_op jit(solution)/shard_map/ppermute | solution.py:321
  48.8 0.1 add.3
  49.0 38.0 %all_to_all.22.got_ref = f32[8,264,128]{2,1,0:T(8,128)S(1)} all-to-all(f32[8,264,128]{2,1,0:T(8,128)S(1)} %add.3), channel_id=1, replica_groups=mesh['z'=8,'core'=2,'y'=4,'x'=4] {'z'}, dimensions={0} | all-to-all | bytes 2162688 | tf_op jit(solution)/shard_map/all_to_all | solution.py:278
  87.0 0.0 copy-start.2
  87.0 0.1 packed.1
  87.0 11.0 %all_to_all.23.got_ref = f32[16,24,128]{2,1,0:T(8,128)S(1)} all-to-all(f32[16,24,128]{2,1,0:T(8,128)S(1)} %packed.1), channel_id=1, replica_groups=mesh['z'=8,'core'=2,'y'=4,'x'=4] {'y','x'}, dimensions={0} | all-to-all | bytes 393216 | tf_op jit(solution)/shard_map/all_to_all | solution.py:278
  98.0 0.0 copy-done.2
  98.0 1.4 %update.1 = (f32[256,128]{1,0:T(8,128)}, f32[256,128]{1,0:T(8,128)}) custom-call(f32[16,24,128]{2,1,0:T(8,128)S(1)} %all_to_all.23.got_ref, f32[16,80,128]{2,1,0:T(8,128)S(1)} %all_to_all.20.got_ref.first_ref, f32[256,128]{1,0:T(8,128)S(1)} %bitcast.23), custom_call_target="tpu_custom_call" | custom-call | tf_op jit(solution)/shard_map/update/pallas_call | solution.py:325
Async XLA Ops:
  0.6 1.6 %copy-start = (f32[2,2,131072]{2,1,0:T(2,128)S(1)}, f32[2,2,131072]{2,1,0:T(2,128)}, u32[]{:S(2)}) copy-start(f32[2,2,131072]{2,1,0:T(2,128)} %param.4) | copy-start | bytes 6291460
  2.2 0.7 copy-start.3
  26.1 14.8 %copy-start.1 = (s32[1,131072]{1,0:T(1,128)S(1)}, s32[1,131072]{1,0:T(1,128)}, u32[]{:S(2)}) copy-start(s32[1,131072]{1,0:T(1,128)} %param.7) | copy-start | bytes 1572868
  26.1 14.8 %copy-start.4 = (s32[1,17]{1,0:T(1,128)S(1)}, s32[1,17]{1,0:T(1,128)}, u32[]{:S(2)}) copy-start(s32[1,17]{1,0:T(1,128)} %labels_ref.3) | copy-start | bytes 208
  46.0 2.8 %collective-permute-start = (f32[8,264,128]{2,1,0:T(8,128)S(1)}, f32[8,264,128]{2,1,0:T(8,128)S(1)}, u32[]{:S(2)}, u32[]{:S(2)}) collective-permute-start(f32[8,264,128]{2,1,0:T(8,128)S(1)} %get-tuple-element.11), channel_id=1, source_target_pairs={{0,16},{16,0},{1,17},{17,1},{2,18},{18,2},{3,19},{19,3},{4,20},{20... | collective-permute-start | bytes 3244040 | tf_op jit(solution)/shard_map/ppermute | solution.py:321
  87.0 11.0 %copy-start.2 = (f32[32,2,512]{2,1,0:T(2,128)S(1)}, f32[32,2,512]{2,1,0:T(2,128)}, u32[]{:S(2)}) copy-start(f32[32,2,512]{2,1,0:T(2,128)} %param.5) | copy-start | bytes 393220
where the time goes:
time: 100 us; the launch traced here: 99.4 us
  blocking collectives  82 us (82%)
  Pallas kernels  11.6 us (12%)
  waiting for transfers between devices  2.69 us (3%)
  local copies, waits for them, and re-layouts  2.25 us (2%)
    all_to_all x4, blocking collectives, exchange(): return lax.all_to_all(array, axis, split_axis=0, concat_axis=0, tiled=True)  82 us
    pallas_call x1, Pallas kernels, shards(): call(back_kernel, 'back', (shape(ZS, 264, LANES), shape(ZS, 264, LANES)),...  5.08 us
    pallas_call x1, Pallas kernels, shards(): call(forward_kernel, 'forward', (shape(4, *matrix), shape(COLS, PCHUNK +...  4.78 us
    ppermute x1, waiting for transfers between devices, shards(): pair = kept + lax.ppermute(sent, 'core', [(0, 1), (1, 0)])  2.69 us
    unnamed x10, local copies, waits for them, and re-layouts  2.25 us
  transfers between devices with their start and end apart: 1, of which 1 were waited for; matrix products, arithmetic and copies ran while one was open for 0% of the time, Pallas kernels for 0%

commit v1 on v0

--- a/solution.py
+++ b/solution.py
@@ -31,6 +31,9 @@
 BF16 = jnp.bfloat16
 HIGH = lax.Precision.HIGHEST
 PCHUNK = ROWS // COLS
+P1 = PCHUNK + 1
+MESSAGE = 17
+PEERS = 128
 VMEM = pl.BlockSpec(memory_space=pltpu.VMEM)
 SMEM = pl.BlockSpec(memory_space=pltpu.SMEM)
 
@@ -122,26 +125,36 @@
         total = total + got_ref[c, pl.ds(0, PCHUNK), :]
     for c in range(COLS):
         rows[pl.ds(16 * c, 16), :] = got_ref[c, pl.ds(PCHUNK, 16), :]
-    parts = both_parts(rows)
+    parts = jnp.concatenate(parts_of(rows), axis=0)
     gram = lax.dot_general(
         parts, parts, (((1,), (1,)), ((), ())), precision=HIGH, preferred_element_type=F32
     )
-    rows[pl.ds(0, 64), :] = jnp.zeros((64, LANES), F32)
-    rows[pl.ds(0, 64), pl.ds(0, 64)] = gram
-    for c in range(COLS):
-        send_ref[c, pl.ds(0, PCHUNK), :] = total
-        send_ref[c, pl.ds(PCHUNK, 8), :] = jnp.zeros((8, LANES), F32)
-        send_ref[c, pl.ds(PCHUNK, 4), :] = rows[pl.ds(4 * c, 4), :]
-
-
-def both_parts(rows):
-    real, imag = (
+    turn = quarter_turn()
+    turned = jnp.dot(turn, gram, precision=HIGH, preferred_element_type=F32)
+    turned = lax.dot_general(
+        turned, turn, (((1,), (1,)), ((), ())), precision=HIGH, preferred_element_type=F32
+    )
+    rows[pl.ds(0, 32), :] = jnp.zeros((32, LANES), F32)
+    rows[pl.ds(0, 32), pl.ds(0, 64)] = (gram + turned)[:32]
+    pairs = rows[pl.ds(0, 16, stride=2), :] + pltpu.roll(rows[pl.ds(1, 16, stride=2), :], 64, 1)
+    for c in range(COLS):
+        send_ref[pl.ds(P1 * c, PCHUNK), :] = total
+    send_ref[pl.ds(PCHUNK, 16, stride=P1), :] = pairs
+
+
+def quarter_turn():
+    i = lax.broadcasted_iota(jnp.int32, (64, 64), 0)
+    j = lax.broadcasted_iota(jnp.int32, (64, 64), 1)
+    return jnp.where(j == i + 32, -1.0, jnp.where(j == i - 32, 1.0, 0.0)).astype(F32)
+
+
+def parts_of(rows):
+    return tuple(
         jnp.concatenate(
             [rows[pl.ds(2 * high + c, 32, stride=2 * HIGHS), :] for high in range(HIGHS)], axis=1
         )
         for c in range(2)
     )
-    return jnp.concatenate([real, imag], axis=0)
 
 
 def back_kernel(labels_ref, got_ref, rotated_ref, counts_ref, keep_ref, send_ref, weight, wh, wl, th, tl, hb):
@@ -157,17 +170,17 @@
 
     ha = hadamard(owners((LEFT, LEFT)), LEFT, a_bits)
     total = jnp.zeros((PCHUNK, LANES), F32)
-    gram = jnp.zeros((8, LANES), F32)
-    for c in range(COLS):
-        total = total + got_ref[c, pl.ds(0, PCHUNK), :]
-        gram = gram + got_ref[c, pl.ds(PCHUNK, 8), :]
+    gram = jnp.zeros((1, LANES), F32)
+    for c in range(COLS):
+        total = total + got_ref[pl.ds(P1 * c, PCHUNK), :]
+        gram = gram + got_ref[pl.ds(P1 * c + PCHUNK, 1), :]
     trace = jnp.sum(total)
     slope = (1.0 - mixing) / trace
     ratio_sum = jnp.zeros((16, LANES), F32)
     for high in range(HIGHS):
         count = counts_ref[pl.ds(high, LEFT, stride=HIGHS), :].astype(F32)
         for c in range(COLS):
-            p = got_ref[c, pl.ds(16 * high, 16), :]
+            p = got_ref[pl.ds(P1 * c + 16 * high, 16), :]
             w = count[16 * c : 16 * c + 16] / ((count_norm * ORDER) * (slope * p + mixing / ORDER))
             weight[pl.ds(16 * c, 16), pl.ds(high * LANES, LANES)] = w
             ratio_sum = ratio_sum + w * p
@@ -206,56 +219,47 @@
                 (1, sign_imag * jnp.where(swap, real, imag)),
             ):
                 for half, out in ((0, keep_ref), (1, send_ref)):
-                    for z in range(ZS):
-                        at = 128 * half + 16 * z
-                        out[z, pl.ds(128 * r + 2 * high + c, 16, stride=2 * HIGHS), :] = turned[
-                            at : at + 16
-                        ]
-    for z in range(ZS):
-        keep_ref[z, pl.ds(256, 8), :] = gram
-        send_ref[z, pl.ds(256, 8), :] = gram
-
-
-def packed_kernel(got_ref, send_ref):
-    total = got_ref[0]
+                    out[pl.ds(8 * r + 2 * high + c, PEERS, stride=MESSAGE), :] = turned[
+                        PEERS * half : PEERS * (half + 1)
+                    ]
+    for out in (keep_ref, send_ref):
+        out[pl.ds(16, PEERS, stride=MESSAGE), :] = jnp.broadcast_to(gram, (PEERS, LANES))
+
+
+def update_kernel(got_ref, first_ref, velocity_ref, new_factor_ref, new_velocity_ref, rows, sums, gram_ref, mixed_ref):
+    block = COLS * MESSAGE
+    total = got_ref[pl.ds(0, block), :]
     for z in range(1, ZS):
-        total = total + got_ref[z]
-    for c in range(COLS):
-        for r in range(2):
-            send_ref[c, pl.ds(8 * r, 8), :] = total[128 * r + 8 * c : 128 * r + 8 * c + 8]
-        send_ref[c, pl.ds(16, 8), :] = total[256:264]
-
-
-def update_kernel(got_ref, first_ref, velocity_ref, factor_ref_out, velocity_ref_out, rows, gram_ref, mixed_ref):
+        total = total + got_ref[pl.ds(block * z, block), :]
+    sums[...] = total
     for c in range(COLS):
         rows[pl.ds(16 * c, 16), :] = first_ref[c, pl.ds(PCHUNK, 16), :]
-        gram_ref[pl.ds(4 * c, 4), :] = got_ref[c, pl.ds(16, 4), :]
+    pairs = sums[pl.ds(16, 16, stride=MESSAGE), :]
+    gram_ref[pl.ds(0, 16, stride=2), :] = pairs
+    gram_ref[pl.ds(1, 16, stride=2), :] = pltpu.roll(pairs, 64, 1)
     gram = gram_ref[:, pl.ds(0, 64)]
-    i = lax.broadcasted_iota(jnp.int32, (64, 64), 0)
-    j = lax.broadcasted_iota(jnp.int32, (64, 64), 1)
-    turn = jnp.where(j == i + 32, -1.0, jnp.where(j == i - 32, 1.0, 0.0)).astype(F32)
-    turned = jnp.dot(turn, gram, precision=HIGH, preferred_element_type=F32)
-    turned = lax.dot_general(
-        turned, turn, (((1,), (1,)), ((), ())), precision=HIGH, preferred_element_type=F32
-    )
-    whole = gram + turned
+    i = lax.broadcasted_iota(jnp.int32, (32, 64), 0)
+    j = lax.broadcasted_iota(jnp.int32, (32, 64), 1)
     trace = jnp.sum(jnp.where(i == j, gram, 0.0))
-    purity = 0.5 * jnp.sum(whole * whole) / (trace * trace)
-    mixed = jnp.dot(whole, both_parts(rows), precision=HIGH, preferred_element_type=F32)
-    for high in range(HIGHS):
-        for c in range(2):
+    purity = jnp.sum(gram * gram) / (trace * trace)
+    real, imag = parts_of(rows)
+    for c, parts in ((0, (real, imag)), (1, (imag, -real))):
+        mixed = jnp.dot(
+            gram, jnp.concatenate(parts, axis=0), precision=HIGH, preferred_element_type=F32
+        )
+        for high in range(HIGHS):
             mixed_ref[pl.ds(2 * high + c, 32, stride=2 * HIGHS), :] = mixed[
-                32 * c : 32 * c + 32, high * LANES : (high + 1) * LANES
+                :, high * LANES : (high + 1) * LANES
             ]
     for c in range(COLS):
         at = pl.ds(16 * c, 16)
         own = rows[at, :]
-        gradient = -((1.0 - mixing) / SETS) * got_ref[c, pl.ds(0, 16), :] + penalty * (
+        gradient = -((1.0 - mixing) / SETS) * sums[pl.ds(MESSAGE * c, 16), :] + penalty * (
             2.0 * mixed_ref[at, :] / trace - 2.0 * purity * own
         )
         velocity = momentum * velocity_ref[at, :] + gradient
-        velocity_ref_out[at, :] = velocity
-        factor_ref_out[at, :] = own - step_size * velocity
+        new_velocity_ref[at, :] = velocity
+        new_factor_ref[at, :] = own - step_size * velocity
 
 
 def shape(*dims):
@@ -276,6 +280,10 @@
 
 def exchange(array, axis):
     return lax.all_to_all(array, axis, split_axis=0, concat_axis=0, tiled=True)
+
+
+def exchange_flat(array, axis, peers):
+    return exchange(array.reshape(peers, 1, -1), axis).reshape(array.shape)
 
 
 def shards(factor, velocity, labels, counts):
@@ -300,13 +308,13 @@
     )(labels, own)
     first = exchange(sent, COL)
     sent = call(
-        summed_kernel, "summed", shape(COLS, PCHUNK + 8, LANES), 1, [pltpu.VMEM((256, LANES), F32)]
+        summed_kernel, "summed", shape(COLS * P1, LANES), 1, [pltpu.VMEM((256, LANES), F32)]
     )(first)
-    second = exchange(sent, COL)
+    second = exchange_flat(sent, COL, COLS)
     kept, sent = call(
         back_kernel,
         "back",
-        (shape(ZS, 264, LANES), shape(ZS, 264, LANES)),
+        (shape(PEERS * MESSAGE, LANES), shape(PEERS * MESSAGE, LANES)),
         4,
         [
             pltpu.VMEM(matrix, F32),
@@ -319,16 +327,19 @@
         scalars=1,
     )(labels, second, rotated, counted)
     pair = kept + lax.ppermute(sent, "core", [(0, 1), (1, 0)])
-    third = exchange(pair, "z")
-    sent = call(packed_kernel, "packed", shape(COLS, 24, LANES), 1)(third)
-    fourth = exchange(sent, COL)
+    third = exchange_flat(pair, ("z", *COL), PEERS)
     new_factor, new_velocity = call(
         update_kernel,
         "update",
         (shape(256, LANES), shape(256, LANES)),
         3,
-        [pltpu.VMEM((256, LANES), F32), pltpu.VMEM((64, LANES), F32), pltpu.VMEM((256, LANES), F32)],
-    )(fourth, first, moved)
+        [
+            pltpu.VMEM((256, LANES), F32),
+            pltpu.VMEM((COLS * MESSAGE, LANES), F32),
+            pltpu.VMEM((32, LANES), F32),
+            pltpu.VMEM((256, LANES), F32),
+        ],
+    )(third, first, moved)
 
     def back_to_rows(array):
         return array.reshape(32, HIGHS, 2, LANES).transpose(0, 2, 1, 3).reshape(32, 2, RIGHT)

time: 100 us -> 95.6 us (0.956)
  blocking collectives: 82 us -> 77.8 us
    all_to_all x4 -> x3, blocking collectives: 82 us -> 77.8 us  [exchange(): return lax.all_to_all(array, axis, split_axis=0, concat_axis=0, tiled=True)]
    pallas_call x3 -> x2, Pallas kernels: 5.42 us -> 5.78 us  [the longest x1 5 us: shards(): call(back_kernel, 'back', (shape(PEERS * MESSAGE, LANES), shape(PEERS * M...]
where the time goes in v1:
time: 95.6 us; the launch traced here: 95.4 us
  blocking collectives  77.8 us (81%)
  Pallas kernels  11.7 us (12%)
  waiting for transfers between devices  2.74 us (3%)
  local copies, waits for them, and re-layouts  2.25 us (2%)
    all_to_all x3, blocking collectives, exchange(): return lax.all_to_all(array, axis, split_axis=0, concat_axis=0, tiled=True)  77.8 us
    pallas_call x1, Pallas kernels, shards(): call(back_kernel, 'back', (shape(PEERS * MESSAGE, LANES), shape(PEERS * M...  5 us
    pallas_call x1, Pallas kernels, shards(): call(forward_kernel, 'forward', (shape(4, *matrix), shape(COLS, PCHUNK +...  4.78 us
    ppermute x1, waiting for transfers between devices, shards(): pair = kept + lax.ppermute(sent, 'core', [(0, 1), (1, 0)])  2.74 us
    unnamed x10, local copies, waits for them, and re-layouts  2.25 us
  transfers between devices with their start and end apart: 1, of which 1 were waited for; matrix products, arithmetic and copies ran while one was open for 0% of the time, Pallas kernels for 0%

profile of v1, /device:TPU:8, one launch (start us, length us, event | category | flops | bytes accessed | tf_op | source)
XLA Modules:
  0.0 95.4 jit_solution(16409012160970453176)
XLA Ops:
  0.6 0.0 copy-start
  0.6 1.6 %copy-done = f32[2,2,131072]{2,1,0:T(2,128)S(1)} copy-done((f32[2,2,131072]{2,1,0:T(2,128)S(1)}, f32[2,2,131072]{2,1,0:T(2,128)}, u32[]{:S(2)}) %copy-start) | copy-done | bytes 2097176
  2.2 0.0 copy-start.3
  2.2 0.7 copy-done.3
  2.9 4.8 %forward.1 = (f32[4,256,512]{2,1,0:T(8,128)S(1)}, f32[16,80,128]{2,1,0:T(8,128)S(1)}) custom-call(s32[1,17]{1,0:T(1,128)S(1)} %copy-done.3, f32[2,2048,128]{2,1,0:T(8,128)S(1)} %bitcast.28), custom_call_target="tpu_custom_call" | custom-call | tf_op jit(solution)/shard_map/forward/pallas_call | solution.py:294
  7.7 18.4 %all_to_all.15.got_ref.first_ref = f32[16,80,128]{2,1,0:T(8,128)S(1)} all-to-all(f32[16,80,128]{2,1,0:T(8,128)S(1)} %get-tuple-element.8), channel_id=1, replica_groups=mesh['z'=8,'core'=2,'y'=4,'x'=4] {'y','x'}, dimensions={0} | all-to-all | bytes 1310720 | tf_op jit(solution)/shard_map/all_to_all | solution.py:282
  26.1 0.0 copy-start.1
  26.1 0.0 copy-start.4
  26.1 0.8 summed.1
  26.9 14.2 %all_to_all.16 = f32[16,1,8320]{2,1,0:T(1,128)S(1)} all-to-all(f32[16,1,8320]{2,1,0:T(1,128)S(1)} %bitcast.26), channel_id=1, replica_groups=mesh['z'=8,'core'=2,'y'=4,'x'=4] {'y','x'}, dimensions={0} | all-to-all | bytes 1064960 | tf_op jit(solution)/shard_map/all_to_all | solution.py:282
  41.1 0.0 copy-done.1
  41.1 0.0 copy-done.4
  41.1 5.0 %back.1 = (f32[2176,128]{1,0:T(8,128)S(1)}, f32[2176,128]{1,0:T(8,128)S(1)}) custom-call(s32[1,17]{1,0:T(1,128)S(1)} %copy-done.4, f32[1040,128]{1,0:T(8,128)S(1)} %bitcast.27, f32[4,256,512]{2,1,0:T(8,128)S(1)} %get-tuple-element.9.rotated_ref, s32[1024,128]{1,0:T(8,128)S(1)} %bitcast.29), custom_call_target="tpu_custom_call" | custom-call | tf_op jit(solution)/shard_map/back/pallas_call | solution.py:314
  46.1 0.1 collective-permute-start
  46.2 2.7 %collective-permute-done = f32[2176,128]{1,0:T(8,128)S(1)} collective-permute-done((f32[2176,128]{1,0:T(8,128)S(1)}, f32[2176,128]{1,0:T(8,128)S(1)}, u32[]{:S(2)}, u32[]{:S(2)}) %collective-permute-start) | collective-permute-done | bytes 1114144 | tf_op jit(solution)/shard_map/ppermute | solution.py:329
  48.9 0.1 add.3
  49.1 0.0 copy-start.2
  49.1 45.2 %all_to_all.17 = f32[128,1,2176]{2,1,0:T(1,128)S(1)} all-to-all(f32[128,1,2176]{2,1,0:T(1,128)S(1)} %bitcast.31), channel_id=1, replica_groups=mesh['z'=8,'core'=2,'y'=4,'x'=4] {'z','y','x'}, dimensions={0} | all-to-all | bytes 2228224 | tf_op jit(solution)/shard_map/all_to_all | solution.py:282
  94.2 0.0 copy-done.2
  94.3 1.1 %update.1 = (f32[256,128]{1,0:T(8,128)}, f32[256,128]{1,0:T(8,128)}) custom-call(f32[2176,128]{1,0:T(8,128)S(1)} %bitcast.25, f32[16,80,128]{2,1,0:T(8,128)S(1)} %all_to_all.15.got_ref.first_ref, f32[256,128]{1,0:T(8,128)S(1)} %bitcast.30), custom_call_target="tpu_custom_call" | custom-call | tf_op jit(solution)/shard_map/update/pallas_call | solution.py:331
Async XLA Ops:
  0.6 1.6 %copy-start = (f32[2,2,131072]{2,1,0:T(2,128)S(1)}, f32[2,2,131072]{2,1,0:T(2,128)}, u32[]{:S(2)}) copy-start(f32[2,2,131072]{2,1,0:T(2,128)} %param.4) | copy-start | bytes 6291460
  2.2 0.7 copy-start.3
  26.1 15.0 %copy-start.1 = (s32[1,131072]{1,0:T(1,128)S(1)}, s32[1,131072]{1,0:T(1,128)}, u32[]{:S(2)}) copy-start(s32[1,131072]{1,0:T(1,128)} %param.7) | copy-start | bytes 1572868
  26.1 15.0 %copy-start.4 = (s32[1,17]{1,0:T(1,128)S(1)}, s32[1,17]{1,0:T(1,128)}, u32[]{:S(2)}) copy-start(s32[1,17]{1,0:T(1,128)} %labels_ref.3) | copy-start | bytes 208
  46.1 2.8 %collective-permute-start = (f32[2176,128]{1,0:T(8,128)S(1)}, f32[2176,128]{1,0:T(8,128)S(1)}, u32[]{:S(2)}, u32[]{:S(2)}) collective-permute-start(f32[2176,128]{1,0:T(8,128)S(1)} %get-tuple-element.11), channel_id=1, source_target_pairs={{0,16},{16,0},{1,17},{17,1},{2,18},{18,2},{3,19},{19,3},{4,20},{20... | collective-permute-start | bytes 3342344 | tf_op jit(solution)/shard_map/ppermute | solution.py:329
  49.1 45.2 %copy-start.2 = (f32[32,2,512]{2,1,0:T(2,128)S(1)}, f32[32,2,512]{2,1,0:T(2,128)}, u32[]{:S(2)}) copy-start(f32[32,2,512]{2,1,0:T(2,128)} %param.5) | copy-start | bytes 393220

commit v2 on v1

v2 whole, which is shorter than its diff:
```python
import functools

import jax
import jax.numpy as jnp
from jax import lax
from jax.experimental import pallas as pl
from jax.experimental.pallas import tpu as pltpu
from jax.sharding import Mesh
from jax.sharding import PartitionSpec as P

QA, QB, QUBITS = 8, 9, 17
ORDER = 2**QUBITS
LEFT, RIGHT = 2**QA, 2**QB
LANES = 128
HIGHS = RIGHT // LANES
ROWS = ORDER // LANES
COLS = 16
SETS = 16
PAIRS = 4

COL = ("y", "x")
SET = ("zh", "zl", "core")

mixing = 0.1
penalty = 8.0
momentum = 0.9
step_size = 0.5
count_norm = 8.0

F32 = jnp.float32
BF16 = jnp.bfloat16
HIGH = lax.Precision.HIGHEST
PCHUNK = ROWS // COLS
P1 = PCHUNK + 1
MESSAGE = 17
PEERS = 64
VMEM = pl.BlockSpec(memory_space=pltpu.VMEM)
SMEM = pl.BlockSpec(memory_space=pltpu.SMEM)
HBM = pl.BlockSpec(memory_space=pltpu.HBM)


def halves(x):
    high = x.astype(BF16)
    return high, (x - high.astype(F32)).astype(BF16)


def two_pass(high, low, matrix):
    return jnp.dot(high, matrix, preferred_element_type=F32) + jnp.dot(
        low, matrix, preferred_element_type=F32
    )


def masks_of(labels_ref):
    rotated_bits = jnp.int32(0)
    y_bits = jnp.int32(0)
    scale = jnp.float32(1.0)
    for q in range(QUBITS):
        label = labels_ref[0, q]
        bit = jnp.int32(1 << (QUBITS - 1 - q))
        rotated_bits = rotated_bits + jnp.where(label == 2, 0, bit)
        y_bits = y_bits + jnp.where(label == 1, bit, 0)
        scale = scale * jnp.where(label == 2, jnp.float32(1.0), jnp.float32(0.5))
    return rotated_bits, y_bits, scale


def tall(tile, rows):
    return jnp.concatenate([tile] * (rows // 8), axis=0)


def store_hadamard(ref, size, bits):
    row = lax.broadcasted_iota(jnp.int32, (LANES, LANES), 0)
    col = lax.broadcasted_iota(jnp.int32, (LANES, LANES), 1)
    lower = tall(bits & (LANES - 1), LANES)
    odd = lax.population_count(row & col & lower) & 1
    same = ((row ^ col) & (LANES - 1 - lower)) == 0
    block = jnp.where(same, (1 - 2 * odd).astype(F32), 0.0)
    count = size // LANES
    signs = {}
    for t in range(2):
        here = ((bits >> (7 + t)) & 1).astype(F32)
        signs[t] = {(0, 0): 1.0, (0, 1): here, (1, 0): here, (1, 1): 1.0 - 2.0 * here}
    for i in range(count):
        for j in range(count):
            sign = signs[0][i & 1, j & 1] * signs[1][i >> 1, j >> 1] * jnp.ones((8, LANES), F32)
            ref[pl.ds(LANES * i, LANES), pl.ds(LANES * j, LANES)] = (
                block * tall(sign, LANES)
            ).astype(BF16)


STEP = 64


def forward_kernel(labels_hbm, factor_hbm, rotated_ref, send_ref, masks_ref, scale_ref, labels_ref, factor_ref, xh, xl, th, tl, prob, ha, hb, sems):
    copies = [
        pltpu.make_async_copy(labels_hbm, labels_ref, sems.at[0]),
        pltpu.make_async_copy(factor_hbm, factor_ref, sems.at[1]),
    ]
    for copy in copies:
        copy.start()
    set_index = (lax.axis_index("zh") * 2 + lax.axis_index("zl")) * 2 + lax.axis_index("core")
    copies[0].wait()
    bits, y_bits, scale = masks_of(labels_ref)
    masks_ref[0] = jnp.full((8, LANES), bits, jnp.int32)
    masks_ref[1] = jnp.full((8, LANES), y_bits, jnp.int32)
    scale_ref[...] = jnp.full((8, LANES), scale, F32)
    store_hadamard(hb, RIGHT, masks_ref[0] & (RIGHT - 1))
    store_hadamard(ha, LEFT, masks_ref[0] >> QB)
    prob[...] = jnp.zeros_like(prob)
    copies[1].wait()
    lane = lax.broadcasted_iota(jnp.int32, (8, LANES), 1)

    def turned(step, carry):
        row = lax.broadcasted_iota(jnp.int32, (STEP, LANES), 0) + step * STEP
        left_turns = lax.population_count((row * RIGHT) & y_bits)
        to = pl.ds(pl.multiple_of(step * STEP, STEP), STEP)
        for high in range(HIGHS):
            right_turns = lax.population_count((lane + high * LANES) & y_bits)
            turns = (left_turns + jnp.concatenate([right_turns] * (STEP // 8), axis=0)) & 3
            swap = (turns & 1) == 1
            sign_real = jnp.where(turns >= 2, -1.0, 1.0)
            sign_imag = jnp.where(((turns + 1) & 2) == 2, -1.0, 1.0)
            block = pl.ds(high * LANES, LANES)
            for r in range(2):
                real, imag = (
                    factor_ref[r, pl.ds(step * (STEP * 8) + 2 * high + c, STEP, stride=8), :]
                    for c in range(2)
                )
                for c, value in (
                    (0, sign_real * jnp.where(swap, imag, real)),
                    (1, sign_imag * jnp.where(swap, real, imag)),
                ):
                    xh[2 * r + c, to, block], xl[2 * r + c, to, block] = halves(value)
        return carry

    lax.fori_loop(0, LEFT // STEP, turned, 0)

    def one(i, carry):
        for n in range(2):
            part = pl.ds(n * 256, 256)
            first = jnp.dot(ha[...], xh[i, :, part], preferred_element_type=F32) + jnp.dot(
                ha[...], xl[i, :, part], preferred_element_type=F32
            )
            th[:, part], tl[:, part] = halves(first)
        for n in range(2):
            part = pl.ds(n * 256, 256)
            second = two_pass(th[...], tl[...], hb[:, part])
            rotated_ref[i, :, part] = second
            prob[:, part] += second * second
        return carry

    lax.fori_loop(0, 4, one, 0)
    for c in range(COLS):
        for high in range(HIGHS):
            send_ref[c, pl.ds(16 * high, 16), :] = (
                prob[pl.ds(16 * c, 16), pl.ds(high * LANES, LANES)] * scale
            )
        start = pl.multiple_of(set_index * (ROWS * 2 // SETS) + 8 * c, 8)
        for r in range(2):
            send_ref[c, pl.ds(PCHUNK + 8 * r, 8), :] = factor_ref[r, pl.ds(start, 8), :]


def prepare(masks_ref, scale_ref, ha_ref, hb_ref, cosine_ref, sine_ref, ha):
    core, parity = lax.axis_index("core"), lax.axis_index("zl")
    bits, y_bits = masks_ref[0], masks_ref[1]
    store_hadamard(hb_ref, RIGHT, bits & (RIGHT - 1))
    store_hadamard(ha, LEFT, bits >> QB)
    lane = lax.broadcasted_iota(jnp.int32, (8, LANES), 1)
    row = lax.broadcasted_iota(jnp.int32, (16, LANES), 0)
    right_turns = [
        tall(lax.population_count((lane + high * LANES) & y_bits), 16) for high in range(HIGHS)
    ]
    y_tall, scale = tall(y_bits, 16), tall(scale_ref[...], 16)
    for half in range(2):
        for kept in range(2):
            for pair in range(PAIRS):
                z = 2 * pair + (parity ^ kept)
                start = pl.multiple_of(z * 32 + (core ^ half) * 16, 16)
                at = 128 * half + 64 * kept + 16 * pair
                ha_ref[pl.ds(at, 16), :] = ha[pl.ds(start, 16), :]
                left_turns = lax.population_count(((row + start) * RIGHT) & y_tall)
                for high in range(HIGHS):
                    turns = (left_turns + right_turns[high]) & 3
                    to = pl.ds(high * LANES, LANES)
                    signed = jnp.where(turns >= 2, -scale, scale)
                    odd = (turns & 1) == 1
                    cosine_ref[pl.ds(at, 16), to] = jnp.where(odd, 0.0, signed)
                    sine_ref[pl.ds(at, 16), to] = jnp.where(odd, signed, 0.0)


def parts_of(rows):
    return tuple(
        jnp.concatenate(
            [rows[pl.ds(2 * high + c, 32, stride=2 * HIGHS), :] for high in range(HIGHS)], axis=1
        )
        for c in range(2)
    )


def summed_kernel(got_ref, send_ref, rows):
    total = got_ref[0, pl.ds(0, PCHUNK), :]
    for c in range(1, COLS):
        total = total + got_ref[c, pl.ds(0, PCHUNK), :]
    for c in range(COLS):
        rows[pl.ds(16 * c, 16), :] = got_ref[c, pl.ds(PCHUNK, 16), :]
    parts = jnp.concatenate(parts_of(rows), axis=0)
    gram = lax.dot_general(
        parts, parts, (((1,), (1,)), ((), ())), precision=HIGH, preferred_element_type=F32
    )
    turn = quarter_turn()
    turned = jnp.dot(turn, gram, precision=HIGH, preferred_element_type=F32)
    turned = lax.dot_general(
        turned, turn, (((1,), (1,)), ((), ())), precision=HIGH, preferred_element_type=F32
    )
    rows[pl.ds(0, 32), :] = jnp.zeros((32, LANES), F32)
    rows[pl.ds(0, 32), pl.ds(0, 64)] = (gram + turned)[:32]
    pairs = rows[pl.ds(0, 16, stride=2), :] + pltpu.roll(rows[pl.ds(1, 16, stride=2), :], 64, 1)
    for c in range(COLS):
        send_ref[pl.ds(P1 * c, PCHUNK), :] = total
    send_ref[pl.ds(PCHUNK, 16, stride=P1), :] = pairs


def quarter_turn():
    i = lax.broadcasted_iota(jnp.int32, (64, 64), 0)
    j = lax.broadcasted_iota(jnp.int32, (64, 64), 1)
    return jnp.where(j == i + 32, -1.0, jnp.where(j == i - 32, 1.0, 0.0)).astype(F32)


def unrotated(r, weight_ref, rotated_ref, ha_ref, hb_ref, cosine_ref, sine_ref, keep_ref, send_ref, wh, wl, th, tl):
    for c in range(2):
        for n in range(2):
            part = pl.ds(n * 256, 256)
            wh[:, part], wl[:, part] = halves(weight_ref[:, part] * rotated_ref[2 * r + c, :, part])
        for n in range(2):
            part = pl.ds(n * 256, 256)
            th[c, :, part], tl[c, :, part] = halves(two_pass(wh[...], wl[...], hb_ref[:, part]))
    for high in range(HIGHS):
        block = pl.ds(high * LANES, LANES)
        real, imag = (
            jnp.dot(ha_ref[...], th[c, :, block], preferred_element_type=F32)
            + jnp.dot(ha_ref[...], tl[c, :, block], preferred_element_type=F32)
            for c in range(2)
        )
        cosine, sine = cosine_ref[:, block], sine_ref[:, block]
        for c, value in ((0, cosine * real - sine * imag), (1, cosine * imag + sine * real)):
            for half, out in ((0, keep_ref), (1, send_ref)):
                for kept in range(2):
                    at = 128 * half + 64 * kept
                    out[kept, 2 * high + c] = value[at : at + 64]


def back_first_kernel(got_ref, counts_ref, rotated_ref, masks_ref, scale_ref, keep_ref, send_ref, weight_ref, ha_ref, hb_ref, cosine_ref, sine_ref, wh, wl, th, tl, ha):
    prepare(masks_ref, scale_ref, ha_ref, hb_ref, cosine_ref, sine_ref, ha)
    total = jnp.zeros((PCHUNK, LANES), F32)
    gram = jnp.zeros((1, LANES), F32)
    for c in range(COLS):
        total = total + got_ref[pl.ds(P1 * c, PCHUNK), :]
        gram = gram + got_ref[pl.ds(P1 * c + PCHUNK, 1), :]
    trace = jnp.sum(total)
    slope = (1.0 - mixing) / trace
    ratio_sum = jnp.zeros((16, LANES), F32)
    for c in range(COLS):
        for high in range(HIGHS):
            count = counts_ref[pl.ds(64 * c + high, 16, stride=HIGHS), :].astype(F32)
            p = got_ref[pl.ds(P1 * c + 16 * high, 16), :]
            w = count / ((slope * p + mixing / ORDER) * (count_norm * ORDER))
            weight_ref[pl.ds(16 * c, 16), pl.ds(high * LANES, LANES)] = w
            ratio_sum = ratio_sum + w * p
    weight_ref[...] = weight_ref[...] - jnp.sum(ratio_sum) / trace
    unrotated(0, weight_ref, rotated_ref, ha_ref, hb_ref, cosine_ref, sine_ref, keep_ref, send_ref, wh, wl, th, tl)
    for out in (keep_ref, send_ref):
        for kept in range(2):
            out[kept, 8] = jnp.broadcast_to(gram, (PEERS, LANES))


def back_second_kernel(weight_ref, *refs):
    unrotated(1, weight_ref, *refs)


def merged_kernel(mine_a, got_a, mine_b, got_b, send_ref):
    for j in range(8):
        send_ref[pl.ds(j, PEERS, stride=MESSAGE), :] = mine_a[j] + got_a[j]
        send_ref[pl.ds(8 + j, PEERS, stride=MESSAGE), :] = mine_b[j] + got_b[j]
    send_ref[pl.ds(16, PEERS, stride=MESSAGE), :] = mine_a[8] + got_a[8]


def update_kernel(got_ref, first_ref, velocity_ref, new_factor_ref, new_velocity_ref, rows, sums, gram_ref, mixed_ref):
    block = COLS * MESSAGE
    total = got_ref[pl.ds(0, block), :]
    for pair in range(1, PAIRS):
        total = total + got_ref[pl.ds(block * pair, block), :]
    sums[...] = total
    for c in range(COLS):
        rows[pl.ds(16 * c, 16), :] = first_ref[c, pl.ds(PCHUNK, 16), :]
    pairs = sums[pl.ds(16, 16, stride=MESSAGE), :]
    gram_ref[pl.ds(0, 16, stride=2), :] = pairs
    gram_ref[pl.ds(1, 16, stride=2), :] = pltpu.roll(pairs, 64, 1)
    gram = gram_ref[:, pl.ds(0, 64)]
    i = lax.broadcasted_iota(jnp.int32, (32, 64), 0)
    j = lax.broadcasted_iota(jnp.int32, (32, 64), 1)
    trace = jnp.sum(jnp.where(i == j, gram, 0.0))
    purity = jnp.sum(gram * gram) / (trace * trace)
    real, imag = parts_of(rows)
    for c, parts in ((0, (real, imag)), (1, (imag, -real))):
        mixed = jnp.dot(
            gram, jnp.concatenate(parts, axis=0), precision=HIGH, preferred_element_type=F32
        )
        for high in range(HIGHS):
            mixed_ref[pl.ds(2 * high + c, 32, stride=2 * HIGHS), :] = mixed[
                :, high * LANES : (high + 1) * LANES
            ]
    for c in range(COLS):
        at = pl.ds(16 * c, 16)
        own = rows[at, :]
        gradient = -((1.0 - mixing) / SETS) * sums[pl.ds(MESSAGE * c, 16), :] + penalty * (
            2.0 * mixed_ref[at, :] / trace - 2.0 * purity * own
        )
        velocity = momentum * velocity_ref[at, :] + gradient
        new_velocity_ref[at, :] = velocity
        new_factor_ref[at, :] = own - step_size * velocity


def shape(*dims, dtype=F32):
    return jax.ShapeDtypeStruct(dims, dtype)


def call(kernel, name, out, specs, scratch=(), flops=0, moved=0, vmem=16 * 2**20):
    return pl.pallas_call(
        kernel,
        name=name,
        out_shape=out,
        in_specs=specs,
        out_specs=jax.tree.map(lambda _: VMEM, out),
        scratch_shapes=list(scratch),
        compiler_params=pltpu.CompilerParams(vmem_limit_bytes=vmem),
        cost_estimate=pl.CostEstimate(flops=flops, bytes_accessed=moved, transcendentals=0),
    )


def exchange(array, axis):
    return lax.all_to_all(array, axis, split_axis=0, concat_axis=0, tiled=True)


def exchange_flat(array, axis, peers):
    return exchange(array.reshape(peers, 1, -1), axis).reshape(array.shape)


def shards(factor, velocity, labels, counts):
    own = factor.reshape(2, 2, ROWS, LANES).transpose(0, 2, 1, 3).reshape(2, 2 * ROWS, LANES)
    moved = velocity.reshape(32, 2, HIGHS, LANES).transpose(0, 2, 1, 3).reshape(256, LANES)
    matrix = (LEFT, RIGHT)
    rotated, sent, masks, scale = call(
        forward_kernel,
        "forward",
        (
            shape(4, *matrix),
            shape(COLS, PCHUNK + 16, LANES),
            shape(2, 8, LANES, dtype=jnp.int32),
            shape(8, LANES),
        ),
        [HBM, HBM],
        [
            pltpu.SMEM((1, QUBITS), jnp.int32),
            pltpu.VMEM((2, 2 * ROWS, LANES), F32),
            pltpu.VMEM((4, *matrix), BF16),
            pltpu.VMEM((4, *matrix), BF16),
            pltpu.VMEM(matrix, BF16),
            pltpu.VMEM(matrix, BF16),
            pltpu.VMEM(matrix, F32),
            pltpu.VMEM((LEFT, LEFT), BF16),
            pltpu.VMEM((RIGHT, RIGHT), BF16),
            pltpu.SemaphoreType.DMA((2,)),
        ],
        flops=2 * 10**9,
        moved=7 * 10**6,
        vmem=int(40 * 2**20),
    )(labels, own)
    first = exchange(sent, COL)
    sent = call(
        summed_kernel,
        "summed",
        shape(COLS * P1, LANES),
        [VMEM],
        [pltpu.VMEM((256, LANES), F32)],
        flops=10**7,
        moved=10**6,
    )(first)
    second = exchange_flat(sent, COL, COLS)
    back_scratch = [
        pltpu.VMEM(matrix, BF16),
        pltpu.VMEM(matrix, BF16),
        pltpu.VMEM((2, *matrix), BF16),
        pltpu.VMEM((2, *matrix), BF16),
    ]
    keep_a, send_a, weight, *forms = call(
        back_first_kernel,
        "back_first",
        (
            shape(2, 9, PEERS, LANES),
            shape(2, 9, PEERS, LANES),
            shape(*matrix),
            shape(LEFT, LEFT, dtype=BF16),
            shape(RIGHT, RIGHT, dtype=BF16),
            shape(*matrix),
            shape(*matrix),
        ),
        [VMEM] * 5,
        [*back_scratch, pltpu.VMEM((LEFT, LEFT), BF16)],
        flops=10**9,
        moved=4 * 10**6,
    )(second, counts.reshape(ROWS, LANES), rotated, masks, scale)
    swap = [(0, 1), (1, 0)]
    got_a = lax.ppermute(send_a, "core", swap)
    keep_b, send_b = call(
        back_second_kernel,
        "back_second",
        (shape(2, 8, PEERS, LANES), shape(2, 8, PEERS, LANES)),
        [VMEM] * 6,
        back_scratch,
        flops=10**9,
        moved=4 * 10**6,
    )(weight, rotated, *forms)
    got_b = lax.ppermute(send_b, "core", swap)
    pair_a = lax.ppermute(keep_a[1] + got_a[1], "zl", swap)
    pair_b = lax.ppermute(
        keep_b[1] + got_b[1], ("zh", "zl"), [(z, (z + (1 if z % 2 else -1)) % 8) for z in range(8)]
    )
    sent = call(
        merged_kernel,
        "merged",
        shape(PEERS * MESSAGE, LANES),
        [VMEM] * 4,
        flops=10**6,
        moved=2 * 10**6,
    )(keep_a[0] + got_a[0], pair_a, keep_b[0] + got_b[0], pair_b)
    third = exchange_flat(sent, ("zh", *COL), PEERS)
    new_factor, new_velocity = call(
        update_kernel,
        "update",
        (shape(256, LANES), shape(256, LANES)),
        [VMEM] * 3,
        [
            pltpu.VMEM((256, LANES), F32),
            pltpu.VMEM((COLS * MESSAGE, LANES), F32),
            pltpu.VMEM((32, LANES), F32),
            pltpu.VMEM((256, LANES), F32),
        ],
        flops=10**7,
        moved=10**6,
    )(third, first, moved)

    def back_to_rows(array):
        return array.reshape(32, HIGHS, 2, LANES).transpose(0, 2, 1, 3).reshape(32, 2, RIGHT)

    return back_to_rows(new_factor), back_to_rows(new_velocity)


def solution(mesh):
    split = Mesh(mesh.devices.reshape(4, 2, 2, 4, 4), ("zh", "zl", "core", "y", "x"))
    every = ("zh", "zl", "core", "y", "x")
    return jax.shard_map(
        shards,
        mesh=split,
        in_specs=(P(COL, None, None), P(None, None, every), P(SET, None), P(SET, None)),
        out_specs=(P(None, None, every), P(None, None, every)),
        check_vma=False,
    )
```

time: 95.6 us -> 89 us (0.931); the launches traced: 95.4 us -> 87.5 us
  blocking collectives: 77.8 us -> 60.1 us
  starting transfers between devices: 0.09 us -> 8.05 us
  waiting for transfers between devices: 2.74 us -> 6.85 us
  Pallas kernels: 11.7 us -> 9.45 us
    all_to_all x3, blocking collectives: 77.8 us -> 60.1 us  [exchange(): return lax.all_to_all(array, axis, split_axis=0, concat_axis=0, tiled=True)]
    ppermute x1 -> x4, starting transfers between devices: 0.09 us -> 8.05 us  [the longest x1 5.39 us: shards(): lax.ppermute(keep_b[1] + got_b[1], ('zh', 'zl'), [(z, (z + (1 if z % 2 el...]
    ppermute x1 -> x4, waiting for transfers between devices: 2.74 us -> 6.85 us  [the longest x1 6.84 us: shards(): lax.ppermute(keep_b[1] + got_b[1], ('zh', 'zl'), [(z, (z + (1 if z % 2 el...]
    pallas_call x3 -> x5, Pallas kernels: 6.88 us -> 5.26 us  [the longest x1 1.92 us: shards(): call(back_first_kernel, 'back_first', (shape(2, 9, PEERS, LANES), shape(2...]
    unnamed x10 -> x8, local copies, waits for them, and re-layouts: 2.25 us -> 2.25 us
  transfers between devices with their start and end apart: 1 -> 4, of which waited for: 1 -> 1; matrix products, arithmetic and copies ran while one was open for 0% -> 0% of each run, Pallas kernels for 0% -> 2%
where the time goes in v2:
time: 89 us; the launch traced here: 87.5 us
  blocking collectives  60.1 us (68%)
  Pallas kernels  9.45 us (11%)
  starting transfers between devices  8.05 us (9%)
  waiting for transfers between devices  6.85 us (8%)
  local copies, waits for them, and re-layouts  2.25 us (3%)
    all_to_all x3, blocking collectives, exchange(): return lax.all_to_all(array, axis, split_axis=0, concat_axis=0, tiled=True)  60.1 us
    ppermute x1, waiting for transfers between devices, shards(): lax.ppermute(keep_b[1] + got_b[1], ('zh', 'zl'), [(z, (z + (1 if z % 2 el...  6.84 us
    ppermute x1, starting transfers between devices, shards(): lax.ppermute(keep_b[1] + got_b[1], ('zh', 'zl'), [(z, (z + (1 if z % 2 el...  5.39 us
    pallas_call x1, Pallas kernels, shards(): call(forward_kernel, 'forward', (shape(4, *matrix), shape(COLS, PCHUNK +...  4.2 us
    unnamed x8, local copies, waits for them, and re-layouts  2.25 us
    ppermute x1, starting transfers between devices, shards(): pair_a = lax.ppermute(keep_a[1] + got_a[1], 'zl', swap)  1.99 us
    pallas_call x1, Pallas kernels, shards(): call(back_first_kernel, 'back_first', (shape(2, 9, PEERS, LANES), shape(2...  1.92 us
  transfers between devices with their start and end apart: 4, of which 1 were waited for; matrix products, arithmetic and copies ran while one was open for 0% of the time, Pallas kernels for 2%

profile of v2, /device:TPU:8, one launch (start us, length us, event | category | flops | bytes accessed | tf_op | source)
XLA Modules:
  0.0 87.5 jit_solution(11156648063329260435)
XLA Ops:
  0.6 0.0 copy-start.1
  0.6 1.6 %copy-done.1 = f32[2,2,131072]{2,1,0:T(2,128)S(1)} copy-done((f32[2,2,131072]{2,1,0:T(2,128)S(1)}, f32[2,2,131072]{2,1,0:T(2,128)}, u32[]{:S(2)}) %copy-start.1) | copy-done | bytes 2097176
  2.2 0.7 copy-done.3
  2.9 4.2 %forward.1 = (f32[4,256,512]{2,1,0:T(8,128)S(1)}, f32[16,80,128]{2,1,0:T(8,128)S(1)}, s32[2,8,128]{2,1,0:T(8,128)S(1)}, f32[8,128]{1,0:T(8,128)S(1)}) custom-call(s32[1,17]{1,0:T(1,128)S(1)} %copy-done.3, f32[2,2048,128]{2,1,0:T(8,128)S(1)} %bitcast.38), custom_call_target="tpu_custom_call" | custom-call | flops 2000000000 | bytes 7000000 | tf_op jit(solution)/shard_map/forward/pallas_call | solution.py:351
  7.1 0.0 copy-start.2
  7.1 18.6 %all_to_all.15.got_ref.first_ref = f32[16,80,128]{2,1,0:T(8,128)S(1)} all-to-all(f32[16,80,128]{2,1,0:T(8,128)S(1)} %get-tuple-element.17), channel_id=1, replica_groups=mesh['zh'=4,'zl'=2,'core'=2,'y'=4,'x'=4] {'y','x'}, dimensions={0} | all-to-all | bytes 1310720 | tf_op jit(solution)/shard_map/all_to_all | solution.py:340
  25.7 0.8 summed.1
  26.5 14.2 %all_to_all.16 = f32[16,1,8320]{2,1,0:T(1,128)S(1)} all-to-all(f32[16,1,8320]{2,1,0:T(1,128)S(1)} %bitcast.35), channel_id=1, replica_groups=mesh['zh'=4,'zl'=2,'core'=2,'y'=4,'x'=4] {'y','x'}, dimensions={0} | all-to-all | bytes 1064960 | tf_op jit(solution)/shard_map/all_to_all | solution.py:340
  40.7 0.0 copy-done.2
  40.7 1.9 %back_first.1 = (f32[2,9,64,128]{3,2,1,0:T(8,128)S(1)}, f32[2,9,64,128]{3,2,1,0:T(8,128)S(1)}, f32[256,512]{1,0:T(8,128)S(1)}, bf16[256,256]{1,0:T(8,128)(2,1)S(...) custom-call(f32[1040,128]{1,0:T(8,128)S(1)} %bitcast.36, ...), custom_call_target="tpu_custom_call" | custom-call | flops 1000000000 | bytes 4000000 | tf_op jit(solution)/shard_map/back_first/pallas_call | solution.py:394
  42.6 0.1 collective-permute-start
  42.7 1.4 %back_second.1 = (f32[2,8,64,128]{3,2,1,0:T(8,128)S(1)}, f32[2,8,64,128]{3,2,1,0:T(8,128)S(1)}) custom-call(f32[256,512]{1,0:T(8,128)S(1)} %get-tuple-element.23.weight_ref, f32[4,256,512]{2,1,0:T(8,128)S(1)} %get-tuple-element.18.rotated_ref.refs_0_, bf16[256,256]{1,0:T(8,128)(2,1)S(1)} %get-tuple-element.24.refs_1_, ...), custom_call_target="tpu_custom_call" | custom-call | flops 1000000000 | bytes 4000000 | tf_op jit(solution)/shard_map/back_second/pallas_call | solution.py:413
  44.1 0.6 collective-permute-start.2
  44.7 0.0 collective-permute-done
  44.7 0.1 fusion
  44.8 2.0 %collective-permute-start.1 = (f32[9,64,128]{2,1,0:T(8,128)S(1)}, f32[9,64,128]{2,1,0:T(8,128)S(1)}, u32[]{:S(2)}, u32[]{:S(2)}) collective-permute-start(f32[9,64,128]{2,1,0:T(8,128)S(1)} %get-tuple-element.32), channel_id=1, source_target_pairs={{0,32},{32,0},{1,33},{33,1},{2,34},{34,2},{3,35},{35,3},{4,36},{36... | collective-permute-start | bytes 884744 | tf_op jit(solution)/shard_map/ppermute | solution.py:423
  46.8 0.0 collective-permute-done.2
  46.8 0.1 fusion.2
  46.9 5.4 %collective-permute-start.3 = (f32[8,64,128]{2,1,0:T(8,128)S(1)}, f32[8,64,128]{2,1,0:T(8,128)S(1)}, u32[]{:S(2)}, u32[]{:S(2)}) collective-permute-start(f32[8,64,128]{2,1,0:T(8,128)S(1)} %get-tuple-element.34), channel_id=1, source_target_pairs={{0,224},{32,64},{64,32},{96,128},{128,96},{160,192},{192,160},{224... | collective-permute-start | bytes 786440 | tf_op jit(solution)/shard_map/ppermute | solution.py:424
  52.2 6.8 %collective-permute-done.3.got_b = f32[8,64,128]{2,1,0:T(8,128)S(1)} collective-permute-done((f32[8,64,128]{2,1,0:T(8,128)S(1)}, f32[8,64,128]{2,1,0:T(8,128)S(1)}, u32[]{:S(2)}, u32[]{:S(2)}) %collective-permute-start.3) | collective-permute-done | bytes 262176 | tf_op jit(solution)/shard_map/ppermute | solution.py:424
  59.1 0.0 collective-permute-done.1.got_a
  59.1 0.1 merged.1
  59.2 27.3 %all_to_all.17 = f32[64,1,2176]{2,1,0:T(1,128)S(1)} all-to-all(f32[64,1,2176]{2,1,0:T(1,128)S(1)} %bitcast.33), channel_id=1, replica_groups=mesh['zh'=4,'zl'=2,'core'=2,'y'=4,'x'=4] {'zh','y','x'}, dimensions={0} | all-to-all | bytes 1114112 | tf_op jit(solution)/shard_map/all_to_all | solution.py:340
  86.5 1.1 %update.1 = (f32[256,128]{1,0:T(8,128)}, f32[256,128]{1,0:T(8,128)}) custom-call(f32[1088,128]{1,0:T(8,128)S(1)} %bitcast.34, f32[16,80,128]{2,1,0:T(8,128)S(1)} %all_to_all.15.got_ref.first_ref, f32[256,128]{1,0:T(8,128)S(1)} %bitcast.37), custom_call_target="tpu_custom_call" | custom-call | flops 10000000 | bytes 1000000 | tf_op jit(solution)/shard_map/update/pallas_call | solution.py:436
  (3 shorter events, 0.0 us)
Async XLA Ops:
  0.6 1.6 %copy-start.1 = (f32[2,2,131072]{2,1,0:T(2,128)S(1)}, f32[2,2,131072]{2,1,0:T(2,128)}, u32[]{:S(2)}) copy-start(f32[2,2,131072]{2,1,0:T(2,128)} %param.4) | copy-start | bytes 6291460
  2.2 0.7 copy-start.3
  7.1 33.6 %copy-start.2 = (s32[1,131072]{1,0:T(1,128)S(1)}, s32[1,131072]{1,0:T(1,128)}, u32[]{:S(2)}) copy-start(s32[1,131072]{1,0:T(1,128)} %param.7) | copy-start | bytes 1572868
  42.6 2.1 %collective-permute-start = (f32[2,9,64,128]{3,2,1,0:T(8,128)S(1)}, f32[2,9,64,128]{3,2,1,0:T(8,128)S(1)}, u32[]{:S(2)}, u32[]{:S(2)}) collective-permute-start(f32[2,9,64,128]{3,2,1,0:T(8,128)S(1)} %get-tuple-element.22), channel_id=1, source_target_pairs={{0,16},{16,0},{1,17},{17,1},{2,18},{18,2},{3,19},{19,3},{4,20},{20... | collective-permute-start | bytes 1769480 | tf_op jit(solution)/shard_map/ppermute | solution.py:412
  44.1 2.7 %collective-permute-start.2 = (f32[2,8,64,128]{3,2,1,0:T(8,128)S(1)}, f32[2,8,64,128]{3,2,1,0:T(8,128)S(1)}, u32[]{:S(2)}, u32[]{:S(2)}) collective-permute-start(f32[2,8,64,128]{3,2,1,0:T(8,128)S(1)} %get-tuple-element.29), channel_id=1, source_target_pairs={{0,16},{16,0},{1,17},{17,1},{2,18},{18,2},{3,19},{19,3},{4,20},{20... | collective-permute-start | bytes 1572872 | tf_op jit(solution)/shard_map/ppermute | solution.py:422
  44.8 14.3 %collective-permute-start.1 = (f32[9,64,128]{2,1,0:T(8,128)S(1)}, f32[9,64,128]{2,1,0:T(8,128)S(1)}, u32[]{:S(2)}, u32[]{:S(2)}) collective-permute-start(f32[9,64,128]{2,1,0:T(8,128)S(1)} %get-tuple-element.32), channel_id=1, source_target_pairs={{0,32},{32,0},{1,33},{33,1},{2,34},{34,2},{3,35},{35,3},{4,36},{36... | collective-permute-start | bytes 884744 | tf_op jit(solution)/shard_map/ppermute | solution.py:423
  46.8 39.7 %copy-start = (f32[32,2,512]{2,1,0:T(2,128)S(1)}, f32[32,2,512]{2,1,0:T(2,128)}, u32[]{:S(2)}) copy-start(f32[32,2,512]{2,1,0:T(2,128)} %param.5) | copy-start | bytes 393220
  46.9 12.2 %collective-permute-start.3 = (f32[8,64,128]{2,1,0:T(8,128)S(1)}, f32[8,64,128]{2,1,0:T(8,128)S(1)}, u32[]{:S(2)}, u32[]{:S(2)}) collective-permute-start(f32[8,64,128]{2,1,0:T(8,128)S(1)} %get-tuple-element.34), channel_id=1, source_target_pairs={{0,224},{32,64},{64,32},{96,128},{128,96},{160,192},{192,160},{224... | collective-permute-start | bytes 786440 | tf_op jit(solution)/shard_map/ppermute | solution.py:424

commit v3 on v2

--- a/solution.py
+++ b/solution.py
@@ -148,7 +148,7 @@
             prob[:, part] += second * second
         return carry
 
-    lax.fori_loop(0, 4, one, 0)
+    lax.fori_loop(0, 4, one, 0, unroll=2)
     for c in range(COLS):
         for high in range(HIGHS):
             send_ref[c, pl.ds(16 * high, 16), :] = (
@@ -202,27 +202,22 @@
         total = total + got_ref[c, pl.ds(0, PCHUNK), :]
     for c in range(COLS):
         rows[pl.ds(16 * c, 16), :] = got_ref[c, pl.ds(PCHUNK, 16), :]
-    parts = jnp.concatenate(parts_of(rows), axis=0)
-    gram = lax.dot_general(
-        parts, parts, (((1,), (1,)), ((), ())), precision=HIGH, preferred_element_type=F32
-    )
-    turn = quarter_turn()
-    turned = jnp.dot(turn, gram, precision=HIGH, preferred_element_type=F32)
-    turned = lax.dot_general(
-        turned, turn, (((1,), (1,)), ((), ())), precision=HIGH, preferred_element_type=F32
+    real, imag = parts_of(rows)
+    left_high, left_low = halves(jnp.concatenate([real, imag], axis=1))
+    both = jnp.concatenate(
+        [jnp.concatenate([real, imag], axis=1), jnp.concatenate([imag, -real], axis=1)], axis=0
+    )
+    both_high, both_low = halves(both)
+    gram = sum(
+        lax.dot_general(x, y, (((1,), (1,)), ((), ())), preferred_element_type=F32)
+        for x, y in ((left_high, both_low), (left_low, both_high), (left_high, both_high))
     )
     rows[pl.ds(0, 32), :] = jnp.zeros((32, LANES), F32)
-    rows[pl.ds(0, 32), pl.ds(0, 64)] = (gram + turned)[:32]
+    rows[pl.ds(0, 32), pl.ds(0, 64)] = gram
     pairs = rows[pl.ds(0, 16, stride=2), :] + pltpu.roll(rows[pl.ds(1, 16, stride=2), :], 64, 1)
     for c in range(COLS):
         send_ref[pl.ds(P1 * c, PCHUNK), :] = total
     send_ref[pl.ds(PCHUNK, 16, stride=P1), :] = pairs
-
-
-def quarter_turn():
-    i = lax.broadcasted_iota(jnp.int32, (64, 64), 0)
-    j = lax.broadcasted_iota(jnp.int32, (64, 64), 1)
-    return jnp.where(j == i + 32, -1.0, jnp.where(j == i - 32, 1.0, 0.0)).astype(F32)
 
 
 def unrotated(r, weight_ref, rotated_ref, ha_ref, hb_ref, cosine_ref, sine_ref, keep_ref, send_ref, wh, wl, th, tl):
@@ -372,7 +367,7 @@
         ],
         flops=2 * 10**9,
         moved=7 * 10**6,
-        vmem=int(40 * 2**20),
+        vmem=50 * 2**20,
     )(labels, own)
     first = exchange(sent, COL)
     sent = call(

time: 89 us -> 87.5 us (0.983)
  local copies, waits for them, and re-layouts: 2.25 us -> 0.66 us
    unnamed x8 -> x6, local copies, waits for them, and re-layouts: 2.25 us -> 0.66 us
where the time goes in v3:
time: 87.5 us; the launch traced here: 86 us
  blocking collectives  60 us (69%)
  Pallas kernels  9.51 us (11%)
  starting transfers between devices  8.09 us (9%)
  waiting for transfers between devices  6.85 us (8%)
    all_to_all x3, blocking collectives, exchange(): return lax.all_to_all(array, axis, split_axis=0, concat_axis=0, tiled=True)  60 us
    ppermute x1, waiting for transfers between devices, shards(): lax.ppermute(keep_b[1] + got_b[1], ('zh', 'zl'), [(z, (z + (1 if z % 2 el...  6.84 us
    ppermute x1, starting transfers between devices, shards(): lax.ppermute(keep_b[1] + got_b[1], ('zh', 'zl'), [(z, (z + (1 if z % 2 el...  5.42 us
    pallas_call x1, Pallas kernels, shards(): call(forward_kernel, 'forward', (shape(4, *matrix), shape(COLS, PCHUNK +...  4.71 us
    ppermute x1, starting transfers between devices, shards(): pair_a = lax.ppermute(keep_a[1] + got_a[1], 'zl', swap)  1.99 us
    pallas_call x1, Pallas kernels, shards(): call(back_first_kernel, 'back_first', (shape(2, 9, PEERS, LANES), shape(2...  1.92 us
  transfers between devices with their start and end apart: 4, of which 1 were waited for; matrix products, arithmetic and copies ran while one was open for 0% of the time, Pallas kernels for 2%

profile of v3, /device:TPU:8, one launch (start us, length us, event | category | flops | bytes accessed | tf_op | source)
XLA Modules:
  0.0 86.0 jit_solution(8298514475039720397)
XLA Ops:
  0.6 0.0 copy-start.2
  0.6 0.6 copy-done.2
  1.3 4.7 %forward.1 = (f32[4,256,512]{2,1,0:T(8,128)S(1)}, f32[16,80,128]{2,1,0:T(8,128)S(1)}, s32[2,8,128]{2,1,0:T(8,128)S(1)}, f32[8,128]{1,0:T(8,128)S(1)}) custom-call(s32[1,17]{1,0:T(1,128)S(1)} %copy-done.2, f32[2,2048,128]{2,1,0:T(8,128)} %bitcast.39), custom_call_target="tpu_custom_call" | custom-call | flops 2000000000 | bytes 7000000 | tf_op jit(solution)/shard_map/forward/pallas_call | solution.py:346
  6.0 0.0 copy-start.1
  6.0 18.6 %all_to_all.15.got_ref.first_ref = f32[16,80,128]{2,1,0:T(8,128)S(1)} all-to-all(f32[16,80,128]{2,1,0:T(8,128)S(1)} %get-tuple-element.17), channel_id=1, replica_groups=mesh['zh'=4,'zl'=2,'core'=2,'y'=4,'x'=4] {'y','x'}, dimensions={0} | all-to-all | bytes 1310720 | tf_op jit(solution)/shard_map/all_to_all | solution.py:335
  24.6 0.3 summed.1
  24.9 14.2 %all_to_all.16 = f32[16,1,8320]{2,1,0:T(1,128)S(1)} all-to-all(f32[16,1,8320]{2,1,0:T(1,128)S(1)} %bitcast.35), channel_id=1, replica_groups=mesh['zh'=4,'zl'=2,'core'=2,'y'=4,'x'=4] {'y','x'}, dimensions={0} | all-to-all | bytes 1064960 | tf_op jit(solution)/shard_map/all_to_all | solution.py:335
  39.1 0.0 copy-done.1
  39.1 1.9 %back_first.1 = (f32[2,9,64,128]{3,2,1,0:T(8,128)S(1)}, f32[2,9,64,128]{3,2,1,0:T(8,128)S(1)}, f32[256,512]{1,0:T(8,128)S(1)}, bf16[256,256]{1,0:T(8,128)(2,1)S(...) custom-call(f32[1040,128]{1,0:T(8,128)S(1)} %bitcast.36, ...), custom_call_target="tpu_custom_call" | custom-call | flops 1000000000 | bytes 4000000 | tf_op jit(solution)/shard_map/back_first/pallas_call | solution.py:389
  41.0 0.1 collective-permute-start
  41.1 1.4 %back_second.1 = (f32[2,8,64,128]{3,2,1,0:T(8,128)S(1)}, f32[2,8,64,128]{3,2,1,0:T(8,128)S(1)}) custom-call(f32[256,512]{1,0:T(8,128)S(1)} %get-tuple-element.23.weight_ref, f32[4,256,512]{2,1,0:T(8,128)S(1)} %get-tuple-element.18.rotated_ref.refs_0_, bf16[256,256]{1,0:T(8,128)(2,1)S(1)} %get-tuple-element.24.refs_1_, ...), custom_call_target="tpu_custom_call" | custom-call | flops 1000000000 | bytes 4000000 | tf_op jit(solution)/shard_map/back_second/pallas_call | solution.py:408
  42.6 0.6 collective-permute-start.2
  43.1 0.0 collective-permute-done
  43.1 0.1 fusion
  43.2 2.0 %collective-permute-start.1 = (f32[9,64,128]{2,1,0:T(8,128)S(1)}, f32[9,64,128]{2,1,0:T(8,128)S(1)}, u32[]{:S(2)}, u32[]{:S(2)}) collective-permute-start(f32[9,64,128]{2,1,0:T(8,128)S(1)} %get-tuple-element.32), channel_id=1, source_target_pairs={{0,32},{32,0},{1,33},{33,1},{2,34},{34,2},{3,35},{35,3},{4,36},{36... | collective-permute-start | bytes 884744 | tf_op jit(solution)/shard_map/ppermute | solution.py:418
  45.2 0.0 collective-permute-done.2
  45.2 0.1 fusion.2
  45.3 5.4 %collective-permute-start.3 = (f32[8,64,128]{2,1,0:T(8,128)S(1)}, f32[8,64,128]{2,1,0:T(8,128)S(1)}, u32[]{:S(2)}, u32[]{:S(2)}) collective-permute-start(f32[8,64,128]{2,1,0:T(8,128)S(1)} %get-tuple-element.34), channel_id=1, source_target_pairs={{0,224},{32,64},{64,32},{96,128},{128,96},{160,192},{192,160},{224... | collective-permute-start | bytes 786440 | tf_op jit(solution)/shard_map/ppermute | solution.py:419
  50.7 6.8 %collective-permute-done.3.got_b = f32[8,64,128]{2,1,0:T(8,128)S(1)} collective-permute-done((f32[8,64,128]{2,1,0:T(8,128)S(1)}, f32[8,64,128]{2,1,0:T(8,128)S(1)}, u32[]{:S(2)}, u32[]{:S(2)}) %collective-permute-start.3) | collective-permute-done | bytes 262176 | tf_op jit(solution)/shard_map/ppermute | solution.py:419
  57.6 0.0 collective-permute-done.1.got_a
  57.6 0.1 merged.1
  57.6 27.3 %all_to_all.17 = f32[64,1,2176]{2,1,0:T(1,128)S(1)} all-to-all(f32[64,1,2176]{2,1,0:T(1,128)S(1)} %bitcast.33), channel_id=1, replica_groups=mesh['zh'=4,'zl'=2,'core'=2,'y'=4,'x'=4] {'zh','y','x'}, dimensions={0} | all-to-all | bytes 1114112 | tf_op jit(solution)/shard_map/all_to_all | solution.py:335
  84.9 0.0 copy-done
  84.9 1.1 %update.1 = (f32[256,128]{1,0:T(8,128)}, f32[256,128]{1,0:T(8,128)}) custom-call(f32[1088,128]{1,0:T(8,128)S(1)} %bitcast.34, f32[16,80,128]{2,1,0:T(8,128)S(1)} %all_to_all.15.got_ref.first_ref, f32[256,128]{1,0:T(8,128)S(1)} %bitcast.37), custom_call_target="tpu_custom_call" | custom-call | flops 10000000 | bytes 1000000 | tf_op jit(solution)/shard_map/update/pallas_call | solution.py:431
  (1 shorter events, 0.0 us)
Async XLA Ops:
  0.6 0.7 copy-start.2
  6.0 33.1 %copy-start.1 = (s32[1,131072]{1,0:T(1,128)S(1)}, s32[1,131072]{1,0:T(1,128)}, u32[]{:S(2)}) copy-start(s32[1,131072]{1,0:T(1,128)} %param.7) | copy-start | bytes 1572868
  41.0 2.1 %collective-permute-start = (f32[2,9,64,128]{3,2,1,0:T(8,128)S(1)}, f32[2,9,64,128]{3,2,1,0:T(8,128)S(1)}, u32[]{:S(2)}, u32[]{:S(2)}) collective-permute-start(f32[2,9,64,128]{3,2,1,0:T(8,128)S(1)} %get-tuple-element.22), channel_id=1, source_target_pairs={{0,16},{16,0},{1,17},{17,1},{2,18},{18,2},{3,19},{19,3},{4,20},{20... | collective-permute-start | bytes 1769480 | tf_op jit(solution)/shard_map/ppermute | solution.py:407
  42.6 2.7 %collective-permute-start.2 = (f32[2,8,64,128]{3,2,1,0:T(8,128)S(1)}, f32[2,8,64,128]{3,2,1,0:T(8,128)S(1)}, u32[]{:S(2)}, u32[]{:S(2)}) collective-permute-start(f32[2,8,64,128]{3,2,1,0:T(8,128)S(1)} %get-tuple-element.29), channel_id=1, source_target_pairs={{0,16},{16,0},{1,17},{17,1},{2,18},{18,2},{3,19},{19,3},{4,20},{20... | collective-permute-start | bytes 1572872 | tf_op jit(solution)/shard_map/ppermute | solution.py:417
  43.2 14.3 %collective-permute-start.1 = (f32[9,64,128]{2,1,0:T(8,128)S(1)}, f32[9,64,128]{2,1,0:T(8,128)S(1)}, u32[]{:S(2)}, u32[]{:S(2)}) collective-permute-start(f32[9,64,128]{2,1,0:T(8,128)S(1)} %get-tuple-element.32), channel_id=1, source_target_pairs={{0,32},{32,0},{1,33},{33,1},{2,34},{34,2},{3,35},{35,3},{4,36},{36... | collective-permute-start | bytes 884744 | tf_op jit(solution)/shard_map/ppermute | solution.py:418
  45.2 39.7 %copy-start = (f32[32,2,512]{2,1,0:T(2,128)S(1)}, f32[32,2,512]{2,1,0:T(2,128)}, u32[]{:S(2)}) copy-start(f32[32,2,512]{2,1,0:T(2,128)} %param.5) | copy-start | bytes 393220
  45.3 12.3 %collective-permute-start.3 = (f32[8,64,128]{2,1,0:T(8,128)S(1)}, f32[8,64,128]{2,1,0:T(8,128)S(1)}, u32[]{:S(2)}, u32[]{:S(2)}) collective-permute-start(f32[8,64,128]{2,1,0:T(8,128)S(1)} %get-tuple-element.34), channel_id=1, source_target_pairs={{0,224},{32,64},{64,32},{96,128},{128,96},{160,192},{192,160},{224... | collective-permute-start | bytes 786440 | tf_op jit(solution)/shard_map/ppermute | solution.py:419

commit v4 on v3

--- a/solution.py
+++ b/solution.py
@@ -87,49 +87,60 @@
             ).astype(BF16)
 
 
+def crossed(left, right, bit):
+    return left + bit * right, bit * left + (1.0 - 2.0 * bit) * right
+
+
 STEP = 64
+HALF = RIGHT // 2
 
 
 def forward_kernel(labels_hbm, factor_hbm, rotated_ref, send_ref, masks_ref, scale_ref, labels_ref, factor_ref, xh, xl, th, tl, prob, ha, hb, sems):
-    copies = [
-        pltpu.make_async_copy(labels_hbm, labels_ref, sems.at[0]),
-        pltpu.make_async_copy(factor_hbm, factor_ref, sems.at[1]),
-    ]
-    for copy in copies:
-        copy.start()
+    def fetch(step):
+        rows = pl.ds(pl.multiple_of(step * (STEP * 8), STEP * 8), STEP * 8)
+        return pltpu.make_async_copy(factor_hbm.at[:, rows], factor_ref.at[:, rows], sems.at[step])
+
+    fetched = pltpu.make_async_copy(labels_hbm, labels_ref, sems.at[LEFT // STEP])
+    fetched.start()
+    for step in range(LEFT // STEP):
+        fetch(step).start()
     set_index = (lax.axis_index("zh") * 2 + lax.axis_index("zl")) * 2 + lax.axis_index("core")
-    copies[0].wait()
+    fetched.wait()
     bits, y_bits, scale = masks_of(labels_ref)
     masks_ref[0] = jnp.full((8, LANES), bits, jnp.int32)
     masks_ref[1] = jnp.full((8, LANES), y_bits, jnp.int32)
     scale_ref[...] = jnp.full((8, LANES), scale, F32)
-    store_hadamard(hb, RIGHT, masks_ref[0] & (RIGHT - 1))
+    store_hadamard(hb, HALF, masks_ref[0] & (HALF - 1))
     store_hadamard(ha, LEFT, masks_ref[0] >> QB)
+    top = ((bits >> (QB - 1)) & 1).astype(F32)
     prob[...] = jnp.zeros_like(prob)
-    copies[1].wait()
     lane = lax.broadcasted_iota(jnp.int32, (8, LANES), 1)
 
     def turned(step, carry):
+        fetch(step).wait()
         row = lax.broadcasted_iota(jnp.int32, (STEP, LANES), 0) + step * STEP
         left_turns = lax.population_count((row * RIGHT) & y_bits)
         to = pl.ds(pl.multiple_of(step * STEP, STEP), STEP)
-        for high in range(HIGHS):
+        values = {}
+        for high in (0, 2, 1, 3):
             right_turns = lax.population_count((lane + high * LANES) & y_bits)
-            turns = (left_turns + jnp.concatenate([right_turns] * (STEP // 8), axis=0)) & 3
+            turns = (left_turns + tall(right_turns, STEP)) & 3
             swap = (turns & 1) == 1
             sign_real = jnp.where(turns >= 2, -1.0, 1.0)
             sign_imag = jnp.where(((turns + 1) & 2) == 2, -1.0, 1.0)
-            block = pl.ds(high * LANES, LANES)
             for r in range(2):
                 real, imag = (
                     factor_ref[r, pl.ds(step * (STEP * 8) + 2 * high + c, STEP, stride=8), :]
                     for c in range(2)
                 )
-                for c, value in (
-                    (0, sign_real * jnp.where(swap, imag, real)),
-                    (1, sign_imag * jnp.where(swap, real, imag)),
-                ):
-                    xh[2 * r + c, to, block], xl[2 * r + c, to, block] = halves(value)
+                values[high, 2 * r] = sign_real * jnp.where(swap, imag, real)
+                values[high, 2 * r + 1] = sign_imag * jnp.where(swap, real, imag)
+            if high >= 2:
+                for i in range(4):
+                    pair = crossed(values[high - 2, i], values[high, i], top)
+                    for at, value in zip((high - 2, high), pair):
+                        block = pl.ds(at * LANES, LANES)
+                        xh[i, to, block], xl[i, to, block] = halves(value)
         return carry
 
     lax.fori_loop(0, LEFT // STEP, turned, 0)
@@ -143,12 +154,12 @@
             th[:, part], tl[:, part] = halves(first)
         for n in range(2):
             part = pl.ds(n * 256, 256)
-            second = two_pass(th[...], tl[...], hb[:, part])
+            second = two_pass(th[:, part], tl[:, part], hb[...])
             rotated_ref[i, :, part] = second
             prob[:, part] += second * second
         return carry
 
-    lax.fori_loop(0, 4, one, 0, unroll=2)
+    lax.fori_loop(0, 4, one, 0, unroll=4)
     for c in range(COLS):
         for high in range(HIGHS):
             send_ref[c, pl.ds(16 * high, 16), :] = (
@@ -162,7 +173,7 @@
 def prepare(masks_ref, scale_ref, ha_ref, hb_ref, cosine_ref, sine_ref, ha):
     core, parity = lax.axis_index("core"), lax.axis_index("zl")
     bits, y_bits = masks_ref[0], masks_ref[1]
-    store_hadamard(hb_ref, RIGHT, bits & (RIGHT - 1))
+    store_hadamard(hb_ref, HALF, bits & (HALF - 1))
     store_hadamard(ha, LEFT, bits >> QB)
     lane = lax.broadcasted_iota(jnp.int32, (8, LANES), 1)
     row = lax.broadcasted_iota(jnp.int32, (16, LANES), 0)
@@ -220,14 +231,19 @@
     send_ref[pl.ds(PCHUNK, 16, stride=P1), :] = pairs
 
 
-def unrotated(r, weight_ref, rotated_ref, ha_ref, hb_ref, cosine_ref, sine_ref, keep_ref, send_ref, wh, wl, th, tl):
+def unrotated(r, weight_ref, rotated_ref, masks_ref, ha_ref, hb_ref, cosine_ref, sine_ref, keep_ref, send_ref, wh, wl, th, tl):
+    top = ((masks_ref[0] >> (QB - 1)) & 1).astype(F32)[:1, :1]
     for c in range(2):
         for n in range(2):
-            part = pl.ds(n * 256, 256)
-            wh[:, part], wl[:, part] = halves(weight_ref[:, part] * rotated_ref[2 * r + c, :, part])
+            parts = [pl.ds(n * LANES, LANES), pl.ds(HALF + n * LANES, LANES)]
+            pair = crossed(
+                *(weight_ref[:, part] * rotated_ref[2 * r + c, :, part] for part in parts), top
+            )
+            for part, value in zip(parts, pair):
+                wh[:, part], wl[:, part] = halves(value)
         for n in range(2):
-            part = pl.ds(n * 256, 256)
-            th[c, :, part], tl[c, :, part] = halves(two_pass(wh[...], wl[...], hb_ref[:, part]))
+            part = pl.ds(n * HALF, HALF)
+            th[c, :, part], tl[c, :, part] = halves(two_pass(wh[:, part], wl[:, part], hb_ref[...]))
     for high in range(HIGHS):
         block = pl.ds(high * LANES, LANES)
         real, imag = (
@@ -261,7 +277,7 @@
             weight_ref[pl.ds(16 * c, 16), pl.ds(high * LANES, LANES)] = w
             ratio_sum = ratio_sum + w * p
     weight_ref[...] = weight_ref[...] - jnp.sum(ratio_sum) / trace
-    unrotated(0, weight_ref, rotated_ref, ha_ref, hb_ref, cosine_ref, sine_ref, keep_ref, send_ref, wh, wl, th, tl)
+    unrotated(0, weight_ref, rotated_ref, masks_ref, ha_ref, hb_ref, cosine_ref, sine_ref, keep_ref, send_ref, wh, wl, th, tl)
     for out in (keep_ref, send_ref):
         for kept in range(2):
             out[kept, 8] = jnp.broadcast_to(gram, (PEERS, LANES))
@@ -362,8 +378,8 @@
             pltpu.VMEM(matrix, BF16),
             pltpu.VMEM(matrix, F32),
             pltpu.VMEM((LEFT, LEFT), BF16),
-            pltpu.VMEM((RIGHT, RIGHT), BF16),
-            pltpu.SemaphoreType.DMA((2,)),
+            pltpu.VMEM((HALF, HALF), BF16),
+            pltpu.SemaphoreType.DMA((LEFT // STEP + 1,)),
         ],
         flops=2 * 10**9,
         moved=7 * 10**6,
@@ -394,7 +410,7 @@
             shape(2, 9, PEERS, LANES),
             shape(*matrix),
             shape(LEFT, LEFT, dtype=BF16),
-            shape(RIGHT, RIGHT, dtype=BF16),
+            shape(HALF, HALF, dtype=BF16),
             shape(*matrix),
             shape(*matrix),
         ),
@@ -409,11 +425,11 @@
         back_second_kernel,
         "back_second",
         (shape(2, 8, PEERS, LANES), shape(2, 8, PEERS, LANES)),
-        [VMEM] * 6,
+        [VMEM] * 7,
         back_scratch,
         flops=10**9,
         moved=4 * 10**6,
-    )(weight, rotated, *forms)
+    )(weight, rotated, masks, *forms)
     got_b = lax.ppermute(send_b, "core", swap)
     pair_a = lax.ppermute(keep_a[1] + got_a[1], "zl", swap)
     pair_b = lax.ppermute(

time: 87.5 us -> 86.5 us (0.989)
  Pallas kernels: 9.51 us -> 8.48 us
    pallas_call x1, Pallas kernels: 4.71 us -> 3.72 us  [shards(): call(forward_kernel, 'forward', (shape(4, *matrix), shape(COLS, PCHUNK +...]
where the time goes in v4:
time: 86.5 us; the launch traced here: 85 us
  blocking collectives  60.1 us (69%)
  Pallas kernels  8.48 us (10%)
  starting transfers between devices  8.04 us (9%)
  waiting for transfers between devices  6.85 us (8%)
    all_to_all x3, blocking collectives, exchange(): return lax.all_to_all(array, axis, split_axis=0, concat_axis=0, tiled=True)  60.1 us
    ppermute x1, waiting for transfers between devices, shards(): lax.ppermute(keep_b[1] + got_b[1], ('zh', 'zl'), [(z, (z + (1 if z % 2 el...  6.84 us
    ppermute x1, starting transfers between devices, shards(): lax.ppermute(keep_b[1] + got_b[1], ('zh', 'zl'), [(z, (z + (1 if z % 2 el...  5.38 us
    pallas_call x1, Pallas kernels, shards(): call(forward_kernel, 'forward', (shape(4, *matrix), shape(COLS, PCHUNK +...  3.72 us
    ppermute x1, starting transfers between devices, shards(): pair_a = lax.ppermute(keep_a[1] + got_a[1], 'zl', swap)  1.99 us
    pallas_call x1, Pallas kernels, shards(): call(back_first_kernel, 'back_first', (shape(2, 9, PEERS, LANES), shape(2...  1.9 us
  transfers between devices with their start and end apart: 4, of which 1 were waited for; matrix products, arithmetic and copies ran while one was open for 0% of the time, Pallas kernels for 2%

profile of v4, /device:TPU:8, one launch (start us, length us, event | category | flops | bytes accessed | tf_op | source)
XLA Modules:
  0.0 85.0 jit_solution(1621027945087801136)
XLA Ops:
  0.6 0.0 copy-start.2
  0.6 0.6 copy-done.2
  1.3 3.7 %forward.1 = (f32[4,256,512]{2,1,0:T(8,128)S(1)}, f32[16,80,128]{2,1,0:T(8,128)S(1)}, s32[2,8,128]{2,1,0:T(8,128)S(1)}, f32[8,128]{1,0:T(8,128)S(1)}) custom-call(s32[1,17]{1,0:T(1,128)S(1)} %copy-done.2, f32[2,2048,128]{2,1,0:T(8,128)} %bitcast.39), custom_call_target="tpu_custom_call" | custom-call | flops 2000000000 | bytes 7000000 | tf_op jit(solution)/shard_map/forward/pallas_call | solution.py:362
  5.0 0.0 copy-start.1
  5.0 18.6 %all_to_all.15.got_ref.first_ref = f32[16,80,128]{2,1,0:T(8,128)S(1)} all-to-all(f32[16,80,128]{2,1,0:T(8,128)S(1)} %get-tuple-element.17), channel_id=1, replica_groups=mesh['zh'=4,'zl'=2,'core'=2,'y'=4,'x'=4] {'y','x'}, dimensions={0} | all-to-all | bytes 1310720 | tf_op jit(solution)/shard_map/all_to_all | solution.py:351
  23.6 0.3 summed.1
  23.9 14.2 %all_to_all.16 = f32[16,1,8320]{2,1,0:T(1,128)S(1)} all-to-all(f32[16,1,8320]{2,1,0:T(1,128)S(1)} %bitcast.35), channel_id=1, replica_groups=mesh['zh'=4,'zl'=2,'core'=2,'y'=4,'x'=4] {'y','x'}, dimensions={0} | all-to-all | bytes 1064960 | tf_op jit(solution)/shard_map/all_to_all | solution.py:351
  38.1 0.0 copy-done.1
  38.1 1.9 %back_first.1 = (f32[2,9,64,128]{3,2,1,0:T(8,128)S(1)}, f32[2,9,64,128]{3,2,1,0:T(8,128)S(1)}, f32[256,512]{1,0:T(8,128)S(1)}, bf16[256,256]{1,0:T(8,128)(2,1)S(...) custom-call(f32[1040,128]{1,0:T(8,128)S(1)} %bitcast.36, ...), custom_call_target="tpu_custom_call" | custom-call | flops 1000000000 | bytes 4000000 | tf_op jit(solution)/shard_map/back_first/pallas_call | solution.py:405
  40.0 0.1 collective-permute-start
  40.1 1.4 %back_second.1 = (f32[2,8,64,128]{3,2,1,0:T(8,128)S(1)}, f32[2,8,64,128]{3,2,1,0:T(8,128)S(1)}) custom-call(f32[256,512]{1,0:T(8,128)S(1)} %get-tuple-element.23.weight_ref, f32[4,256,512]{2,1,0:T(8,128)S(1)} %get-tuple-element.18.rotated_ref.refs_0_, s32[2,8,128]{2,1,0:T(8,128)S(1)} %get-tuple-element.19.masks_ref.refs_1_, ...), custom_call_target="tpu_custom_call" | custom-call | flops 1000000000 | bytes 4000000 | tf_op jit(solution)/shard_map/back_second/pallas_call | solution.py:424
  41.5 0.6 collective-permute-start.2
  42.1 0.0 collective-permute-done
  42.1 0.1 fusion
  42.2 2.0 %collective-permute-start.1 = (f32[9,64,128]{2,1,0:T(8,128)S(1)}, f32[9,64,128]{2,1,0:T(8,128)S(1)}, u32[]{:S(2)}, u32[]{:S(2)}) collective-permute-start(f32[9,64,128]{2,1,0:T(8,128)S(1)} %get-tuple-element.32), channel_id=1, source_target_pairs={{0,32},{32,0},{1,33},{33,1},{2,34},{34,2},{3,35},{35,3},{4,36},{36... | collective-permute-start | bytes 884744 | tf_op jit(solution)/shard_map/ppermute | solution.py:434
  44.2 0.0 collective-permute-done.2
  44.2 0.1 fusion.2
  44.3 5.4 %collective-permute-start.3 = (f32[8,64,128]{2,1,0:T(8,128)S(1)}, f32[8,64,128]{2,1,0:T(8,128)S(1)}, u32[]{:S(2)}, u32[]{:S(2)}) collective-permute-start(f32[8,64,128]{2,1,0:T(8,128)S(1)} %get-tuple-element.34), channel_id=1, source_target_pairs={{0,224},{32,64},{64,32},{96,128},{128,96},{160,192},{192,160},{224... | collective-permute-start | bytes 786440 | tf_op jit(solution)/shard_map/ppermute | solution.py:435
  49.7 6.8 %collective-permute-done.3.got_b = f32[8,64,128]{2,1,0:T(8,128)S(1)} collective-permute-done((f32[8,64,128]{2,1,0:T(8,128)S(1)}, f32[8,64,128]{2,1,0:T(8,128)S(1)}, u32[]{:S(2)}, u32[]{:S(2)}) %collective-permute-start.3) | collective-permute-done | bytes 262176 | tf_op jit(solution)/shard_map/ppermute | solution.py:435
  56.5 0.0 collective-permute-done.1.got_a
  56.5 0.1 merged.1
  56.6 27.3 %all_to_all.17 = f32[64,1,2176]{2,1,0:T(1,128)S(1)} all-to-all(f32[64,1,2176]{2,1,0:T(1,128)S(1)} %bitcast.33), channel_id=1, replica_groups=mesh['zh'=4,'zl'=2,'core'=2,'y'=4,'x'=4] {'zh','y','x'}, dimensions={0} | all-to-all | bytes 1114112 | tf_op jit(solution)/shard_map/all_to_all | solution.py:351
  83.9 0.0 copy-done
  83.9 1.1 %update.1 = (f32[256,128]{1,0:T(8,128)}, f32[256,128]{1,0:T(8,128)}) custom-call(f32[1088,128]{1,0:T(8,128)S(1)} %bitcast.34, f32[16,80,128]{2,1,0:T(8,128)S(1)} %all_to_all.15.got_ref.first_ref, f32[256,128]{1,0:T(8,128)S(1)} %bitcast.37), custom_call_target="tpu_custom_call" | custom-call | flops 10000000 | bytes 1000000 | tf_op jit(solution)/shard_map/update/pallas_call | solution.py:447
  (1 shorter events, 0.0 us)
Async XLA Ops:
  0.6 0.7 copy-start.2
  5.0 33.1 %copy-start.1 = (s32[1,131072]{1,0:T(1,128)S(1)}, s32[1,131072]{1,0:T(1,128)}, u32[]{:S(2)}) copy-start(s32[1,131072]{1,0:T(1,128)} %param.7) | copy-start | bytes 1572868
  40.0 2.1 %collective-permute-start = (f32[2,9,64,128]{3,2,1,0:T(8,128)S(1)}, f32[2,9,64,128]{3,2,1,0:T(8,128)S(1)}, u32[]{:S(2)}, u32[]{:S(2)}) collective-permute-start(f32[2,9,64,128]{3,2,1,0:T(8,128)S(1)} %get-tuple-element.22), channel_id=1, source_target_pairs={{0,16},{16,0},{1,17},{17,1},{2,18},{18,2},{3,19},{19,3},{4,20},{20... | collective-permute-start | bytes 1769480 | tf_op jit(solution)/shard_map/ppermute | solution.py:423
  41.5 2.7 %collective-permute-start.2 = (f32[2,8,64,128]{3,2,1,0:T(8,128)S(1)}, f32[2,8,64,128]{3,2,1,0:T(8,128)S(1)}, u32[]{:S(2)}, u32[]{:S(2)}) collective-permute-start(f32[2,8,64,128]{3,2,1,0:T(8,128)S(1)} %get-tuple-element.29), channel_id=1, source_target_pairs={{0,16},{16,0},{1,17},{17,1},{2,18},{18,2},{3,19},{19,3},{4,20},{20... | collective-permute-start | bytes 1572872 | tf_op jit(solution)/shard_map/ppermute | solution.py:433
  42.2 14.3 %collective-permute-start.1 = (f32[9,64,128]{2,1,0:T(8,128)S(1)}, f32[9,64,128]{2,1,0:T(8,128)S(1)}, u32[]{:S(2)}, u32[]{:S(2)}) collective-permute-start(f32[9,64,128]{2,1,0:T(8,128)S(1)} %get-tuple-element.32), channel_id=1, source_target_pairs={{0,32},{32,0},{1,33},{33,1},{2,34},{34,2},{3,35},{35,3},{4,36},{36... | collective-permute-start | bytes 884744 | tf_op jit(solution)/shard_map/ppermute | solution.py:434
  44.2 39.7 %copy-start = (f32[32,2,512]{2,1,0:T(2,128)S(1)}, f32[32,2,512]{2,1,0:T(2,128)}, u32[]{:S(2)}) copy-start(f32[32,2,512]{2,1,0:T(2,128)} %param.5) | copy-start | bytes 393220
  44.3 12.2 %collective-permute-start.3 = (f32[8,64,128]{2,1,0:T(8,128)S(1)}, f32[8,64,128]{2,1,0:T(8,128)S(1)}, u32[]{:S(2)}, u32[]{:S(2)}) collective-permute-start(f32[8,64,128]{2,1,0:T(8,128)S(1)} %get-tuple-element.34), channel_id=1, source_target_pairs={{0,224},{32,64},{64,32},{96,128},{128,96},{160,192},{192,160},{224... | collective-permute-start | bytes 786440 | tf_op jit(solution)/shard_map/ppermute | solution.py:435

commit v5 on v4

--- a/solution.py
+++ b/solution.py
@@ -91,7 +91,7 @@
     return left + bit * right, bit * left + (1.0 - 2.0 * bit) * right
 
 
-STEP = 64
+STEP = 32
 HALF = RIGHT // 2
 
 
@@ -244,19 +244,22 @@
         for n in range(2):
             part = pl.ds(n * HALF, HALF)
             th[c, :, part], tl[c, :, part] = halves(two_pass(wh[:, part], wl[:, part], hb_ref[...]))
-    for high in range(HIGHS):
-        block = pl.ds(high * LANES, LANES)
+    for n in range(2):
+        part = pl.ds(n * HALF, HALF)
         real, imag = (
-            jnp.dot(ha_ref[...], th[c, :, block], preferred_element_type=F32)
-            + jnp.dot(ha_ref[...], tl[c, :, block], preferred_element_type=F32)
+            jnp.dot(ha_ref[...], th[c, :, part], preferred_element_type=F32)
+            + jnp.dot(ha_ref[...], tl[c, :, part], preferred_element_type=F32)
             for c in range(2)
         )
-        cosine, sine = cosine_ref[:, block], sine_ref[:, block]
+        cosine, sine = cosine_ref[:, part], sine_ref[:, part]
         for c, value in ((0, cosine * real - sine * imag), (1, cosine * imag + sine * real)):
             for half, out in ((0, keep_ref), (1, send_ref)):
                 for kept in range(2):
                     at = 128 * half + 64 * kept
-                    out[kept, 2 * high + c] = value[at : at + 64]
+                    for k in range(2):
+                        out[kept, 4 * n + 2 * k + c] = value[
+                            at : at + 64, k * LANES : (k + 1) * LANES
+                        ]
 
 
 def back_first_kernel(got_ref, counts_ref, rotated_ref, masks_ref, scale_ref, keep_ref, send_ref, weight_ref, ha_ref, hb_ref, cosine_ref, sine_ref, wh, wl, th, tl, ha):

time: 86.5 us -> 85.8 us (level)
  transfers between devices with their start and end apart: 4 -> 4, of which waited for: 1 -> 2; matrix products, arithmetic and copies ran while one was open for 0% -> 0% of each run, Pallas kernels for 2% -> 1%
where the time goes in v5:
time: 85.8 us; the launch traced here: 84.3 us
  blocking collectives  60.1 us (70%)
  Pallas kernels  7.8 us (9%)
  starting transfers between devices  7.8 us (9%)
  waiting for transfers between devices  7.12 us (8%)
    all_to_all x3, blocking collectives, exchange(): return lax.all_to_all(array, axis, split_axis=0, concat_axis=0, tiled=True)  60.1 us
    ppermute x1, waiting for transfers between devices, shards(): lax.ppermute(keep_b[1] + got_b[1], ('zh', 'zl'), [(z, (z + (1 if z % 2 el...  6.84 us
    ppermute x1, starting transfers between devices, shards(): lax.ppermute(keep_b[1] + got_b[1], ('zh', 'zl'), [(z, (z + (1 if z % 2 el...  5.15 us
    pallas_call x1, Pallas kernels, shards(): call(forward_kernel, 'forward', (shape(4, *matrix), shape(COLS, PCHUNK +...  3.58 us
    ppermute x1, starting transfers between devices, shards(): pair_a = lax.ppermute(keep_a[1] + got_a[1], 'zl', swap)  1.98 us
  transfers between devices with their start and end apart: 4, of which 2 were waited for; matrix products, arithmetic and copies ran while one was open for 0% of the time, Pallas kernels for 1%

profile of v5, /device:TPU:8, one launch (start us, length us, event | category | flops | bytes accessed | tf_op | source)
XLA Modules:
  0.0 84.3 jit_solution(14269425362223536318)
XLA Ops:
  0.6 0.0 copy-start.2
  0.6 0.6 copy-done.2
  1.3 3.6 %forward.1 = (f32[4,256,512]{2,1,0:T(8,128)S(1)}, f32[16,80,128]{2,1,0:T(8,128)S(1)}, s32[2,8,128]{2,1,0:T(8,128)S(1)}, f32[8,128]{1,0:T(8,128)S(1)}) custom-call(s32[1,17]{1,0:T(1,128)S(1)} %copy-done.2, f32[2,2048,128]{2,1,0:T(8,128)} %bitcast.39), custom_call_target="tpu_custom_call" | custom-call | flops 2000000000 | bytes 7000000 | tf_op jit(solution)/shard_map/forward/pallas_call | solution.py:365
  4.9 0.0 copy-start.1
  4.9 18.6 %all_to_all.15.got_ref.first_ref = f32[16,80,128]{2,1,0:T(8,128)S(1)} all-to-all(f32[16,80,128]{2,1,0:T(8,128)S(1)} %get-tuple-element.17), channel_id=1, replica_groups=mesh['zh'=4,'zl'=2,'core'=2,'y'=4,'x'=4] {'y','x'}, dimensions={0} | all-to-all | bytes 1310720 | tf_op jit(solution)/shard_map/all_to_all | solution.py:354
  23.5 0.3 summed.1
  23.8 14.2 %all_to_all.16 = f32[16,1,8320]{2,1,0:T(1,128)S(1)} all-to-all(f32[16,1,8320]{2,1,0:T(1,128)S(1)} %bitcast.35), channel_id=1, replica_groups=mesh['zh'=4,'zl'=2,'core'=2,'y'=4,'x'=4] {'y','x'}, dimensions={0} | all-to-all | bytes 1064960 | tf_op jit(solution)/shard_map/all_to_all | solution.py:354
  38.0 0.0 copy-done.1
  38.0 1.6 %back_first.1 = (f32[2,9,64,128]{3,2,1,0:T(8,128)S(1)}, f32[2,9,64,128]{3,2,1,0:T(8,128)S(1)}, f32[256,512]{1,0:T(8,128)S(1)}, bf16[256,256]{1,0:T(8,128)(2,1)S(...) custom-call(f32[1040,128]{1,0:T(8,128)S(1)} %bitcast.36, ...), custom_call_target="tpu_custom_call" | custom-call | flops 1000000000 | bytes 4000000 | tf_op jit(solution)/shard_map/back_first/pallas_call | solution.py:408
  39.6 0.1 collective-permute-start
  39.7 1.1 %back_second.1 = (f32[2,8,64,128]{3,2,1,0:T(8,128)S(1)}, f32[2,8,64,128]{3,2,1,0:T(8,128)S(1)}) custom-call(f32[256,512]{1,0:T(8,128)S(1)} %get-tuple-element.23.weight_ref, f32[4,256,512]{2,1,0:T(8,128)S(1)} %get-tuple-element.18.rotated_ref.refs_0_, s32[2,8,128]{2,1,0:T(8,128)S(1)} %get-tuple-element.19.masks_ref.refs_1_, ...), custom_call_target="tpu_custom_call" | custom-call | flops 1000000000 | bytes 4000000 | tf_op jit(solution)/shard_map/back_second/pallas_call | solution.py:427
  40.9 0.6 collective-permute-start.2
  41.4 0.3 collective-permute-done
  41.7 0.1 fusion
  41.8 2.0 %collective-permute-start.1 = (f32[9,64,128]{2,1,0:T(8,128)S(1)}, f32[9,64,128]{2,1,0:T(8,128)S(1)}, u32[]{:S(2)}, u32[]{:S(2)}) collective-permute-start(f32[9,64,128]{2,1,0:T(8,128)S(1)} %get-tuple-element.32), channel_id=1, source_target_pairs={{0,32},{32,0},{1,33},{33,1},{2,34},{34,2},{3,35},{35,3},{4,36},{36... | collective-permute-start | bytes 884744 | tf_op jit(solution)/shard_map/ppermute | solution.py:437
  43.8 0.0 collective-permute-done.2
  43.8 0.1 fusion.2
  43.8 5.1 %collective-permute-start.3 = (f32[8,64,128]{2,1,0:T(8,128)S(1)}, f32[8,64,128]{2,1,0:T(8,128)S(1)}, u32[]{:S(2)}, u32[]{:S(2)}) collective-permute-start(f32[8,64,128]{2,1,0:T(8,128)S(1)} %get-tuple-element.34), channel_id=1, source_target_pairs={{0,224},{32,64},{64,32},{96,128},{128,96},{160,192},{192,160},{224... | collective-permute-start | bytes 786440 | tf_op jit(solution)/shard_map/ppermute | solution.py:438
  49.0 6.8 %collective-permute-done.3.got_b = f32[8,64,128]{2,1,0:T(8,128)S(1)} collective-permute-done((f32[8,64,128]{2,1,0:T(8,128)S(1)}, f32[8,64,128]{2,1,0:T(8,128)S(1)}, u32[]{:S(2)}, u32[]{:S(2)}) %collective-permute-start.3) | collective-permute-done | bytes 262176 | tf_op jit(solution)/shard_map/ppermute | solution.py:438
  55.8 0.0 collective-permute-done.1.got_a
  55.8 0.1 merged.1
  55.9 27.3 %all_to_all.17 = f32[64,1,2176]{2,1,0:T(1,128)S(1)} all-to-all(f32[64,1,2176]{2,1,0:T(1,128)S(1)} %bitcast.33), channel_id=1, replica_groups=mesh['zh'=4,'zl'=2,'core'=2,'y'=4,'x'=4] {'zh','y','x'}, dimensions={0} | all-to-all | bytes 1114112 | tf_op jit(solution)/shard_map/all_to_all | solution.py:354
  83.2 0.0 copy-done
  83.2 1.1 %update.1 = (f32[256,128]{1,0:T(8,128)}, f32[256,128]{1,0:T(8,128)}) custom-call(f32[1088,128]{1,0:T(8,128)S(1)} %bitcast.34, f32[16,80,128]{2,1,0:T(8,128)S(1)} %all_to_all.15.got_ref.first_ref, f32[256,128]{1,0:T(8,128)S(1)} %bitcast.37), custom_call_target="tpu_custom_call" | custom-call | flops 10000000 | bytes 1000000 | tf_op jit(solution)/shard_map/update/pallas_call | solution.py:450
  (1 shorter events, 0.0 us)
Async XLA Ops:
  0.6 0.7 copy-start.2
  4.9 33.1 %copy-start.1 = (s32[1,131072]{1,0:T(1,128)S(1)}, s32[1,131072]{1,0:T(1,128)}, u32[]{:S(2)}) copy-start(s32[1,131072]{1,0:T(1,128)} %param.7) | copy-start | bytes 1572868
  39.6 2.1 %collective-permute-start = (f32[2,9,64,128]{3,2,1,0:T(8,128)S(1)}, f32[2,9,64,128]{3,2,1,0:T(8,128)S(1)}, u32[]{:S(2)}, u32[]{:S(2)}) collective-permute-start(f32[2,9,64,128]{3,2,1,0:T(8,128)S(1)} %get-tuple-element.22), channel_id=1, source_target_pairs={{0,16},{16,0},{1,17},{17,1},{2,18},{18,2},{3,19},{19,3},{4,20},{20... | collective-permute-start | bytes 1769480 | tf_op jit(solution)/shard_map/ppermute | solution.py:426
  40.9 2.9 %collective-permute-start.2 = (f32[2,8,64,128]{3,2,1,0:T(8,128)S(1)}, f32[2,8,64,128]{3,2,1,0:T(8,128)S(1)}, u32[]{:S(2)}, u32[]{:S(2)}) collective-permute-start(f32[2,8,64,128]{3,2,1,0:T(8,128)S(1)} %get-tuple-element.29), channel_id=1, source_target_pairs={{0,16},{16,0},{1,17},{17,1},{2,18},{18,2},{3,19},{19,3},{4,20},{20... | collective-permute-start | bytes 1572872 | tf_op jit(solution)/shard_map/ppermute | solution.py:436
  41.8 14.1 %collective-permute-start.1 = (f32[9,64,128]{2,1,0:T(8,128)S(1)}, f32[9,64,128]{2,1,0:T(8,128)S(1)}, u32[]{:S(2)}, u32[]{:S(2)}) collective-permute-start(f32[9,64,128]{2,1,0:T(8,128)S(1)} %get-tuple-element.32), channel_id=1, source_target_pairs={{0,32},{32,0},{1,33},{33,1},{2,34},{34,2},{3,35},{35,3},{4,36},{36... | collective-permute-start | bytes 884744 | tf_op jit(solution)/shard_map/ppermute | solution.py:437
  43.8 39.4 %copy-start = (f32[32,2,512]{2,1,0:T(2,128)S(1)}, f32[32,2,512]{2,1,0:T(2,128)}, u32[]{:S(2)}) copy-start(f32[32,2,512]{2,1,0:T(2,128)} %param.5) | copy-start | bytes 393220
  43.8 12.0 %collective-permute-start.3 = (f32[8,64,128]{2,1,0:T(8,128)S(1)}, f32[8,64,128]{2,1,0:T(8,128)S(1)}, u32[]{:S(2)}, u32[]{:S(2)}) collective-permute-start(f32[8,64,128]{2,1,0:T(8,128)S(1)} %get-tuple-element.34), channel_id=1, source_target_pairs={{0,224},{32,64},{64,32},{96,128},{128,96},{160,192},{192,160},{224... | collective-permute-start | bytes 786440 | tf_op jit(solution)/shard_map/ppermute | solution.py:438

commit v6 on v5

--- a/solution.py
+++ b/solution.py
@@ -91,11 +91,35 @@
     return left + bit * right, bit * left + (1.0 - 2.0 * bit) * right
 
 
+def store_tables(y_bits, scale, turned_ha_ref, cosine_ref, sine_ref, ha):
+    core, parity = lax.axis_index("core"), lax.axis_index("zl")
+    lane = lax.broadcasted_iota(jnp.int32, (8, LANES), 1)
+    row = lax.broadcasted_iota(jnp.int32, (16, LANES), 0)
+    right_turns = [
+        tall(lax.population_count((lane + high * LANES) & y_bits), 16) for high in range(HIGHS)
+    ]
+    for half in range(2):
+        for kept in range(2):
+            for pair in range(PAIRS):
+                z = 2 * pair + (parity ^ kept)
+                start = pl.multiple_of(z * 32 + (core ^ half) * 16, 16)
+                at = 128 * half + 64 * kept + 16 * pair
+                turned_ha_ref[pl.ds(at, 16), :] = ha[pl.ds(start, 16), :]
+                left_turns = lax.population_count(((row + start) * RIGHT) & y_bits)
+                for high in range(HIGHS):
+                    turns = (left_turns + right_turns[high]) & 3
+                    to = pl.ds(high * LANES, LANES)
+                    signed = jnp.where(turns >= 2, -scale, scale)
+                    odd = (turns & 1) == 1
+                    cosine_ref[pl.ds(at, 16), to] = jnp.where(odd, 0.0, signed)
+                    sine_ref[pl.ds(at, 16), to] = jnp.where(odd, signed, 0.0)
+
+
 STEP = 32
 HALF = RIGHT // 2
 
 
-def forward_kernel(labels_hbm, factor_hbm, rotated_ref, send_ref, masks_ref, scale_ref, labels_ref, factor_ref, xh, xl, th, tl, prob, ha, hb, sems):
+def forward_kernel(labels_hbm, factor_hbm, rotated_ref, send_ref, top_ref, turned_ha_ref, hb, cosine_ref, sine_ref, labels_ref, factor_ref, xh, xl, th, tl, prob, ha, sems):
     def fetch(step):
         rows = pl.ds(pl.multiple_of(step * (STEP * 8), STEP * 8), STEP * 8)
         return pltpu.make_async_copy(factor_hbm.at[:, rows], factor_ref.at[:, rows], sems.at[step])
@@ -107,12 +131,12 @@
     set_index = (lax.axis_index("zh") * 2 + lax.axis_index("zl")) * 2 + lax.axis_index("core")
     fetched.wait()
     bits, y_bits, scale = masks_of(labels_ref)
-    masks_ref[0] = jnp.full((8, LANES), bits, jnp.int32)
-    masks_ref[1] = jnp.full((8, LANES), y_bits, jnp.int32)
-    scale_ref[...] = jnp.full((8, LANES), scale, F32)
-    store_hadamard(hb, HALF, masks_ref[0] & (HALF - 1))
-    store_hadamard(ha, LEFT, masks_ref[0] >> QB)
+    tile = jnp.full((8, LANES), bits, jnp.int32)
+    store_hadamard(hb, HALF, tile & (HALF - 1))
+    store_hadamard(ha, LEFT, tile >> QB)
     top = ((bits >> (QB - 1)) & 1).astype(F32)
+    top_ref[...] = jnp.full((8, LANES), top, F32)
+    store_tables(y_bits, scale, turned_ha_ref, cosine_ref, sine_ref, ha)
     prob[...] = jnp.zeros_like(prob)
     lane = lax.broadcasted_iota(jnp.int32, (8, LANES), 1)
 
@@ -170,34 +194,6 @@
             send_ref[c, pl.ds(PCHUNK + 8 * r, 8), :] = factor_ref[r, pl.ds(start, 8), :]
 
 
-def prepare(masks_ref, scale_ref, ha_ref, hb_ref, cosine_ref, sine_ref, ha):
-    core, parity = lax.axis_index("core"), lax.axis_index("zl")
-    bits, y_bits = masks_ref[0], masks_ref[1]
-    store_hadamard(hb_ref, HALF, bits & (HALF - 1))
-    store_hadamard(ha, LEFT, bits >> QB)
-    lane = lax.broadcasted_iota(jnp.int32, (8, LANES), 1)
-    row = lax.broadcasted_iota(jnp.int32, (16, LANES), 0)
-    right_turns = [
-        tall(lax.population_count((lane + high * LANES) & y_bits), 16) for high in range(HIGHS)
-    ]
-    y_tall, scale = tall(y_bits, 16), tall(scale_ref[...], 16)
-    for half in range(2):
-        for kept in range(2):
-            for pair in range(PAIRS):
-                z = 2 * pair + (parity ^ kept)
-                start = pl.multiple_of(z * 32 + (core ^ half) * 16, 16)
-                at = 128 * half + 64 * kept + 16 * pair
-                ha_ref[pl.ds(at, 16), :] = ha[pl.ds(start, 16), :]
-                left_turns = lax.population_count(((row + start) * RIGHT) & y_tall)
-                for high in range(HIGHS):
-                    turns = (left_turns + right_turns[high]) & 3
-                    to = pl.ds(high * LANES, LANES)
-                    signed = jnp.where(turns >= 2, -scale, scale)
-                    odd = (turns & 1) == 1
-                    cosine_ref[pl.ds(at, 16), to] = jnp.where(odd, 0.0, signed)
-                    sine_ref[pl.ds(at, 16), to] = jnp.where(odd, signed, 0.0)
-
-
 def parts_of(rows):
     return tuple(
         jnp.concatenate(
@@ -231,8 +227,8 @@
     send_ref[pl.ds(PCHUNK, 16, stride=P1), :] = pairs
 
 
-def unrotated(r, weight_ref, rotated_ref, masks_ref, ha_ref, hb_ref, cosine_ref, sine_ref, keep_ref, send_ref, wh, wl, th, tl):
-    top = ((masks_ref[0] >> (QB - 1)) & 1).astype(F32)[:1, :1]
+def unrotated(r, weight_ref, rotated_ref, top_ref, ha_ref, hb_ref, cosine_ref, sine_ref, keep_ref, send_ref, wh, wl, th, tl):
+    top = top_ref[:1, :1]
     for c in range(2):
         for n in range(2):
             parts = [pl.ds(n * LANES, LANES), pl.ds(HALF + n * LANES, LANES)]
@@ -262,8 +258,7 @@
                         ]
 
 
-def back_first_kernel(got_ref, counts_ref, rotated_ref, masks_ref, scale_ref, keep_ref, send_ref, weight_ref, ha_ref, hb_ref, cosine_ref, sine_ref, wh, wl, th, tl, ha):
-    prepare(masks_ref, scale_ref, ha_ref, hb_ref, cosine_ref, sine_ref, ha)
+def back_first_kernel(got_ref, counts_ref, rotated_ref, top_ref, ha_ref, hb_ref, cosine_ref, sine_ref, keep_ref, send_ref, weight_ref, wh, wl, th, tl):
     total = jnp.zeros((PCHUNK, LANES), F32)
     gram = jnp.zeros((1, LANES), F32)
     for c in range(COLS):
@@ -280,7 +275,7 @@
             weight_ref[pl.ds(16 * c, 16), pl.ds(high * LANES, LANES)] = w
             ratio_sum = ratio_sum + w * p
     weight_ref[...] = weight_ref[...] - jnp.sum(ratio_sum) / trace
-    unrotated(0, weight_ref, rotated_ref, masks_ref, ha_ref, hb_ref, cosine_ref, sine_ref, keep_ref, send_ref, wh, wl, th, tl)
+    unrotated(0, weight_ref, rotated_ref, top_ref, ha_ref, hb_ref, cosine_ref, sine_ref, keep_ref, send_ref, wh, wl, th, tl)
     for out in (keep_ref, send_ref):
         for kept in range(2):
             out[kept, 8] = jnp.broadcast_to(gram, (PEERS, LANES))
@@ -362,14 +357,17 @@
     own = factor.reshape(2, 2, ROWS, LANES).transpose(0, 2, 1, 3).reshape(2, 2 * ROWS, LANES)
     moved = velocity.reshape(32, 2, HIGHS, LANES).transpose(0, 2, 1, 3).reshape(256, LANES)
     matrix = (LEFT, RIGHT)
-    rotated, sent, masks, scale = call(
+    rotated, sent, *forms = call(
         forward_kernel,
         "forward",
         (
             shape(4, *matrix),
             shape(COLS, PCHUNK + 16, LANES),
-            shape(2, 8, LANES, dtype=jnp.int32),
             shape(8, LANES),
+            shape(LEFT, LEFT, dtype=BF16),
+            shape(HALF, HALF, dtype=BF16),
+            shape(*matrix),
+            shape(*matrix),
         ),
         [HBM, HBM],
         [
@@ -381,13 +379,11 @@
             pltpu.VMEM(matrix, BF16),
             pltpu.VMEM(matrix, F32),
             pltpu.VMEM((LEFT, LEFT), BF16),
-            pltpu.VMEM((HALF, HALF), BF16),
             pltpu.SemaphoreType.DMA((LEFT // STEP + 1,)),
         ],
         flops=2 * 10**9,
         moved=7 * 10**6,
-        vmem=50 * 2**20,
-    )(labels, own)
+    )(*(pltpu.with_memory_space_constraint(x, pltpu.HBM) for x in (labels, own)))
     first = exchange(sent, COL)
     sent = call(
         summed_kernel,
@@ -405,23 +401,15 @@
         pltpu.VMEM((2, *matrix), BF16),
         pltpu.VMEM((2, *matrix), BF16),
     ]
-    keep_a, send_a, weight, *forms = call(
+    keep_a, send_a, weight = call(
         back_first_kernel,
         "back_first",
-        (
-            shape(2, 9, PEERS, LANES),
-            shape(2, 9, PEERS, LANES),
-            shape(*matrix),
-            shape(LEFT, LEFT, dtype=BF16),
-            shape(HALF, HALF, dtype=BF16),
-            shape(*matrix),
-            shape(*matrix),
-        ),
-        [VMEM] * 5,
-        [*back_scratch, pltpu.VMEM((LEFT, LEFT), BF16)],
+        (shape(2, 9, PEERS, LANES), shape(2, 9, PEERS, LANES), shape(*matrix)),
+        [VMEM] * 8,
+        back_scratch,
         flops=10**9,
         moved=4 * 10**6,
-    )(second, counts.reshape(ROWS, LANES), rotated, masks, scale)
+    )(second, counts.reshape(ROWS, LANES), rotated, *forms)
     swap = [(0, 1), (1, 0)]
     got_a = lax.ppermute(send_a, "core", swap)
     keep_b, send_b = call(
@@ -432,7 +420,7 @@
         back_scratch,
         flops=10**9,
         moved=4 * 10**6,
-    )(weight, rotated, masks, *forms)
+    )(weight, rotated, *forms)
     got_b = lax.ppermute(send_b, "core", swap)
     pair_a = lax.ppermute(keep_a[1] + got_a[1], "zl", swap)
     pair_b = lax.ppermute(

time: 85.8 us -> 85.1 us (level)
  no operation moved by 1% of the time
where the time goes in v6:
time: 85.1 us; the launch traced here: 83.6 us
  blocking collectives  60.1 us (71%)
  Pallas kernels  7.8 us (9%)
  starting transfers between devices  7.79 us (9%)
  waiting for transfers between devices  7.12 us (8%)
    all_to_all x3, blocking collectives, exchange(): return lax.all_to_all(array, axis, split_axis=0, concat_axis=0, tiled=True)  60.1 us
    ppermute x1, waiting for transfers between devices, shards(): lax.ppermute(keep_b[1] + got_b[1], ('zh', 'zl'), [(z, (z + (1 if z % 2 el...  6.84 us
    ppermute x1, starting transfers between devices, shards(): lax.ppermute(keep_b[1] + got_b[1], ('zh', 'zl'), [(z, (z + (1 if z % 2 el...  5.11 us
    pallas_call x1, Pallas kernels, shards(): call(forward_kernel, 'forward', (shape(4, *matrix), shape(COLS, PCHUNK +...  3.62 us
    ppermute x1, starting transfers between devices, shards(): pair_a = lax.ppermute(keep_a[1] + got_a[1], 'zl', swap)  2.01 us
  transfers between devices with their start and end apart: 4, of which 2 were waited for; matrix products, arithmetic and copies ran while one was open for 0% of the time, Pallas kernels for 1%

profile of v6, /device:TPU:8, one launch (start us, length us, event | category | flops | bytes accessed | tf_op | source)
XLA Modules:
  0.0 83.6 jit_solution(14435586199059776152)
XLA Ops:
  0.6 3.6 %forward.1 = (f32[4,256,512]{2,1,0:T(8,128)S(1)}, f32[16,80,128]{2,1,0:T(8,128)S(1)}, f32[8,128]{1,0:T(8,128)S(1)}, bf16[256,256]{1,0:T(8,128)(2,1)S(1)}, bf16[2...) custom-call(s32[1,17]{1,0:T(1,128)} %labels_hbm.1, f32[2,2048,128]{2,1,0:T(8,128)} %bitcast.39), custom_call_target="tpu_custom_call" | custom-call | flops 2000000000 | bytes 7000000 | tf_op jit(solution)/shard_map/forward/pallas_call | solution.py:360
  4.3 0.0 copy-start
  4.3 18.6 %all_to_all.15.got_ref.first_ref = f32[16,80,128]{2,1,0:T(8,128)S(1)} all-to-all(f32[16,80,128]{2,1,0:T(8,128)S(1)} %get-tuple-element.16), channel_id=1, replica_groups=mesh['zh'=4,'zl'=2,'core'=2,'y'=4,'x'=4] {'y','x'}, dimensions={0} | all-to-all | bytes 1310720 | tf_op jit(solution)/shard_map/all_to_all | solution.py:349
  22.8 0.3 summed.1
  23.2 14.2 %all_to_all.16 = f32[16,1,8320]{2,1,0:T(1,128)S(1)} all-to-all(f32[16,1,8320]{2,1,0:T(1,128)S(1)} %bitcast.36), channel_id=1, replica_groups=mesh['zh'=4,'zl'=2,'core'=2,'y'=4,'x'=4] {'y','x'}, dimensions={0} | all-to-all | bytes 1064960 | tf_op jit(solution)/shard_map/all_to_all | solution.py:349
  37.4 0.0 copy-done
  37.4 1.6 %back_first.1 = (f32[2,9,64,128]{3,2,1,0:T(8,128)S(1)}, f32[2,9,64,128]{3,2,1,0:T(8,128)S(1)}, f32[256,512]{1,0:T(8,128)S(1)}) custom-call(f32[1040,128]{1,0:T(8,128)S(1)} %bitcast.35, s32[1024,128]{1,0:T(8,128)S(1)} %bitcast.37, f32[4,256,512]{2,1,0:T(8,128)S(1)} %get-tuple-element.17.rotated_ref.refs_0_, f32[8,128]{1,0:T(8,128)S(1)} %get-tuple-element.18.top_ref.refs_1_, ...), custom_call_target="tpu_custom_call" | custom-call | flops 1000000000 | bytes 4000000 | tf_op jit(solution)/shard_map/back_first/pallas_call | solution.py:404
  39.0 0.1 collective-permute-start
  39.1 1.1 %back_second.1 = (f32[2,8,64,128]{3,2,1,0:T(8,128)S(1)}, f32[2,8,64,128]{3,2,1,0:T(8,128)S(1)}) custom-call(f32[256,512]{1,0:T(8,128)S(1)} %get-tuple-element.25.weight_ref, f32[4,256,512]{2,1,0:T(8,128)S(1)} %get-tuple-element.17.rotated_ref.refs_0_, f32[8,128]{1,0:T(8,128)S(1)} %get-tuple-element.18.top_ref.refs_1_, ...), custom_call_target="tpu_custom_call" | custom-call | flops 1000000000 | bytes 4000000 | tf_op jit(solution)/shard_map/back_second/pallas_call | solution.py:415
  40.2 0.6 collective-permute-start.2
  40.8 0.3 collective-permute-done
  41.1 0.1 fusion
  41.1 2.0 %collective-permute-start.1 = (f32[9,64,128]{2,1,0:T(8,128)S(1)}, f32[9,64,128]{2,1,0:T(8,128)S(1)}, u32[]{:S(2)}, u32[]{:S(2)}) collective-permute-start(f32[9,64,128]{2,1,0:T(8,128)S(1)} %get-tuple-element.30), channel_id=1, source_target_pairs={{0,32},{32,0},{1,33},{33,1},{2,34},{34,2},{3,35},{35,3},{4,36},{36... | collective-permute-start | bytes 884744 | tf_op jit(solution)/shard_map/ppermute | solution.py:425
  43.2 0.0 collective-permute-done.2
  43.2 0.0 copy-start.1
  43.2 0.1 fusion.2
  43.2 5.1 %collective-permute-start.3 = (f32[8,64,128]{2,1,0:T(8,128)S(1)}, f32[8,64,128]{2,1,0:T(8,128)S(1)}, u32[]{:S(2)}, u32[]{:S(2)}) collective-permute-start(f32[8,64,128]{2,1,0:T(8,128)S(1)} %get-tuple-element.32), channel_id=1, source_target_pairs={{0,224},{32,64},{64,32},{96,128},{128,96},{160,192},{192,160},{224... | collective-permute-start | bytes 786440 | tf_op jit(solution)/shard_map/ppermute | solution.py:426
  48.3 6.8 %collective-permute-done.3.got_b = f32[8,64,128]{2,1,0:T(8,128)S(1)} collective-permute-done((f32[8,64,128]{2,1,0:T(8,128)S(1)}, f32[8,64,128]{2,1,0:T(8,128)S(1)}, u32[]{:S(2)}, u32[]{:S(2)}) %collective-permute-start.3) | collective-permute-done | bytes 262176 | tf_op jit(solution)/shard_map/ppermute | solution.py:426
  55.2 0.0 collective-permute-done.1.got_a
  55.2 0.1 merged.1
  55.3 27.3 %all_to_all.17 = f32[64,1,2176]{2,1,0:T(1,128)S(1)} all-to-all(f32[64,1,2176]{2,1,0:T(1,128)S(1)} %bitcast.33), channel_id=1, replica_groups=mesh['zh'=4,'zl'=2,'core'=2,'y'=4,'x'=4] {'zh','y','x'}, dimensions={0} | all-to-all | bytes 1114112 | tf_op jit(solution)/shard_map/all_to_all | solution.py:349
  82.6 0.0 copy-done.1
  82.6 1.1 %update.1 = (f32[256,128]{1,0:T(8,128)}, f32[256,128]{1,0:T(8,128)}) custom-call(f32[1088,128]{1,0:T(8,128)S(1)} %bitcast.34, f32[16,80,128]{2,1,0:T(8,128)S(1)} %all_to_all.15.got_ref.first_ref, f32[256,128]{1,0:T(8,128)S(1)} %bitcast.38), custom_call_target="tpu_custom_call" | custom-call | flops 10000000 | bytes 1000000 | tf_op jit(solution)/shard_map/update/pallas_call | solution.py:438
Async XLA Ops:
  4.3 33.1 %copy-start = (s32[1,131072]{1,0:T(1,128)S(1)}, s32[1,131072]{1,0:T(1,128)}, u32[]{:S(2)}) copy-start(s32[1,131072]{1,0:T(1,128)} %param.7) | copy-start | bytes 1572868
  39.0 2.1 %collective-permute-start = (f32[2,9,64,128]{3,2,1,0:T(8,128)S(1)}, f32[2,9,64,128]{3,2,1,0:T(8,128)S(1)}, u32[]{:S(2)}, u32[]{:S(2)}) collective-permute-start(f32[2,9,64,128]{3,2,1,0:T(8,128)S(1)} %get-tuple-element.24), channel_id=1, source_target_pairs={{0,16},{16,0},{1,17},{17,1},{2,18},{18,2},{3,19},{19,3},{4,20},{20... | collective-permute-start | bytes 1769480 | tf_op jit(solution)/shard_map/ppermute | solution.py:414
  40.2 3.0 %collective-permute-start.2 = (f32[2,8,64,128]{3,2,1,0:T(8,128)S(1)}, f32[2,8,64,128]{3,2,1,0:T(8,128)S(1)}, u32[]{:S(2)}, u32[]{:S(2)}) collective-permute-start(f32[2,8,64,128]{3,2,1,0:T(8,128)S(1)} %get-tuple-element.27), channel_id=1, source_target_pairs={{0,16},{16,0},{1,17},{17,1},{2,18},{18,2},{3,19},{19,3},{4,20},{20... | collective-permute-start | bytes 1572872 | tf_op jit(solution)/shard_map/ppermute | solution.py:424
  41.1 14.0 %collective-permute-start.1 = (f32[9,64,128]{2,1,0:T(8,128)S(1)}, f32[9,64,128]{2,1,0:T(8,128)S(1)}, u32[]{:S(2)}, u32[]{:S(2)}) collective-permute-start(f32[9,64,128]{2,1,0:T(8,128)S(1)} %get-tuple-element.30), channel_id=1, source_target_pairs={{0,32},{32,0},{1,33},{33,1},{2,34},{34,2},{3,35},{35,3},{4,36},{36... | collective-permute-start | bytes 884744 | tf_op jit(solution)/shard_map/ppermute | solution.py:425
  43.2 39.4 %copy-start.1 = (f32[32,2,512]{2,1,0:T(2,128)S(1)}, f32[32,2,512]{2,1,0:T(2,128)}, u32[]{:S(2)}) copy-start(f32[32,2,512]{2,1,0:T(2,128)} %param.5) | copy-start | bytes 393220
  43.2 12.0 %collective-permute-start.3 = (f32[8,64,128]{2,1,0:T(8,128)S(1)}, f32[8,64,128]{2,1,0:T(8,128)S(1)}, u32[]{:S(2)}, u32[]{:S(2)}) collective-permute-start(f32[8,64,128]{2,1,0:T(8,128)S(1)} %get-tuple-element.32), channel_id=1, source_target_pairs={{0,224},{32,64},{64,32},{96,128},{128,96},{160,192},{192,160},{224... | collective-permute-start | bytes 786440 | tf_op jit(solution)/shard_map/ppermute | solution.py:426

commit v7 on v6

--- a/solution.py
+++ b/solution.py
@@ -16,10 +16,10 @@
 ROWS = ORDER // LANES
 COLS = 16
 SETS = 16
-PAIRS = 4
+TOPS = 2
 
 COL = ("y", "x")
-SET = ("zh", "zl", "core")
+SET = ("zt", "zm", "zl", "core")
 
 mixing = 0.1
 penalty = 8.0
@@ -33,7 +33,7 @@
 PCHUNK = ROWS // COLS
 P1 = PCHUNK + 1
 MESSAGE = 17
-PEERS = 64
+PEERS = 32
 VMEM = pl.BlockSpec(memory_space=pltpu.VMEM)
 SMEM = pl.BlockSpec(memory_space=pltpu.SMEM)
 HBM = pl.BlockSpec(memory_space=pltpu.HBM)
@@ -92,18 +92,18 @@
 
 
 def store_tables(y_bits, scale, turned_ha_ref, cosine_ref, sine_ref, ha):
-    core, parity = lax.axis_index("core"), lax.axis_index("zl")
+    core = lax.axis_index("core")
+    own = lax.axis_index("zm") * 2 + lax.axis_index("zl")
     lane = lax.broadcasted_iota(jnp.int32, (8, LANES), 1)
     row = lax.broadcasted_iota(jnp.int32, (16, LANES), 0)
     right_turns = [
         tall(lax.population_count((lane + high * LANES) & y_bits), 16) for high in range(HIGHS)
     ]
     for half in range(2):
-        for kept in range(2):
-            for pair in range(PAIRS):
-                z = 2 * pair + (parity ^ kept)
-                start = pl.multiple_of(z * 32 + (core ^ half) * 16, 16)
-                at = 128 * half + 64 * kept + 16 * pair
+        for q, place in enumerate((own, 3 - own, own ^ 1, (3 - own) ^ 1)):
+            for zt in range(TOPS):
+                start = pl.multiple_of((zt * 4 + place) * 32 + (core ^ half) * 16, 16)
+                at = 128 * half + 32 * q + 16 * zt
                 turned_ha_ref[pl.ds(at, 16), :] = ha[pl.ds(start, 16), :]
                 left_turns = lax.population_count(((row + start) * RIGHT) & y_bits)
                 for high in range(HIGHS):
@@ -128,7 +128,7 @@
     fetched.start()
     for step in range(LEFT // STEP):
         fetch(step).start()
-    set_index = (lax.axis_index("zh") * 2 + lax.axis_index("zl")) * 2 + lax.axis_index("core")
+    set_index = lax.axis_index(SET)
     fetched.wait()
     bits, y_bits, scale = masks_of(labels_ref)
     tile = jnp.full((8, LANES), bits, jnp.int32)
@@ -227,6 +227,9 @@
     send_ref[pl.ds(PCHUNK, 16, stride=P1), :] = pairs
 
 
+ORDERS = ((0, 1, 2, 3), (0, 2, 1, 3))
+
+
 def unrotated(r, weight_ref, rotated_ref, top_ref, ha_ref, hb_ref, cosine_ref, sine_ref, keep_ref, send_ref, wh, wl, th, tl):
     top = top_ref[:1, :1]
     for c in range(2):
@@ -250,12 +253,10 @@
         cosine, sine = cosine_ref[:, part], sine_ref[:, part]
         for c, value in ((0, cosine * real - sine * imag), (1, cosine * imag + sine * real)):
             for half, out in ((0, keep_ref), (1, send_ref)):
-                for kept in range(2):
-                    at = 128 * half + 64 * kept
+                for at, q in enumerate(ORDERS[r]):
+                    rows = slice(128 * half + PEERS * q, 128 * half + PEERS * (q + 1))
                     for k in range(2):
-                        out[kept, 4 * n + 2 * k + c] = value[
-                            at : at + 64, k * LANES : (k + 1) * LANES
-                        ]
+                        out[at, 4 * n + 2 * k + c] = value[rows, k * LANES : (k + 1) * LANES]
 
 
 def back_first_kernel(got_ref, counts_ref, rotated_ref, top_ref, ha_ref, hb_ref, cosine_ref, sine_ref, keep_ref, send_ref, weight_ref, wh, wl, th, tl):
@@ -277,8 +278,8 @@
     weight_ref[...] = weight_ref[...] - jnp.sum(ratio_sum) / trace
     unrotated(0, weight_ref, rotated_ref, top_ref, ha_ref, hb_ref, cosine_ref, sine_ref, keep_ref, send_ref, wh, wl, th, tl)
     for out in (keep_ref, send_ref):
-        for kept in range(2):
-            out[kept, 8] = jnp.broadcast_to(gram, (PEERS, LANES))
+        for at in range(4):
+            out[at, 8] = jnp.broadcast_to(gram, (PEERS, LANES))
 
 
 def back_second_kernel(weight_ref, *refs):
@@ -295,8 +296,8 @@
 def update_kernel(got_ref, first_ref, velocity_ref, new_factor_ref, new_velocity_ref, rows, sums, gram_ref, mixed_ref):
     block = COLS * MESSAGE
     total = got_ref[pl.ds(0, block), :]
-    for pair in range(1, PAIRS):
-        total = total + got_ref[pl.ds(block * pair, block), :]
+    for zt in range(1, TOPS):
+        total = total + got_ref[pl.ds(block * zt, block), :]
     sums[...] = total
     for c in range(COLS):
         rows[pl.ds(16 * c, 16), :] = first_ref[c, pl.ds(PCHUNK, 16), :]
@@ -404,7 +405,7 @@
     keep_a, send_a, weight = call(
         back_first_kernel,
         "back_first",
-        (shape(2, 9, PEERS, LANES), shape(2, 9, PEERS, LANES), shape(*matrix)),
+        (shape(4, 9, PEERS, LANES), shape(4, 9, PEERS, LANES), shape(*matrix)),
         [VMEM] * 8,
         back_scratch,
         flops=10**9,
@@ -415,17 +416,21 @@
     keep_b, send_b = call(
         back_second_kernel,
         "back_second",
-        (shape(2, 8, PEERS, LANES), shape(2, 8, PEERS, LANES)),
+        (shape(4, 8, PEERS, LANES), shape(4, 8, PEERS, LANES)),
         [VMEM] * 7,
         back_scratch,
         flops=10**9,
         moved=4 * 10**6,
     )(weight, rotated, *forms)
     got_b = lax.ppermute(send_b, "core", swap)
-    pair_a = lax.ppermute(keep_a[1] + got_a[1], "zl", swap)
-    pair_b = lax.ppermute(
-        keep_b[1] + got_b[1], ("zh", "zl"), [(z, (z + (1 if z % 2 else -1)) % 8) for z in range(8)]
-    )
+    sides = (
+        ("zl", swap),
+        (("zt", "zm", "zl"), [(z, (z + (1 if z % 2 else -1)) % 8) for z in range(8)]),
+    )
+    pair_a = lax.ppermute(keep_a[2:] + got_a[2:], *sides[0])
+    pair_b = lax.ppermute(keep_b[2:] + got_b[2:], *sides[1])
+    four_a = lax.ppermute(keep_a[1] + got_a[1] + pair_a[1], *sides[1])
+    four_b = lax.ppermute(keep_b[1] + got_b[1] + pair_b[1], *sides[0])
     sent = call(
         merged_kernel,
         "merged",
@@ -433,8 +438,10 @@
         [VMEM] * 4,
         flops=10**6,
         moved=2 * 10**6,
-    )(keep_a[0] + got_a[0], pair_a, keep_b[0] + got_b[0], pair_b)
-    third = exchange_flat(sent, ("zh", *COL), PEERS)
+    )(
+        keep_a[0] + got_a[0] + pair_a[0], four_a, keep_b[0] + got_b[0] + pair_b[0], four_b
+    )
+    third = exchange_flat(sent, ("zt", *COL), PEERS)
     new_factor, new_velocity = call(
         update_kernel,
         "update",
@@ -457,8 +464,8 @@
 
 
 def solution(mesh):
-    split = Mesh(mesh.devices.reshape(4, 2, 2, 4, 4), ("zh", "zl", "core", "y", "x"))
-    every = ("zh", "zl", "core", "y", "x")
+    split = Mesh(mesh.devices.reshape(2, 2, 2, 2, 4, 4), ("zt", "zm", "zl", "core", "y", "x"))
+    every = ("zt", "zm", "zl", "core", "y", "x")
     return jax.shard_map(
         shards,
         mesh=split,

time: 85.1 us -> 82.1 us (0.965); the launches traced: 83.6 us -> 81.9 us
  blocking collectives: 60.1 us -> 52.1 us
  starting transfers between devices: 7.79 us -> 13.7 us
    all_to_all x3, blocking collectives: 60.1 us -> 52.1 us  [exchange(): return lax.all_to_all(array, axis, split_axis=0, concat_axis=0, tiled=True)]
    ppermute x2 -> x4, starting transfers between devices: 7.12 us -> 13 us  [the longest x1 5.77 us: shards(): four_a = lax.ppermute(keep_a[1] + got_a[1] + pair_a[1], *sides[1])]
    ppermute x2 -> x4, waiting for transfers between devices: 6.85 us -> 7.05 us  [the longest x1 4.95 us: shards(): four_b = lax.ppermute(keep_b[1] + got_b[1] + pair_b[1], *sides[0])]
  transfers between devices with their start and end apart: 4 -> 6, of which waited for: 2 -> 3; matrix products, arithmetic and copies ran while one was open for 0% -> 0% of each run, Pallas kernels for 1% -> 1%
where the time goes in v7:
time: 82.1 us; the launch traced here: 81.9 us
  blocking collectives  52.1 us (63%)
  starting transfers between devices  13.7 us (17%)
  Pallas kernels  7.8 us (10%)
  waiting for transfers between devices  7.31 us (9%)
    all_to_all x3, blocking collectives, exchange(): return lax.all_to_all(array, axis, split_axis=0, concat_axis=0, tiled=True)  52.1 us
    ppermute x1, starting transfers between devices, shards(): four_a = lax.ppermute(keep_a[1] + got_a[1] + pair_a[1], *sides[1])  5.77 us
    ppermute x1, starting transfers between devices, shards(): pair_b = lax.ppermute(keep_b[2:] + got_b[2:], *sides[1])  5.16 us
    ppermute x1, waiting for transfers between devices, shards(): four_b = lax.ppermute(keep_b[1] + got_b[1] + pair_b[1], *sides[0])  4.95 us
    pallas_call x1, Pallas kernels, shards(): call(forward_kernel, 'forward', (shape(4, *matrix), shape(COLS, PCHUNK +...  3.62 us
    ppermute x1, waiting for transfers between devices, shards(): pair_a = lax.ppermute(keep_a[2:] + got_a[2:], *sides[0])  2.09 us
    ppermute x1, starting transfers between devices, shards(): pair_a = lax.ppermute(keep_a[2:] + got_a[2:], *sides[0])  1.98 us
  transfers between devices with their start and end apart: 6, of which 3 were waited for; matrix products, arithmetic and copies ran while one was open for 0% of the time, Pallas kernels for 1%

profile of v7, /device:TPU:8, one launch (start us, length us, event | category | flops | bytes accessed | tf_op | source)
XLA Modules:
  0.0 81.9 jit_solution(16957336432294133447)
XLA Ops:
  0.6 3.6 %forward.1 = (f32[4,256,512]{2,1,0:T(8,128)S(1)}, f32[16,80,128]{2,1,0:T(8,128)S(1)}, f32[8,128]{1,0:T(8,128)S(1)}, bf16[256,256]{1,0:T(8,128)(2,1)S(1)}, bf16[2...) custom-call(s32[1,17]{1,0:T(1,128)} %labels_hbm.1, f32[2,2048,128]{2,1,0:T(8,128)} %bitcast.39), custom_call_target="tpu_custom_call" | custom-call | flops 2000000000 | bytes 7000000 | tf_op jit(solution)/shard_map/forward/pallas_call | solution.py:361
  4.3 0.0 copy-start
  4.3 18.6 %all_to_all.15.got_ref.first_ref = f32[16,80,128]{2,1,0:T(8,128)S(1)} all-to-all(f32[16,80,128]{2,1,0:T(8,128)S(1)} %get-tuple-element.16), channel_id=1, replica_groups=mesh['zt'=2,'zm'=2,'zl'=2,'core'=2,'y'=4,'x'=4] {'y','x'}, dimensions={0} | all-to-all | bytes 1310720 | tf_op jit(solution)/shard_map/all_to_all | solution.py:350
  22.8 0.3 summed.1
  23.2 14.2 %all_to_all.16 = f32[16,1,8320]{2,1,0:T(1,128)S(1)} all-to-all(f32[16,1,8320]{2,1,0:T(1,128)S(1)} %bitcast.34), channel_id=1, replica_groups=mesh['zt'=2,'zm'=2,'zl'=2,'core'=2,'y'=4,'x'=4] {'y','x'}, dimensions={0} | all-to-all | bytes 1064960 | tf_op jit(solution)/shard_map/all_to_all | solution.py:350
  37.4 1.6 %back_first.1 = (f32[4,9,32,128]{3,2,1,0:T(8,128)S(1)}, f32[4,9,32,128]{3,2,1,0:T(8,128)S(1)}, f32[256,512]{1,0:T(8,128)S(1)}) custom-call(f32[1040,128]{1,0:T(8,128)S(1)} %bitcast.33, s32[1024,128]{1,0:T(8,128)S(1)} %bitcast.37, f32[4,256,512]{2,1,0:T(8,128)S(1)} %get-tuple-element.17.rotated_ref.refs_0_, f32[8,128]{1,0:T(8,128)S(1)} %get-tuple-element.18.top_ref.refs_1_, ...), custom_call_target="tpu_custom_call" | custom-call | flops 1000000000 | bytes 4000000 | tf_op jit(solution)/shard_map/back_first/pallas_call | solution.py:405
  39.0 0.1 collective-permute-start
  39.1 1.1 %back_second.1 = (f32[4,8,32,128]{3,2,1,0:T(8,128)S(1)}, f32[4,8,32,128]{3,2,1,0:T(8,128)S(1)}) custom-call(f32[256,512]{1,0:T(8,128)S(1)} %get-tuple-element.25.weight_ref, f32[4,256,512]{2,1,0:T(8,128)S(1)} %get-tuple-element.17.rotated_ref.refs_0_, f32[8,128]{1,0:T(8,128)S(1)} %get-tuple-element.18.top_ref.refs_1_, ...), custom_call_target="tpu_custom_call" | custom-call | flops 1000000000 | bytes 4000000 | tf_op jit(solution)/shard_map/back_second/pallas_call | solution.py:416
  40.2 0.6 collective-permute-start.3
  40.8 0.3 collective-permute-done
  41.1 0.1 slice_add_fusion
  41.1 2.0 %collective-permute-start.1 = (f32[2,9,32,128]{3,2,1,0:T(8,128)S(1)}, f32[2,9,32,128]{3,2,1,0:T(8,128)S(1)}, u32[]{:S(2)}, u32[]{:S(2)}) collective-permute-start(f32[2,9,32,128]{3,2,1,0:T(8,128)S(1)} %slice_add_fusion), channel_id=1, source_target_pairs={{0,32},{32,0},{1,33},{33,1},{2,34},{34,2},{3,35},{35,3},{4,36},{36... | collective-permute-start | bytes 884744 | tf_op jit(solution)/shard_map/ppermute | solution.py:430
  43.1 0.0 collective-permute-done.3
  43.2 5.2 %collective-permute-start.4 = (f32[2,8,32,128]{3,2,1,0:T(8,128)S(1)}, f32[2,8,32,128]{3,2,1,0:T(8,128)S(1)}, u32[]{:S(2)}, u32[]{:S(2)}) collective-permute-start(f32[2,8,32,128]{3,2,1,0:T(8,128)S(1)} %slice_add_fusion.1), channel_id=1, source_target_pairs={{0,224},{32,64},{64,32},{96,128},{128,96},{160,192},{192,160},{224... | collective-permute-start | bytes 786440 | tf_op jit(solution)/shard_map/ppermute | solution.py:431
  48.3 2.1 %collective-permute-done.1 = f32[2,9,32,128]{3,2,1,0:T(8,128)S(1)} collective-permute-done((f32[2,9,32,128]{3,2,1,0:T(8,128)S(1)}, f32[2,9,32,128]{3,2,1,0:T(8,128)S(1)}, u32[]{:S(2)}, u32[]{:S(2)}) %collective-permute-start.1) | collective-permute-done | bytes 294944 | tf_op jit(solution)/shard_map/ppermute | solution.py:430
  50.4 0.1 fusion
  50.5 5.8 %collective-permute-start.2 = (f32[9,32,128]{2,1,0:T(8,128)S(1)}, f32[9,32,128]{2,1,0:T(8,128)S(1)}, u32[]{:S(2)}, u32[]{:S(2)}) collective-permute-start(f32[9,32,128]{2,1,0:T(8,128)S(1)} %get-tuple-element.30), channel_id=1, source_target_pairs={{0,224},{32,64},{64,32},{96,128},{128,96},{160,192},{192,160},{224... | collective-permute-start | bytes 442376 | tf_op jit(solution)/shard_map/ppermute | solution.py:432
  56.3 0.0 collective-permute-done.4
  56.3 0.1 fusion.2
  56.3 0.1 collective-permute-start.5
  56.4 5.0 %collective-permute-done.5.got_b = f32[8,32,128]{2,1,0:T(8,128)S(1)} collective-permute-done((f32[8,32,128]{2,1,0:T(8,128)S(1)}, f32[8,32,128]{2,1,0:T(8,128)S(1)}, u32[]{:S(2)}, u32[]{:S(2)}) %collective-permute-start.5) | collective-permute-done | bytes 131104 | tf_op jit(solution)/shard_map/ppermute | solution.py:433
  61.4 0.0 collective-permute-done.2.got_a
  61.4 19.3 %all_to_all.17 = f32[32,1,2176]{2,1,0:T(1,128)S(1)} all-to-all(f32[32,1,2176]{2,1,0:T(1,128)S(1)} %bitcast.35), channel_id=1, replica_groups=mesh['zt'=2,'zm'=2,'zl'=2,'core'=2,'y'=4,'x'=4] {'zt','y','x'}, dimensions={0} | all-to-all | bytes 557056 | tf_op jit(solution)/shard_map/all_to_all | solution.py:350
  80.8 1.1 %update.1 = (f32[256,128]{1,0:T(8,128)}, f32[256,128]{1,0:T(8,128)}) custom-call(f32[544,128]{1,0:T(8,128)S(1)} %bitcast.36, f32[16,80,128]{2,1,0:T(8,128)S(1)} %all_to_all.15.got_ref.first_ref, f32[256,128]{1,0:T(8,128)S(1)} %bitcast.38), custom_call_target="tpu_custom_call" | custom-call | flops 10000000 | bytes 1000000 | tf_op jit(solution)/shard_map/update/pallas_call | solution.py:445
  (5 shorter events, 0.1 us)
Async XLA Ops:
  4.3 33.1 %copy-start = (s32[1,131072]{1,0:T(1,128)S(1)}, s32[1,131072]{1,0:T(1,128)}, u32[]{:S(2)}) copy-start(s32[1,131072]{1,0:T(1,128)} %param.7) | copy-start | bytes 1572868
  39.0 2.1 %collective-permute-start = (f32[4,9,32,128]{3,2,1,0:T(8,128)S(1)}, f32[4,9,32,128]{3,2,1,0:T(8,128)S(1)}, u32[]{:S(2)}, u32[]{:S(2)}) collective-permute-start(f32[4,9,32,128]{3,2,1,0:T(8,128)S(1)} %get-tuple-element.24), channel_id=1, source_target_pairs={{0,16},{16,0},{1,17},{17,1},{2,18},{18,2},{3,19},{19,3},{4,20},{20... | collective-permute-start | bytes 1769480 | tf_op jit(solution)/shard_map/ppermute | solution.py:415
  40.2 2.9 %collective-permute-start.3 = (f32[4,8,32,128]{3,2,1,0:T(8,128)S(1)}, f32[4,8,32,128]{3,2,1,0:T(8,128)S(1)}, u32[]{:S(2)}, u32[]{:S(2)}) collective-permute-start(f32[4,8,32,128]{3,2,1,0:T(8,128)S(1)} %get-tuple-element.27), channel_id=1, source_target_pairs={{0,16},{16,0},{1,17},{17,1},{2,18},{18,2},{3,19},{19,3},{4,20},{20... | collective-permute-start | bytes 1572872 | tf_op jit(solution)/shard_map/ppermute | solution.py:425
  41.1 9.3 %collective-permute-start.1 = (f32[2,9,32,128]{3,2,1,0:T(8,128)S(1)}, f32[2,9,32,128]{3,2,1,0:T(8,128)S(1)}, u32[]{:S(2)}, u32[]{:S(2)}) collective-permute-start(f32[2,9,32,128]{3,2,1,0:T(8,128)S(1)} %slice_add_fusion), channel_id=1, source_target_pairs={{0,32},{32,0},{1,33},{33,1},{2,34},{34,2},{3,35},{35,3},{4,36},{36... | collective-permute-start | bytes 884744 | tf_op jit(solution)/shard_map/ppermute | solution.py:430
  43.1 37.7 %copy-start.1 = (f32[32,2,512]{2,1,0:T(2,128)S(1)}, f32[32,2,512]{2,1,0:T(2,128)}, u32[]{:S(2)}) copy-start(f32[32,2,512]{2,1,0:T(2,128)} %param.5) | copy-start | bytes 393220
  43.2 13.1 %collective-permute-start.4 = (f32[2,8,32,128]{3,2,1,0:T(8,128)S(1)}, f32[2,8,32,128]{3,2,1,0:T(8,128)S(1)}, u32[]{:S(2)}, u32[]{:S(2)}) collective-permute-start(f32[2,8,32,128]{3,2,1,0:T(8,128)S(1)} %slice_add_fusion.1), channel_id=1, source_target_pairs={{0,224},{32,64},{64,32},{96,128},{128,96},{160,192},{192,160},{224... | collective-permute-start | bytes 786440 | tf_op jit(solution)/shard_map/ppermute | solution.py:431
  50.5 10.9 %collective-permute-start.2 = (f32[9,32,128]{2,1,0:T(8,128)S(1)}, f32[9,32,128]{2,1,0:T(8,128)S(1)}, u32[]{:S(2)}, u32[]{:S(2)}) collective-permute-start(f32[9,32,128]{2,1,0:T(8,128)S(1)} %get-tuple-element.30), channel_id=1, source_target_pairs={{0,224},{32,64},{64,32},{96,128},{128,96},{160,192},{192,160},{224... | collective-permute-start | bytes 442376 | tf_op jit(solution)/shard_map/ppermute | solution.py:432
  56.3 5.1 %collective-permute-start.5 = (f32[8,32,128]{2,1,0:T(8,128)S(1)}, f32[8,32,128]{2,1,0:T(8,128)S(1)}, u32[]{:S(2)}, u32[]{:S(2)}) collective-permute-start(f32[8,32,128]{2,1,0:T(8,128)S(1)} %get-tuple-element.32), channel_id=1, source_target_pairs={{0,32},{32,0},{1,33},{33,1},{2,34},{34,2},{3,35},{35,3},{4,36},{36... | collective-permute-start | bytes 393224 | tf_op jit(solution)/shard_map/ppermute | solution.py:433

commit v8 on v7

--- a/solution.py
+++ b/solution.py
@@ -286,22 +286,25 @@
     unrotated(1, weight_ref, *refs)
 
 
+def split_kernel(mine, got, keep_ref, send_ref):
+    own = lax.axis_index("zt")
+    here, there = (pl.ds(pl.multiple_of(16 * half, 16), 16) for half in (own, 1 - own))
+    for j in range(mine.shape[0]):
+        keep_ref[j] = mine[j, here, :] + got[j, here, :]
+        send_ref[j] = mine[j, there, :] + got[j, there, :]
+
+
 def merged_kernel(mine_a, got_a, mine_b, got_b, send_ref):
     for j in range(8):
-        send_ref[pl.ds(j, PEERS, stride=MESSAGE), :] = mine_a[j] + got_a[j]
-        send_ref[pl.ds(8 + j, PEERS, stride=MESSAGE), :] = mine_b[j] + got_b[j]
-    send_ref[pl.ds(16, PEERS, stride=MESSAGE), :] = mine_a[8] + got_a[8]
-
-
-def update_kernel(got_ref, first_ref, velocity_ref, new_factor_ref, new_velocity_ref, rows, sums, gram_ref, mixed_ref):
-    block = COLS * MESSAGE
-    total = got_ref[pl.ds(0, block), :]
-    for zt in range(1, TOPS):
-        total = total + got_ref[pl.ds(block * zt, block), :]
-    sums[...] = total
+        send_ref[pl.ds(j, COLS, stride=MESSAGE), :] = mine_a[j] + got_a[j]
+        send_ref[pl.ds(8 + j, COLS, stride=MESSAGE), :] = mine_b[j] + got_b[j]
+    send_ref[pl.ds(16, COLS, stride=MESSAGE), :] = mine_a[8] + got_a[8]
+
+
+def update_kernel(got_ref, first_ref, velocity_ref, new_factor_ref, new_velocity_ref, rows, gram_ref, mixed_ref):
     for c in range(COLS):
         rows[pl.ds(16 * c, 16), :] = first_ref[c, pl.ds(PCHUNK, 16), :]
-    pairs = sums[pl.ds(16, 16, stride=MESSAGE), :]
+    pairs = got_ref[pl.ds(16, 16, stride=MESSAGE), :]
     gram_ref[pl.ds(0, 16, stride=2), :] = pairs
     gram_ref[pl.ds(1, 16, stride=2), :] = pltpu.roll(pairs, 64, 1)
     gram = gram_ref[:, pl.ds(0, 64)]
@@ -321,7 +324,7 @@
     for c in range(COLS):
         at = pl.ds(16 * c, 16)
         own = rows[at, :]
-        gradient = -((1.0 - mixing) / SETS) * sums[pl.ds(MESSAGE * c, 16), :] + penalty * (
+        gradient = -((1.0 - mixing) / SETS) * got_ref[pl.ds(MESSAGE * c, 16), :] + penalty * (
             2.0 * mixed_ref[at, :] / trace - 2.0 * purity * own
         )
         velocity = momentum * velocity_ref[at, :] + gradient
@@ -431,17 +434,25 @@
     pair_b = lax.ppermute(keep_b[2:] + got_b[2:], *sides[1])
     four_a = lax.ppermute(keep_a[1] + got_a[1] + pair_a[1], *sides[1])
     four_b = lax.ppermute(keep_b[1] + got_b[1] + pair_b[1], *sides[0])
+    merged = []
+    for mine, got in (
+        (keep_a[0] + got_a[0] + pair_a[0], four_a),
+        (keep_b[0] + got_b[0] + pair_b[0], four_b),
+    ):
+        half = shape(mine.shape[0], COLS, LANES)
+        kept, sent = call(
+            split_kernel, "split", (half, half), [VMEM] * 2, flops=10**5, moved=10**6
+        )(mine, got)
+        merged += [kept, lax.ppermute(sent, "zt", swap)]
     sent = call(
         merged_kernel,
         "merged",
-        shape(PEERS * MESSAGE, LANES),
+        shape(COLS * MESSAGE, LANES),
         [VMEM] * 4,
-        flops=10**6,
-        moved=2 * 10**6,
-    )(
-        keep_a[0] + got_a[0] + pair_a[0], four_a, keep_b[0] + got_b[0] + pair_b[0], four_b
-    )
-    third = exchange_flat(sent, ("zt", *COL), PEERS)
+        flops=10**5,
+        moved=10**6,
+    )(*merged)
+    third = exchange_flat(sent, COL, COLS)
     new_factor, new_velocity = call(
         update_kernel,
         "update",
@@ -449,7 +460,6 @@
         [VMEM] * 3,
         [
             pltpu.VMEM((256, LANES), F32),
-            pltpu.VMEM((COLS * MESSAGE, LANES), F32),
             pltpu.VMEM((32, LANES), F32),
             pltpu.VMEM((256, LANES), F32),
         ],

time: 82.1 us -> 84.9 us (1.034)
  blocking collectives: 52.1 us -> 43.5 us
  starting transfers between devices: 13.7 us -> 19.8 us
  waiting for transfers between devices: 7.31 us -> 12.3 us
    all_to_all x3, blocking collectives: 52.1 us -> 43.5 us  [exchange(): return lax.all_to_all(array, axis, split_axis=0, concat_axis=0, tiled=True)]
    ppermute x0 -> x2, waiting for transfers between devices: none -> 6.78 us  [shards(): merged += [kept, lax.ppermute(sent, 'zt', swap)]]
    ppermute x0 -> x2, starting transfers between devices: none -> 6.11 us  [shards(): merged += [kept, lax.ppermute(sent, 'zt', swap)]]
    ppermute x1, waiting for transfers between devices: 4.95 us -> 0.01 us  [shards(): four_b = lax.ppermute(keep_b[1] + got_b[1] + pair_b[1], *sides[0])]
    ppermute x1, waiting for transfers between devices: 0.01 us -> 3.12 us  [shards(): four_a = lax.ppermute(keep_a[1] + got_a[1] + pair_a[1], *sides[1])]
  transfers between devices with their start and end apart: 6 -> 8, of which waited for: 3 -> 4; matrix products, arithmetic and copies ran while one was open for 0% -> 0% of each run, Pallas kernels for 1% -> 1%
where the time goes in v8:
time: 84.9 us; the launch traced here: 84.3 us
  blocking collectives  43.5 us (51%)
  starting transfers between devices  19.8 us (23%)
  waiting for transfers between devices  12.3 us (14%)
  Pallas kernels  7.82 us (9%)
    all_to_all x3, blocking collectives, exchange(): return lax.all_to_all(array, axis, split_axis=0, concat_axis=0, tiled=True)  43.5 us
    ppermute x2, waiting for transfers between devices, shards(): merged += [kept, lax.ppermute(sent, 'zt', swap)]  6.78 us
    ppermute x2, starting transfers between devices, shards(): merged += [kept, lax.ppermute(sent, 'zt', swap)]  6.11 us
    ppermute x1, starting transfers between devices, shards(): four_a = lax.ppermute(keep_a[1] + got_a[1] + pair_a[1], *sides[1])  5.77 us
    ppermute x1, starting transfers between devices, shards(): pair_b = lax.ppermute(keep_b[2:] + got_b[2:], *sides[1])  5.16 us
    pallas_call x1, Pallas kernels, shards(): call(forward_kernel, 'forward', (shape(4, *matrix), shape(COLS, PCHUNK +...  3.62 us
    ppermute x1, waiting for transfers between devices, shards(): four_a = lax.ppermute(keep_a[1] + got_a[1] + pair_a[1], *sides[1])  3.12 us
    ppermute x1, waiting for transfers between devices, shards(): pair_a = lax.ppermute(keep_a[2:] + got_a[2:], *sides[0])  2.09 us
  transfers between devices with their start and end apart: 8, of which 4 were waited for; matrix products, arithmetic and copies ran while one was open for 0% of the time, Pallas kernels for 1%

profile of v8, /device:TPU:8, one launch (start us, length us, event | category | flops | bytes accessed | tf_op | source)
XLA Modules:
  0.0 84.3 jit_solution(13757165377512549211)
XLA Ops:
  0.6 3.6 %forward.1 = (f32[4,256,512]{2,1,0:T(8,128)S(1)}, f32[16,80,128]{2,1,0:T(8,128)S(1)}, f32[8,128]{1,0:T(8,128)S(1)}, bf16[256,256]{1,0:T(8,128)(2,1)S(1)}, bf16[2...) custom-call(s32[1,17]{1,0:T(1,128)} %labels_hbm.1, f32[2,2048,128]{2,1,0:T(8,128)} %bitcast.39), custom_call_target="tpu_custom_call" | custom-call | flops 2000000000 | bytes 7000000 | tf_op jit(solution)/shard_map/forward/pallas_call | solution.py:364
  4.3 0.0 copy-start
  4.3 18.6 %all_to_all.15.got_ref.first_ref = f32[16,80,128]{2,1,0:T(8,128)S(1)} all-to-all(f32[16,80,128]{2,1,0:T(8,128)S(1)} %get-tuple-element.20), channel_id=1, replica_groups=mesh['zt'=2,'zm'=2,'zl'=2,'core'=2,'y'=4,'x'=4] {'y','x'}, dimensions={0} | all-to-all | bytes 1310720 | tf_op jit(solution)/shard_map/all_to_all | solution.py:353
  22.8 0.3 summed.1
  23.2 14.2 %all_to_all.16 = f32[16,1,8320]{2,1,0:T(1,128)S(1)} all-to-all(f32[16,1,8320]{2,1,0:T(1,128)S(1)} %bitcast.34), channel_id=1, replica_groups=mesh['zt'=2,'zm'=2,'zl'=2,'core'=2,'y'=4,'x'=4] {'y','x'}, dimensions={0} | all-to-all | bytes 1064960 | tf_op jit(solution)/shard_map/all_to_all | solution.py:353
  37.4 1.6 %back_first.1 = (f32[4,9,32,128]{3,2,1,0:T(8,128)S(1)}, f32[4,9,32,128]{3,2,1,0:T(8,128)S(1)}, f32[256,512]{1,0:T(8,128)S(1)}) custom-call(f32[1040,128]{1,0:T(8,128)S(1)} %bitcast.33, s32[1024,128]{1,0:T(8,128)S(1)} %bitcast.37, f32[4,256,512]{2,1,0:T(8,128)S(1)} %get-tuple-element.21.rotated_ref.refs_0_, f32[8,128]{1,0:T(8,128)S(1)} %get-tuple-element.22.top_ref.refs_1_, ...), custom_call_target="tpu_custom_call" | custom-call | flops 1000000000 | bytes 4000000 | tf_op jit(solution)/shard_map/back_first/pallas_call | solution.py:408
  39.0 0.1 collective-permute-start
  39.1 1.1 %back_second.1 = (f32[4,8,32,128]{3,2,1,0:T(8,128)S(1)}, f32[4,8,32,128]{3,2,1,0:T(8,128)S(1)}) custom-call(f32[256,512]{1,0:T(8,128)S(1)} %get-tuple-element.31.weight_ref, f32[4,256,512]{2,1,0:T(8,128)S(1)} %get-tuple-element.21.rotated_ref.refs_0_, f32[8,128]{1,0:T(8,128)S(1)} %get-tuple-element.22.top_ref.refs_1_, ...), custom_call_target="tpu_custom_call" | custom-call | flops 1000000000 | bytes 4000000 | tf_op jit(solution)/shard_map/back_second/pallas_call | solution.py:419
  40.2 0.6 collective-permute-start.4
  40.8 0.3 collective-permute-done
  41.1 0.1 slice_add_fusion
  41.1 2.0 %collective-permute-start.1 = (f32[2,9,32,128]{3,2,1,0:T(8,128)S(1)}, f32[2,9,32,128]{3,2,1,0:T(8,128)S(1)}, u32[]{:S(2)}, u32[]{:S(2)}) collective-permute-start(f32[2,9,32,128]{3,2,1,0:T(8,128)S(1)} %slice_add_fusion), channel_id=1, source_target_pairs={{0,32},{32,0},{1,33},{33,1},{2,34},{34,2},{3,35},{35,3},{4,36},{36... | collective-permute-start | bytes 884744 | tf_op jit(solution)/shard_map/ppermute | solution.py:433
  43.2 5.2 %collective-permute-start.5 = (f32[2,8,32,128]{3,2,1,0:T(8,128)S(1)}, f32[2,8,32,128]{3,2,1,0:T(8,128)S(1)}, u32[]{:S(2)}, u32[]{:S(2)}) collective-permute-start(f32[2,8,32,128]{3,2,1,0:T(8,128)S(1)} %slice_add_fusion.1), channel_id=1, source_target_pairs={{0,224},{32,64},{64,32},{96,128},{128,96},{160,192},{192,160},{224... | collective-permute-start | bytes 786440 | tf_op jit(solution)/shard_map/ppermute | solution.py:434
  48.3 2.1 %collective-permute-done.1 = f32[2,9,32,128]{3,2,1,0:T(8,128)S(1)} collective-permute-done((f32[2,9,32,128]{3,2,1,0:T(8,128)S(1)}, f32[2,9,32,128]{3,2,1,0:T(8,128)S(1)}, u32[]{:S(2)}, u32[]{:S(2)}) %collective-permute-start.1) | collective-permute-done | bytes 294944 | tf_op jit(solution)/shard_map/ppermute | solution.py:433
  50.4 0.1 fusion
  50.5 5.8 %collective-permute-start.2 = (f32[9,32,128]{2,1,0:T(8,128)S(1)}, f32[9,32,128]{2,1,0:T(8,128)S(1)}, u32[]{:S(2)}, u32[]{:S(2)}) collective-permute-start(f32[9,32,128]{2,1,0:T(8,128)S(1)} %get-tuple-element.38), channel_id=1, source_target_pairs={{0,224},{32,64},{64,32},{96,128},{128,96},{160,192},{192,160},{224... | collective-permute-start | bytes 442376 | tf_op jit(solution)/shard_map/ppermute | solution.py:435
  56.3 0.1 fusion.2
  56.3 0.1 collective-permute-start.6
  56.4 3.1 %collective-permute-done.2.got = f32[9,32,128]{2,1,0:T(8,128)S(1)} collective-permute-done((f32[9,32,128]{2,1,0:T(8,128)S(1)}, f32[9,32,128]{2,1,0:T(8,128)S(1)}, u32[]{:S(2)}, u32[]{:S(2)}) %collective-permute-start.2) | collective-permute-done | bytes 147488 | tf_op jit(solution)/shard_map/ppermute | solution.py:435
  59.6 4.5 %collective-permute-start.3 = (f32[9,16,128]{2,1,0:T(8,128)S(1)}, f32[9,16,128]{2,1,0:T(8,128)S(1)}, u32[]{:S(2)}, u32[]{:S(2)}) collective-permute-start(f32[9,16,128]{2,1,0:T(8,128)S(1)} %get-tuple-element.30), channel_id=1, source_target_pairs={{0,128},{128,0},{1,129},{129,1},{2,130},{130,2},{3,131},{131,3},{4... | collective-permute-start | bytes 221192 | tf_op jit(solution)/shard_map/ppermute | solution.py:446
  64.1 1.6 %collective-permute-start.7 = (f32[8,16,128]{2,1,0:T(8,128)S(1)}, f32[8,16,128]{2,1,0:T(8,128)S(1)}, u32[]{:S(2)}, u32[]{:S(2)}) collective-permute-start(f32[8,16,128]{2,1,0:T(8,128)S(1)} %get-tuple-element.35), channel_id=1, source_target_pairs={{0,128},{128,0},{1,129},{129,1},{2,130},{130,2},{3,131},{131,3},{4... | collective-permute-start | bytes 196616 | tf_op jit(solution)/shard_map/ppermute | solution.py:446
  65.7 6.8 %collective-permute-done.7.got_b = f32[8,16,128]{2,1,0:T(8,128)S(1)} collective-permute-done((f32[8,16,128]{2,1,0:T(8,128)S(1)}, f32[8,16,128]{2,1,0:T(8,128)S(1)}, u32[]{:S(2)}, u32[]{:S(2)}) %collective-permute-start.7) | collective-permute-done | bytes 65568 | tf_op jit(solution)/shard_map/ppermute | solution.py:446
  72.5 10.7 %all_to_all.17 = f32[16,1,2176]{2,1,0:T(1,128)S(1)} all-to-all(f32[16,1,2176]{2,1,0:T(1,128)S(1)} %bitcast.36), channel_id=1, replica_groups=mesh['zt'=2,'zm'=2,'zl'=2,'core'=2,'y'=4,'x'=4] {'y','x'}, dimensions={0} | all-to-all | bytes 278528 | tf_op jit(solution)/shard_map/all_to_all | solution.py:353
  83.3 1.1 %update.1 = (f32[256,128]{1,0:T(8,128)}, f32[256,128]{1,0:T(8,128)}) custom-call(f32[272,128]{1,0:T(8,128)S(1)} %bitcast.35, f32[16,80,128]{2,1,0:T(8,128)S(1)} %all_to_all.15.got_ref.first_ref, f32[256,128]{1,0:T(8,128)S(1)} %bitcast.38), custom_call_target="tpu_custom_call" | custom-call | flops 10000000 | bytes 1000000 | tf_op jit(solution)/shard_map/update/pallas_call | solution.py:456
  (11 shorter events, 0.1 us)
Async XLA Ops:
  4.3 33.1 %copy-start = (s32[1,131072]{1,0:T(1,128)S(1)}, s32[1,131072]{1,0:T(1,128)}, u32[]{:S(2)}) copy-start(s32[1,131072]{1,0:T(1,128)} %param.7) | copy-start | bytes 1572868
  39.0 2.1 %collective-permute-start = (f32[4,9,32,128]{3,2,1,0:T(8,128)S(1)}, f32[4,9,32,128]{3,2,1,0:T(8,128)S(1)}, u32[]{:S(2)}, u32[]{:S(2)}) collective-permute-start(f32[4,9,32,128]{3,2,1,0:T(8,128)S(1)} %get-tuple-element.28), channel_id=1, source_target_pairs={{0,16},{16,0},{1,17},{17,1},{2,18},{18,2},{3,19},{19,3},{4,20},{20... | collective-permute-start | bytes 1769480 | tf_op jit(solution)/shard_map/ppermute | solution.py:418
  40.2 2.9 %collective-permute-start.4 = (f32[4,8,32,128]{3,2,1,0:T(8,128)S(1)}, f32[4,8,32,128]{3,2,1,0:T(8,128)S(1)}, u32[]{:S(2)}, u32[]{:S(2)}) collective-permute-start(f32[4,8,32,128]{3,2,1,0:T(8,128)S(1)} %get-tuple-element.33), channel_id=1, source_target_pairs={{0,16},{16,0},{1,17},{17,1},{2,18},{18,2},{3,19},{19,3},{4,20},{20... | collective-permute-start | bytes 1572872 | tf_op jit(solution)/shard_map/ppermute | solution.py:428
  41.1 9.3 %collective-permute-start.1 = (f32[2,9,32,128]{3,2,1,0:T(8,128)S(1)}, f32[2,9,32,128]{3,2,1,0:T(8,128)S(1)}, u32[]{:S(2)}, u32[]{:S(2)}) collective-permute-start(f32[2,9,32,128]{3,2,1,0:T(8,128)S(1)} %slice_add_fusion), channel_id=1, source_target_pairs={{0,32},{32,0},{1,33},{33,1},{2,34},{34,2},{3,35},{35,3},{4,36},{36... | collective-permute-start | bytes 884744 | tf_op jit(solution)/shard_map/ppermute | solution.py:433
  43.1 40.2 %copy-start.1 = (f32[32,2,512]{2,1,0:T(2,128)S(1)}, f32[32,2,512]{2,1,0:T(2,128)}, u32[]{:S(2)}) copy-start(f32[32,2,512]{2,1,0:T(2,128)} %param.5) | copy-start | bytes 393220
  43.2 13.1 %collective-permute-start.5 = (f32[2,8,32,128]{3,2,1,0:T(8,128)S(1)}, f32[2,8,32,128]{3,2,1,0:T(8,128)S(1)}, u32[]{:S(2)}, u32[]{:S(2)}) collective-permute-start(f32[2,8,32,128]{3,2,1,0:T(8,128)S(1)} %slice_add_fusion.1), channel_id=1, source_target_pairs={{0,224},{32,64},{64,32},{96,128},{128,96},{160,192},{192,160},{224... | collective-permute-start | bytes 786440 | tf_op jit(solution)/shard_map/ppermute | solution.py:434
  50.5 9.1 %collective-permute-start.2 = (f32[9,32,128]{2,1,0:T(8,128)S(1)}, f32[9,32,128]{2,1,0:T(8,128)S(1)}, u32[]{:S(2)}, u32[]{:S(2)}) collective-permute-start(f32[9,32,128]{2,1,0:T(8,128)S(1)} %get-tuple-element.38), channel_id=1, source_target_pairs={{0,224},{32,64},{64,32},{96,128},{128,96},{160,192},{192,160},{224... | collective-permute-start | bytes 442376 | tf_op jit(solution)/shard_map/ppermute | solution.py:435
  56.3 7.7 %collective-permute-start.6 = (f32[8,32,128]{2,1,0:T(8,128)S(1)}, f32[8,32,128]{2,1,0:T(8,128)S(1)}, u32[]{:S(2)}, u32[]{:S(2)}) collective-permute-start(f32[8,32,128]{2,1,0:T(8,128)S(1)} %get-tuple-element.40), channel_id=1, source_target_pairs={{0,32},{32,0},{1,33},{33,1},{2,34},{34,2},{3,35},{35,3},{4,36},{36... | collective-permute-start | bytes 393224 | tf_op jit(solution)/shard_map/ppermute | solution.py:436
  59.6 12.9 %collective-permute-start.3 = (f32[9,16,128]{2,1,0:T(8,128)S(1)}, f32[9,16,128]{2,1,0:T(8,128)S(1)}, u32[]{:S(2)}, u32[]{:S(2)}) collective-permute-start(f32[9,16,128]{2,1,0:T(8,128)S(1)} %get-tuple-element.30), channel_id=1, source_target_pairs={{0,128},{128,0},{1,129},{129,1},{2,130},{130,2},{3,131},{131,3},{4... | collective-permute-start | bytes 221192 | tf_op jit(solution)/shard_map/ppermute | solution.py:446
  64.1 8.4 %collective-permute-start.7 = (f32[8,16,128]{2,1,0:T(8,128)S(1)}, f32[8,16,128]{2,1,0:T(8,128)S(1)}, u32[]{:S(2)}, u32[]{:S(2)}) collective-permute-start(f32[8,16,128]{2,1,0:T(8,128)S(1)} %get-tuple-element.35), channel_id=1, source_target_pairs={{0,128},{128,0},{1,129},{129,1},{2,130},{130,2},{3,131},{131,3},{4... | collective-permute-start | bytes 196616 | tf_op jit(solution)/shard_map/ppermute | solution.py:446

commit v9 on v7

--- a/solution.py
+++ b/solution.py
@@ -239,10 +239,10 @@
                 *(weight_ref[:, part] * rotated_ref[2 * r + c, :, part] for part in parts), top
             )
             for part, value in zip(parts, pair):
-                wh[:, part], wl[:, part] = halves(value)
+                wh[c, :, part], wl[c, :, part] = halves(value)
         for n in range(2):
             part = pl.ds(n * HALF, HALF)
-            th[c, :, part], tl[c, :, part] = halves(two_pass(wh[:, part], wl[:, part], hb_ref[...]))
+            th[c, :, part], tl[c, :, part] = halves(two_pass(wh[c, :, part], wl[c, :, part], hb_ref[...]))
     for n in range(2):
         part = pl.ds(n * HALF, HALF)
         real, imag = (
@@ -397,8 +397,8 @@
     )(first)
     second = exchange_flat(sent, COL, COLS)
     back_scratch = [
-        pltpu.VMEM(matrix, BF16),
-        pltpu.VMEM(matrix, BF16),
+        pltpu.VMEM((2, *matrix), BF16),
+        pltpu.VMEM((2, *matrix), BF16),
         pltpu.VMEM((2, *matrix), BF16),
         pltpu.VMEM((2, *matrix), BF16),
     ]

time: 82.1 us -> 81.9 us (level)
  no operation moved by 1% of the time
where the time goes in v9:
time: 81.9 us; the launch traced here: 81.7 us
  blocking collectives  52 us (63%)
  starting transfers between devices  13.6 us (17%)
  Pallas kernels  7.59 us (9%)
  waiting for transfers between devices  7.53 us (9%)
    all_to_all x3, blocking collectives, exchange(): return lax.all_to_all(array, axis, split_axis=0, concat_axis=0, tiled=True)  52 us
    ppermute x1, starting transfers between devices, shards(): four_a = lax.ppermute(keep_a[1] + got_a[1] + pair_a[1], *sides[1])  5.77 us
    ppermute x1, starting transfers between devices, shards(): pair_b = lax.ppermute(keep_b[2:] + got_b[2:], *sides[1])  5.05 us
    ppermute x1, waiting for transfers between devices, shards(): four_b = lax.ppermute(keep_b[1] + got_b[1] + pair_b[1], *sides[0])  4.95 us
    pallas_call x1, Pallas kernels, shards(): call(forward_kernel, 'forward', (shape(4, *matrix), shape(COLS, PCHUNK +...  3.62 us
    ppermute x1, waiting for transfers between devices, shards(): pair_a = lax.ppermute(keep_a[2:] + got_a[2:], *sides[0])  2.2 us
    ppermute x1, starting transfers between devices, shards(): pair_a = lax.ppermute(keep_a[2:] + got_a[2:], *sides[0])  1.98 us
  transfers between devices with their start and end apart: 6, of which 3 were waited for; matrix products, arithmetic and copies ran while one was open for 0% of the time, Pallas kernels for 1%

profile of v9, /device:TPU:8, one launch (start us, length us, event | category | flops | bytes accessed | tf_op | source)
XLA Modules:
  0.0 81.7 jit_solution(15697106595103506125)
XLA Ops:
  0.6 3.6 %forward.1 = (f32[4,256,512]{2,1,0:T(8,128)S(1)}, f32[16,80,128]{2,1,0:T(8,128)S(1)}, f32[8,128]{1,0:T(8,128)S(1)}, bf16[256,256]{1,0:T(8,128)(2,1)S(1)}, bf16[2...) custom-call(s32[1,17]{1,0:T(1,128)} %labels_hbm.1, f32[2,2048,128]{2,1,0:T(8,128)} %bitcast.39), custom_call_target="tpu_custom_call" | custom-call | flops 2000000000 | bytes 7000000 | tf_op jit(solution)/shard_map/forward/pallas_call | solution.py:361
  4.3 0.0 copy-start
  4.3 18.6 %all_to_all.15.got_ref.first_ref = f32[16,80,128]{2,1,0:T(8,128)S(1)} all-to-all(f32[16,80,128]{2,1,0:T(8,128)S(1)} %get-tuple-element.16), channel_id=1, replica_groups=mesh['zt'=2,'zm'=2,'zl'=2,'core'=2,'y'=4,'x'=4] {'y','x'}, dimensions={0} | all-to-all | bytes 1310720 | tf_op jit(solution)/shard_map/all_to_all | solution.py:350
  22.8 0.3 summed.1
  23.2 14.2 %all_to_all.16 = f32[16,1,8320]{2,1,0:T(1,128)S(1)} all-to-all(f32[16,1,8320]{2,1,0:T(1,128)S(1)} %bitcast.34), channel_id=1, replica_groups=mesh['zt'=2,'zm'=2,'zl'=2,'core'=2,'y'=4,'x'=4] {'y','x'}, dimensions={0} | all-to-all | bytes 1064960 | tf_op jit(solution)/shard_map/all_to_all | solution.py:350
  37.4 1.5 %back_first.1 = (f32[4,9,32,128]{3,2,1,0:T(8,128)S(1)}, f32[4,9,32,128]{3,2,1,0:T(8,128)S(1)}, f32[256,512]{1,0:T(8,128)S(1)}) custom-call(f32[1040,128]{1,0:T(8,128)S(1)} %bitcast.33, s32[1024,128]{1,0:T(8,128)S(1)} %bitcast.37, f32[4,256,512]{2,1,0:T(8,128)S(1)} %get-tuple-element.17.rotated_ref.refs_0_, f32[8,128]{1,0:T(8,128)S(1)} %get-tuple-element.18.top_ref.refs_1_, ...), custom_call_target="tpu_custom_call" | custom-call | flops 1000000000 | bytes 4000000 | tf_op jit(solution)/shard_map/back_first/pallas_call | solution.py:405
  38.9 0.1 collective-permute-start
  39.0 1.0 %back_second.1 = (f32[4,8,32,128]{3,2,1,0:T(8,128)S(1)}, f32[4,8,32,128]{3,2,1,0:T(8,128)S(1)}) custom-call(f32[256,512]{1,0:T(8,128)S(1)} %get-tuple-element.25.weight_ref, f32[4,256,512]{2,1,0:T(8,128)S(1)} %get-tuple-element.17.rotated_ref.refs_0_, f32[8,128]{1,0:T(8,128)S(1)} %get-tuple-element.18.top_ref.refs_1_, ...), custom_call_target="tpu_custom_call" | custom-call | flops 1000000000 | bytes 4000000 | tf_op jit(solution)/shard_map/back_second/pallas_call | solution.py:416
  40.0 0.6 collective-permute-start.3
  40.6 0.4 collective-permute-done
  41.0 0.1 slice_add_fusion
  41.0 2.0 %collective-permute-start.1 = (f32[2,9,32,128]{3,2,1,0:T(8,128)S(1)}, f32[2,9,32,128]{3,2,1,0:T(8,128)S(1)}, u32[]{:S(2)}, u32[]{:S(2)}) collective-permute-start(f32[2,9,32,128]{3,2,1,0:T(8,128)S(1)} %slice_add_fusion), channel_id=1, source_target_pairs={{0,32},{32,0},{1,33},{33,1},{2,34},{34,2},{3,35},{35,3},{4,36},{36... | collective-permute-start | bytes 884744 | tf_op jit(solution)/shard_map/ppermute | solution.py:430
  43.0 0.0 collective-permute-done.3
  43.1 5.1 %collective-permute-start.4 = (f32[2,8,32,128]{3,2,1,0:T(8,128)S(1)}, f32[2,8,32,128]{3,2,1,0:T(8,128)S(1)}, u32[]{:S(2)}, u32[]{:S(2)}) collective-permute-start(f32[2,8,32,128]{3,2,1,0:T(8,128)S(1)} %slice_add_fusion.1), channel_id=1, source_target_pairs={{0,224},{32,64},{64,32},{96,128},{128,96},{160,192},{192,160},{224... | collective-permute-start | bytes 786440 | tf_op jit(solution)/shard_map/ppermute | solution.py:431
  48.1 2.2 %collective-permute-done.1 = f32[2,9,32,128]{3,2,1,0:T(8,128)S(1)} collective-permute-done((f32[2,9,32,128]{3,2,1,0:T(8,128)S(1)}, f32[2,9,32,128]{3,2,1,0:T(8,128)S(1)}, u32[]{:S(2)}, u32[]{:S(2)}) %collective-permute-start.1) | collective-permute-done | bytes 294944 | tf_op jit(solution)/shard_map/ppermute | solution.py:430
  50.3 0.1 fusion
  50.4 5.8 %collective-permute-start.2 = (f32[9,32,128]{2,1,0:T(8,128)S(1)}, f32[9,32,128]{2,1,0:T(8,128)S(1)}, u32[]{:S(2)}, u32[]{:S(2)}) collective-permute-start(f32[9,32,128]{2,1,0:T(8,128)S(1)} %get-tuple-element.30), channel_id=1, source_target_pairs={{0,224},{32,64},{64,32},{96,128},{128,96},{160,192},{192,160},{224... | collective-permute-start | bytes 442376 | tf_op jit(solution)/shard_map/ppermute | solution.py:432
  56.2 0.0 collective-permute-done.4
  56.2 0.1 fusion.2
  56.2 0.1 collective-permute-start.5
  56.3 5.0 %collective-permute-done.5.got_b = f32[8,32,128]{2,1,0:T(8,128)S(1)} collective-permute-done((f32[8,32,128]{2,1,0:T(8,128)S(1)}, f32[8,32,128]{2,1,0:T(8,128)S(1)}, u32[]{:S(2)}, u32[]{:S(2)}) %collective-permute-start.5) | collective-permute-done | bytes 131104 | tf_op jit(solution)/shard_map/ppermute | solution.py:433
  61.3 0.0 collective-permute-done.2.got_a
  61.3 19.2 %all_to_all.17 = f32[32,1,2176]{2,1,0:T(1,128)S(1)} all-to-all(f32[32,1,2176]{2,1,0:T(1,128)S(1)} %bitcast.35), channel_id=1, replica_groups=mesh['zt'=2,'zm'=2,'zl'=2,'core'=2,'y'=4,'x'=4] {'zt','y','x'}, dimensions={0} | all-to-all | bytes 557056 | tf_op jit(solution)/shard_map/all_to_all | solution.py:350
  80.6 1.1 %update.1 = (f32[256,128]{1,0:T(8,128)}, f32[256,128]{1,0:T(8,128)}) custom-call(f32[544,128]{1,0:T(8,128)S(1)} %bitcast.36, f32[16,80,128]{2,1,0:T(8,128)S(1)} %all_to_all.15.got_ref.first_ref, f32[256,128]{1,0:T(8,128)S(1)} %bitcast.38), custom_call_target="tpu_custom_call" | custom-call | flops 10000000 | bytes 1000000 | tf_op jit(solution)/shard_map/update/pallas_call | solution.py:445
  (5 shorter events, 0.1 us)
Async XLA Ops:
  4.3 33.1 %copy-start = (s32[1,131072]{1,0:T(1,128)S(1)}, s32[1,131072]{1,0:T(1,128)}, u32[]{:S(2)}) copy-start(s32[1,131072]{1,0:T(1,128)} %param.7) | copy-start | bytes 1572868
  38.9 2.1 %collective-permute-start = (f32[4,9,32,128]{3,2,1,0:T(8,128)S(1)}, f32[4,9,32,128]{3,2,1,0:T(8,128)S(1)}, u32[]{:S(2)}, u32[]{:S(2)}) collective-permute-start(f32[4,9,32,128]{3,2,1,0:T(8,128)S(1)} %get-tuple-element.24), channel_id=1, source_target_pairs={{0,16},{16,0},{1,17},{17,1},{2,18},{18,2},{3,19},{19,3},{4,20},{20... | collective-permute-start | bytes 1769480 | tf_op jit(solution)/shard_map/ppermute | solution.py:415
  40.0 3.0 %collective-permute-start.3 = (f32[4,8,32,128]{3,2,1,0:T(8,128)S(1)}, f32[4,8,32,128]{3,2,1,0:T(8,128)S(1)}, u32[]{:S(2)}, u32[]{:S(2)}) collective-permute-start(f32[4,8,32,128]{3,2,1,0:T(8,128)S(1)} %get-tuple-element.27), channel_id=1, source_target_pairs={{0,16},{16,0},{1,17},{17,1},{2,18},{18,2},{3,19},{19,3},{4,20},{20... | collective-permute-start | bytes 1572872 | tf_op jit(solution)/shard_map/ppermute | solution.py:425
  41.0 9.3 %collective-permute-start.1 = (f32[2,9,32,128]{3,2,1,0:T(8,128)S(1)}, f32[2,9,32,128]{3,2,1,0:T(8,128)S(1)}, u32[]{:S(2)}, u32[]{:S(2)}) collective-permute-start(f32[2,9,32,128]{3,2,1,0:T(8,128)S(1)} %slice_add_fusion), channel_id=1, source_target_pairs={{0,32},{32,0},{1,33},{33,1},{2,34},{34,2},{3,35},{35,3},{4,36},{36... | collective-permute-start | bytes 884744 | tf_op jit(solution)/shard_map/ppermute | solution.py:430
  43.0 37.6 %copy-start.1 = (f32[32,2,512]{2,1,0:T(2,128)S(1)}, f32[32,2,512]{2,1,0:T(2,128)}, u32[]{:S(2)}) copy-start(f32[32,2,512]{2,1,0:T(2,128)} %param.5) | copy-start | bytes 393220
  43.1 13.1 %collective-permute-start.4 = (f32[2,8,32,128]{3,2,1,0:T(8,128)S(1)}, f32[2,8,32,128]{3,2,1,0:T(8,128)S(1)}, u32[]{:S(2)}, u32[]{:S(2)}) collective-permute-start(f32[2,8,32,128]{3,2,1,0:T(8,128)S(1)} %slice_add_fusion.1), channel_id=1, source_target_pairs={{0,224},{32,64},{64,32},{96,128},{128,96},{160,192},{192,160},{224... | collective-permute-start | bytes 786440 | tf_op jit(solution)/shard_map/ppermute | solution.py:431
  50.4 10.9 %collective-permute-start.2 = (f32[9,32,128]{2,1,0:T(8,128)S(1)}, f32[9,32,128]{2,1,0:T(8,128)S(1)}, u32[]{:S(2)}, u32[]{:S(2)}) collective-permute-start(f32[9,32,128]{2,1,0:T(8,128)S(1)} %get-tuple-element.30), channel_id=1, source_target_pairs={{0,224},{32,64},{64,32},{96,128},{128,96},{160,192},{192,160},{224... | collective-permute-start | bytes 442376 | tf_op jit(solution)/shard_map/ppermute | solution.py:432
  56.2 5.1 %collective-permute-start.5 = (f32[8,32,128]{2,1,0:T(8,128)S(1)}, f32[8,32,128]{2,1,0:T(8,128)S(1)}, u32[]{:S(2)}, u32[]{:S(2)}) collective-permute-start(f32[8,32,128]{2,1,0:T(8,128)S(1)} %get-tuple-element.32), channel_id=1, source_target_pairs={{0,32},{32,0},{1,33},{33,1},{2,34},{34,2},{3,35},{35,3},{4,36},{36... | collective-permute-start | bytes 393224 | tf_op jit(solution)/shard_map/ppermute | solution.py:433
